TPU v7x, 32 devices: a whole 2x2x4 slice. The times are simulated.
32 devices in a mesh: gx: 4 (over y, x), gy: 8 (over z, core).
Axes of the slice: x: 2, y: 2, z: 4, core: 2. Of those that a mesh axis runs over, the one named last changes fastest.
Arguments:
- features: bfloat16 [32, 32, 64, 128], P(None, 'gx', 'gy'), may hold values from -6 to 6
- weight_two: bfloat16 [27, 32, 32], replicated, may hold values from -0.21875 to 0.21875
- bias_two: float32 [32], replicated, may hold values from -3 to 3
- weight_three: bfloat16 [27, 64, 32], replicated, may hold values from -0.21875 to 0.21875
- bias_three: float32 [64], replicated, may hold values from -3 to 3
- weight_four: bfloat16 [27, 128, 64], replicated, may hold values from -0.25 to 0.25
- bias_four: float32 [128], replicated, may hold values from -3 to 3
Outputs:
- level_two: bfloat16 [32, 32, 64, 128], P(None, 'gx', 'gy')
- level_three: bfloat16 [64, 16, 32, 64], P(None, 'gx', 'gy')
- bottleneck: bfloat16 [128, 8, 16, 32], P(None, None, None, 'gy')
All inputs are finite; a program needn't handle non-finite values.
Results may differ from a plain program's by a relative error of at most 0.0085.
Values may be sent and summed in bfloat16 or wider, within the bound.
No kernel may reach another device: no remote copies, remote signals or barrier semaphores. Data moves between devices by JAX's collectives and lax.ppermute only.
A program may use at most 64 MiB of HBM per device.

v0:
```python
import jax
import jax.numpy as jnp
from jax import lax
from jax.sharding import PartitionSpec as P


def extended(cells, sides, width):
    for axis, dim in sides:
        count = lax.axis_size(axis)
        head = lax.slice_in_dim(cells, 0, width, axis=dim)
        tail = lax.slice_in_dim(cells, cells.shape[dim] - width, cells.shape[dim], axis=dim)
        cells = jnp.concatenate(
            [
                lax.ppermute(tail, axis, [(i, (i + 1) % count) for i in range(count)]),
                cells,
                lax.ppermute(head, axis, [((i + 1) % count, i) for i in range(count)]),
            ],
            axis=dim,
        )
    return cells


def wrap_axis(source, axis):
    first = lax.slice_in_dim(source, 0, 1, axis=axis)
    final = lax.slice_in_dim(source, source.shape[axis] - 1, source.shape[axis], axis=axis)
    return jnp.concatenate([final, source, first], axis=axis)


def convolve(padded, weights, bias_values):
    in_channels = padded.shape[0]
    extent_x = padded.shape[1] - 2
    extent_y = padded.shape[2] - 2
    extent_z = padded.shape[3] - 2
    out_channels = weights.shape[1]
    running = jnp.zeros((out_channels, extent_x * extent_y * extent_z), jnp.float32)
    for offset_x in range(3):
        for offset_y in range(3):
            stacked = jnp.concatenate(
                [
                    padded[
                        :,
                        offset_x : offset_x + extent_x,
                        offset_y : offset_y + extent_y,
                        offset_z : offset_z + extent_z,
                    ]
                    for offset_z in range(3)
                ],
                axis=0,
            ).reshape(3 * in_channels, -1)
            first_row = offset_x * 9 + offset_y * 3
            mixing = (
                weights[first_row : first_row + 3]
                .transpose(1, 0, 2)
                .reshape(out_channels, 3 * in_channels)
            )
            running = running + jnp.dot(mixing, stacked, preferred_element_type=jnp.float32)
    result = running + bias_values[:, None]
    result = jax.nn.leaky_relu(result, 0.1).astype(jnp.bfloat16)
    return result.reshape(out_channels, extent_x, extent_y, extent_z)


def average_pool(source):
    channels, extent_x, extent_y, extent_z = source.shape
    blocks = source.astype(jnp.float32).reshape(
        channels, extent_x // 2, 2, extent_y // 2, 2, extent_z // 2, 2
    )
    return blocks.mean(axis=(2, 4, 6)).astype(jnp.bfloat16)


def shards(features, weight_two, bias_two, weight_three, bias_three, weight_four, bias_four):
    rimmed = extended(features, (("gx", 1), ("gy", 2)), 1)
    level_two = convolve(wrap_axis(rimmed, 3), weight_two, bias_two)
    pooled = average_pool(level_two)
    rimmed_three = extended(pooled, (("gx", 1), ("gy", 2)), 1)
    level_three = convolve(wrap_axis(rimmed_three, 3), weight_three, bias_three)
    coarse = average_pool(level_three)
    pieces = lax.all_to_all(coarse, "gy", split_axis=3, concat_axis=2, tiled=True)
    slab_rows = lax.all_gather(pieces, "gx", axis=1, tiled=True)
    deepened = extended(slab_rows, (("gy", 3),), 1)
    padded = wrap_axis(wrap_axis(deepened, 1), 2)
    bottleneck = convolve(padded, weight_four, bias_four)
    return (level_two, level_three, bottleneck)


def solution(mesh):
    return jax.shard_map(
        shards,
        mesh=mesh,
        in_specs=(P(None, "gx", "gy", None), P(), P(), P(), P(), P(), P()),
        out_specs=(P(None, "gx", "gy", None), P(None, "gx", "gy", None), P(None, None, None, "gy")),
        check_vma=False,
    )
```

profile of v0, /device:TPU:0, one launch (start us, length us, event | category | flops | bytes accessed | tf_op | source)
XLA Modules:
  0.0 100.0 jit_solution(3070848087950724654)
XLA Ops:
  0.6 1.5 %copy.174 = bf16[32,8,8,128]{3,0,2,1:T(8,128)(2,1)S(1)} copy(bf16[32,8,8,128]{3,2,1,0:T(8,128)(2,1)} %param.7) | data formatting | bytes 1048576 | tf_op args[0]
  2.1 3.0 %collective-permute-start = (bf16[32,1,8,128]{3,0,2,1:T(8,128)(2,1)S(1)}, bf16[32,1,8,128]{3,0,2,1:T(8,128)(2,1)S(1)}, u32[]{:S(2)}, u32[]{:S(2)}) collective-permute-start(bf16[32,1,8,128]{3,0,2,1:T(8,128)(2,1)S(1)} %get-tuple-element.57), channel_id=1, source_target_pairs={{0,8},{8,16},{16,24},{24,0},{1,9},{9,17},{17,25},{25,1},{2,10},{10... | collective-permute-start | bytes 196616 | tf_op jit(solution)/shard_map/ppermute | solution.py:14
  5.1 1.0 %collective-permute-start.1 = (bf16[32,1,8,128]{3,0,2,1:T(8,128)(2,1)S(1)}, bf16[32,1,8,128]{3,0,2,1:T(8,128)(2,1)S(1)}, u32[]{:S(2)}, u32[]{:S(2)}) collective-permute-start(bf16[32,1,8,128]{3,0,2,1:T(8,128)(2,1)S(1)} %get-tuple-element.56), channel_id=1, source_target_pairs={{8,0},{16,8},{24,16},{0,24},{9,1},{17,9},{25,17},{1,25},{10,2},{18... | collective-permute-start | bytes 196616 | tf_op jit(solution)/shard_map/ppermute | solution.py:16
  6.2 2.3 %collective-permute-done = bf16[32,1,8,128]{3,0,2,1:T(8,128)(2,1)S(1)} collective-permute-done((bf16[32,1,8,128]{3,0,2,1:T(8,128)(2,1)S(1)}, bf16[32,1,8,128]{3,0,2,1:T(8,128)(2,1)S(1)}, u32[]{:S(2)}, u32[]{:S(2)}) %collective-permute-start) | collective-permute-done | bytes 65568 | tf_op jit(solution)/shard_map/ppermute | solution.py:14
  8.8 1.0 %collective-permute-done.1 = bf16[32,1,8,128]{3,0,2,1:T(8,128)(2,1)S(1)} collective-permute-done((bf16[32,1,8,128]{3,0,2,1:T(8,128)(2,1)S(1)}, bf16[32,1,8,128]{3,0,2,1:T(8,128)(2,1)S(1)}, u32[]{:S(2)}, u32[]{:S(2)}) %collective-permute-start.1) | collective-permute-done | bytes 65568 | tf_op jit(solution)/shard_map/ppermute | solution.py:16
  9.9 2.2 %collective-permute-start.3 = (bf16[32,10,1,128]{3,0,2,1:T(8,128)(2,1)S(1)}, bf16[32,10,1,128]{3,0,2,1:T(8,128)(2,1)S(1)}, u32[]{:S(2)}, u32[]{:S(2)}) collective-permute-start(bf16[32,10,1,128]{3,0,2,1:T(8,128)(2,1)S(1)} %get-tuple-element.52), channel_id=1, source_target_pairs={{1,0},{2,1},{3,2},{4,3},{5,4},{6,5},{7,6},{0,7},{9,8},{10,9},{11,1... | collective-permute-start | bytes 245768 | tf_op jit(solution)/shard_map/ppermute | solution.py:16
  13.2 1.0 %collective-permute-done.3 = bf16[32,10,1,128]{3,0,2,1:T(8,128)(2,1)S(1)} collective-permute-done((bf16[32,10,1,128]{3,0,2,1:T(8,128)(2,1)S(1)}, bf16[32,10,1,128]{3,0,2,1:T(8,128)(2,1)S(1)}, u32[]{:S(2)}, u32[]{:S(2)}) %collective-permute-start.3) | collective-permute-done | bytes 81952 | tf_op jit(solution)/shard_map/ppermute | solution.py:16
  14.2 3.6 %collective-permute-done.2 = bf16[32,10,1,128]{3,0,2,1:T(8,128)(2,1)S(1)} collective-permute-done((bf16[32,10,1,128]{3,0,2,1:T(8,128)(2,1)S(1)}, bf16[32,10,1,128]{3,0,2,1:T(8,128)(2,1)S(1)}, u32[]{:S(2)}, u32[]{:S(2)}) %collective-permute-start.2) | collective-permute-done | bytes 81952 | tf_op jit(solution)/shard_map/ppermute | solution.py:14
  18.2 1.7 %maximum_maximum_fusion = (bf16[32,10,10,129]{3,0,2,1:T(8,128)(2,1)S(1)}, bf16[32,10,10,129]{3,0,2,1:T(8,128)(2,1)S(1)}) fusion(bf16[32,10,1,128]{3,0,2,1:T(8,128)(2,1)S(1)} %collective-permute-done.3, bf16[32,10,8,128]{3,0,2,1:T(8,128)(2,1)S(1)} %constant_dynamic-update-slice_fusion, bf16[32,10,1,128]{3,0,2,1:T(8,128)(2,1)S(1)} %collective-permute-done.2, ...), kind=kLoop, calls=%fused_computation.11 | loop fusion | flops 6604800 | bytes 2483200 | tf_op jit(solution)/shard_map/concatenate | solution.py:26
  19.9 2.8 %fusion.60 = (bf16[32,8,8,128]{3,0,2,1:T(8,128)(2,1)S(1)}, bf16[32,8,8,128]{3,0,2,1:T(8,128)(2,1)S(1)}, bf16[32,8,8,128]{3,0,2,1:T(8,128)(2,1)S(1)}, bf16[32,8,8...) fusion(bf16[32,10,10,129]{3,0,2,1:T(8,128)(2,1)S(1)} %get-tuple, ...), kind=kLoop, calls=%fused_computation.164 | loop fusion | bytes 18874368 | tf_op jit(solution)/shard_map/slice | solution.py:40
  30.0 1.1 %fusion.18 = f32[8192,32]{0,1:T(8,128)S(1)} fusion(bf16[32,96]{1,0:T(8,128)(2,1)S(1)} %reshape.189, bf16[12,8,64,128]{3,2,1,0:T(8,128)(2,1)S(1)} %bitcast.226), kind=kOutput, calls=%fused_computation.29 | convolution fusion | flops 50331648 | bytes 2627584 | tf_op jit(solution)/shard_map/dot_general | solution.py:56
  31.1 1.1 %convolution_add_fusion.7 = f32[8192,32]{0,1:T(8,128)S(1)} fusion(f32[8192,32]{0,1:T(8,128)S(1)} %fusion.18, bf16[32,96]{1,0:T(8,128)(2,1)S(1)} %reshape.191, bf16[12,8,64,128]{3,2,1,0:T(8,128)(2,1)S(1)} %bitcast.227), kind=kOutput, calls=%fused_computation.9 | convolution fusion | flops 50593792 | bytes 3676160 | tf_op jit(solution)/shard_map/dot_general | solution.py:56
  32.2 1.1 %convolution_add_fusion.6 = f32[8192,32]{0,1:T(8,128)S(1)} fusion(f32[8192,32]{0,1:T(8,128)S(1)} %convolution_add_fusion.7, bf16[32,96]{1,0:T(8,128)(2,1)S(1)} %reshape.193, bf16[12,8,64,128]{3,2,1,0:T(8,128)(2,1)S(1)} %bitcast.228), kind=kOutput, calls=%fused_computation.8 | convolution fusion | flops 50593792 | bytes 3676160 | tf_op jit(solution)/shard_map/dot_general | solution.py:56
  33.4 1.1 %convolution_add_fusion.5 = f32[8192,32]{0,1:T(8,128)S(1)} fusion(f32[8192,32]{0,1:T(8,128)S(1)} %convolution_add_fusion.6, bf16[32,96]{1,0:T(8,128)(2,1)S(1)} %reshape.195, bf16[12,8,64,128]{3,2,1,0:T(8,128)(2,1)S(1)} %bitcast.230), kind=kOutput, calls=%fused_computation.7 | convolution fusion | flops 50593792 | bytes 3676160 | tf_op jit(solution)/shard_map/dot_general | solution.py:56
  34.5 1.1 %convolution_add_fusion.4 = f32[8192,32]{0,1:T(8,128)S(1)} fusion(f32[8192,32]{0,1:T(8,128)S(1)} %convolution_add_fusion.5, bf16[32,96]{1,0:T(8,128)(2,1)S(1)} %reshape.197, bf16[12,8,64,128]{3,2,1,0:T(8,128)(2,1)S(1)} %bitcast.229), kind=kOutput, calls=%fused_computation.6 | convolution fusion | flops 50593792 | bytes 3676160 | tf_op jit(solution)/shard_map/dot_general | solution.py:56
  35.6 1.1 %convolution_add_fusion.3 = f32[8192,32]{0,1:T(8,128)S(1)} fusion(f32[8192,32]{0,1:T(8,128)S(1)} %convolution_add_fusion.4, bf16[32,96]{1,0:T(8,128)(2,1)S(1)} %reshape.199, bf16[12,8,64,128]{3,2,1,0:T(8,128)(2,1)S(1)} %bitcast.231), kind=kOutput, calls=%fused_computation.5 | convolution fusion | flops 50593792 | bytes 3676160 | tf_op jit(solution)/shard_map/dot_general | solution.py:56
  36.7 1.1 %convolution_add_fusion.2 = f32[8192,32]{0,1:T(8,128)S(1)} fusion(f32[8192,32]{0,1:T(8,128)S(1)} %convolution_add_fusion.3, bf16[32,96]{1,0:T(8,128)(2,1)S(1)} %reshape.201, bf16[12,8,64,128]{3,2,1,0:T(8,128)(2,1)S(1)} %bitcast.233), kind=kOutput, calls=%fused_computation.4 | convolution fusion | flops 50593792 | bytes 3676160 | tf_op jit(solution)/shard_map/dot_general | solution.py:56
  37.9 1.1 %convolution_add_fusion.1 = f32[8192,32]{0,1:T(8,128)S(1)} fusion(f32[8192,32]{0,1:T(8,128)S(1)} %convolution_add_fusion.2, bf16[32,96]{1,0:T(8,128)(2,1)S(1)} %reshape.203, bf16[12,8,64,128]{3,2,1,0:T(8,128)(2,1)S(1)} %bitcast.232), kind=kOutput, calls=%fused_computation.3 | convolution fusion | flops 50593792 | bytes 3676160 | tf_op jit(solution)/shard_map/dot_general | solution.py:56
  39.0 1.1 %fusion.31 = bf16[32,8192]{1,0:T(8,128)(2,1)S(1)} fusion(f32[8192,32]{0,1:T(8,128)S(1)} %convolution_add_fusion.1, bf16[32,96]{1,0:T(8,128)(2,1)S(1)} %reshape.205, bf16[12,8,64,128]{3,2,1,0:T(8,128)(2,1)S(1)} %bitcast.234, f32[32]{0:T(128)S(1)} %copy-done.13), kind=kOutput, calls=%fused_computation.49 | convolution fusion | flops 51904512 | bytes 3152000 | tf_op jit(solution)/shard_map/dot_general | solution.py:56
  40.1 2.4 %copy.198 = f32[32,8192]{0,1:T(8,128)} copy(bf16[32,8192]{1,0:T(8,128)(2,1)S(1)} %fusion.31) | data formatting | bytes 1572864 | tf_op jit(solution)/shard_map/convert_element_type | solution.py:64
  42.5 4.8 %reduce_sum.18 = f32[32,4,4,64]{0,3,2,1:T(8,128)S(1)} reduce(f32[32,4,2,4,2,64,2]{0,6,5,4,3,2,1:T(2,128)} %bitcast.225, f32[]{:T(128)} %constant.6.clone.1), dimensions={2,4,6}, to_apply=%region_0.1 | reduce | flops 229376 | bytes 1179652 | tf_op jit(solution)/shard_map/reduce_sum | solution.py:67
  47.4 2.1 %collective-permute-start.5 = (bf16[32,1,4,64]{0,3,2,1:T(8,128)(2,1)S(1)}, bf16[32,1,4,64]{0,3,2,1:T(8,128)(2,1)S(1)}, u32[]{:S(2)}, u32[]{:S(2)}) collective-permute-start(bf16[32,1,4,64]{0,3,2,1:T(8,128)(2,1)S(1)} %get-tuple-element.99), channel_id=1, source_target_pairs={{8,0},{16,8},{24,16},{0,24},{9,1},{17,9},{25,17},{1,25},{10,2},{18... | collective-permute-start | bytes 49160 | tf_op jit(solution)/shard_map/ppermute | solution.py:16
  49.6 2.2 %collective-permute-done.5 = bf16[32,1,4,64]{0,3,2,1:T(8,128)(2,1)S(1)} collective-permute-done((bf16[32,1,4,64]{0,3,2,1:T(8,128)(2,1)S(1)}, bf16[32,1,4,64]{0,3,2,1:T(8,128)(2,1)S(1)}, u32[]{:S(2)}, u32[]{:S(2)}) %collective-permute-start.5) | collective-permute-done | bytes 16416 | tf_op jit(solution)/shard_map/ppermute | solution.py:16
  51.8 2.9 %collective-permute-done.4 = bf16[32,1,4,64]{0,3,2,1:T(8,128)(2,1)S(1)} collective-permute-done((bf16[32,1,4,64]{0,3,2,1:T(8,128)(2,1)S(1)}, bf16[32,1,4,64]{0,3,2,1:T(8,128)(2,1)S(1)}, u32[]{:S(2)}, u32[]{:S(2)}) %collective-permute-start.4) | collective-permute-done | bytes 16416 | tf_op jit(solution)/shard_map/ppermute | solution.py:14
  55.3 2.5 %collective-permute-done.7 = bf16[32,6,1,64]{0,3,2,1:T(8,128)(2,1)S(1)} collective-permute-done((bf16[32,6,1,64]{0,3,2,1:T(8,128)(2,1)S(1)}, bf16[32,6,1,64]{0,3,2,1:T(8,128)(2,1)S(1)}, u32[]{:S(2)}, u32[]{:S(2)}) %collective-permute-start.7) | collective-permute-done | bytes 24608 | tf_op jit(solution)/shard_map/ppermute | solution.py:16
  57.8 2.9 %collective-permute-done.6 = bf16[32,6,1,64]{0,3,2,1:T(8,128)(2,1)S(1)} collective-permute-done((bf16[32,6,1,64]{0,3,2,1:T(8,128)(2,1)S(1)}, bf16[32,6,1,64]{0,3,2,1:T(8,128)(2,1)S(1)}, u32[]{:S(2)}, u32[]{:S(2)}) %collective-permute-start.6) | collective-permute-done | bytes 24608 | tf_op jit(solution)/shard_map/ppermute | solution.py:14
  67.9 8.0 %all_to_all.18 = bf16[8,2,512]{2,1,0:T(2,128)(2,1)S(1)} all-to-all(bf16[8,2,512]{2,1,0:T(2,128)(2,1)S(1)} %reshape.247), channel_id=1, replica_groups=mesh['gx'=4,'gy'=8] {'gy'}, dimensions={0} | all-to-all | bytes 32768 | tf_op jit(solution)/shard_map/all_to_all | solution.py:77
  76.0 8.5 %all_gather.3 = bf16[64,8,16,4]{0,2,3,1:T(8,128)(2,1)S(1)} all-gather(bf16[64,2,16,4]{0,2,3,1:T(8,128)(2,1)S(1)} %bitcast.257), channel_id=1, replica_groups=mesh['gx'=4,'gy'=8] {'gx'}, dimensions={1}, use_global_device_ids=true | all-gather | bytes 81920 | tf_op jit(solution)/shard_map/all_gather | solution.py:78
  85.3 0.9 copy.221
  86.2 0.9 reshape.225
  87.1 3.5 %collective-permute-start.9 = (bf16[64,8,16,1]{0,2,3,1:T(8,128)(2,1)S(1)}, bf16[64,8,16,1]{0,2,3,1:T(8,128)(2,1)S(1)}, u32[]{:S(2)}, u32[]{:S(2)}) collective-permute-start(bf16[64,8,16,1]{0,2,3,1:T(8,128)(2,1)S(1)} %get-tuple-element.130), channel_id=1, source_target_pairs={{1,0},{2,1},{3,2},{4,3},{5,4},{6,5},{7,6},{0,7},{9,8},{10,9},{11,1... | collective-permute-start | bytes 49160 | tf_op jit(solution)/shard_map/ppermute | solution.py:16
  90.7 1.6 %collective-permute-done.9 = bf16[64,8,16,1]{0,2,3,1:T(8,128)(2,1)S(1)} collective-permute-done((bf16[64,8,16,1]{0,2,3,1:T(8,128)(2,1)S(1)}, bf16[64,8,16,1]{0,2,3,1:T(8,128)(2,1)S(1)}, u32[]{:S(2)}, u32[]{:S(2)}) %collective-permute-start.9) | collective-permute-done | bytes 16416 | tf_op jit(solution)/shard_map/ppermute | solution.py:16
  (156 shorter events, 25.2 us)
Async XLA Ops:
  0.6 7.8 %copy-start = (bf16[32,8,8,128]{3,2,1,0:T(8,128)(2,1)S(1)}, bf16[32,8,8,128]{3,2,1,0:T(8,128)(2,1)}, u32[]{:S(2)}) copy-start(bf16[32,8,8,128]{3,2,1,0:T(8,128)(2,1)} %param.7) | copy-start | bytes 1572868
  0.6 11.5 %copy-start.2 = (bf16[27,32,32]{2,1,0:T(8,128)(2,1)S(1)}, bf16[27,32,32]{2,1,0:T(8,128)(2,1)}, u32[]{:S(2)}) copy-start(bf16[27,32,32]{2,1,0:T(8,128)(2,1)} %param.8) | copy-start | bytes 165892
  2.1 6.3 %collective-permute-start = (bf16[32,1,8,128]{3,0,2,1:T(8,128)(2,1)S(1)}, bf16[32,1,8,128]{3,0,2,1:T(8,128)(2,1)S(1)}, u32[]{:S(2)}, u32[]{:S(2)}) collective-permute-start(bf16[32,1,8,128]{3,0,2,1:T(8,128)(2,1)S(1)} %get-tuple-element.57), channel_id=1, source_target_pairs={{0,8},{8,16},{16,24},{24,0},{1,9},{9,17},{17,25},{25,1},{2,10},{10... | collective-permute-start | bytes 196616 | tf_op jit(solution)/shard_map/ppermute | solution.py:14
  5.1 4.7 %collective-permute-start.1 = (bf16[32,1,8,128]{3,0,2,1:T(8,128)(2,1)S(1)}, bf16[32,1,8,128]{3,0,2,1:T(8,128)(2,1)S(1)}, u32[]{:S(2)}, u32[]{:S(2)}) collective-permute-start(bf16[32,1,8,128]{3,0,2,1:T(8,128)(2,1)S(1)} %get-tuple-element.56), channel_id=1, source_target_pairs={{8,0},{16,8},{24,16},{0,24},{9,1},{17,9},{25,17},{1,25},{10,2},{18... | collective-permute-start | bytes 196616 | tf_op jit(solution)/shard_map/ppermute | solution.py:16
  9.9 4.3 %collective-permute-start.3 = (bf16[32,10,1,128]{3,0,2,1:T(8,128)(2,1)S(1)}, bf16[32,10,1,128]{3,0,2,1:T(8,128)(2,1)S(1)}, u32[]{:S(2)}, u32[]{:S(2)}) collective-permute-start(bf16[32,10,1,128]{3,0,2,1:T(8,128)(2,1)S(1)} %get-tuple-element.52), channel_id=1, source_target_pairs={{1,0},{2,1},{3,2},{4,3},{5,4},{6,5},{7,6},{0,7},{9,8},{10,9},{11,1... | collective-permute-start | bytes 245768 | tf_op jit(solution)/shard_map/ppermute | solution.py:16
  12.1 5.7 %collective-permute-start.2 = (bf16[32,10,1,128]{3,0,2,1:T(8,128)(2,1)S(1)}, bf16[32,10,1,128]{3,0,2,1:T(8,128)(2,1)S(1)}, u32[]{:S(2)}, u32[]{:S(2)}) collective-permute-start(bf16[32,10,1,128]{3,0,2,1:T(8,128)(2,1)S(1)} %get-tuple-element.51), channel_id=1, source_target_pairs={{0,1},{1,2},{2,3},{3,4},{4,5},{5,6},{6,7},{7,0},{8,9},{9,10},{10,1... | collective-permute-start | bytes 245768 | tf_op jit(solution)/shard_map/ppermute | solution.py:14
  37.8 1.1 %copy-start.13 = (f32[32]{0:T(128)S(1)}, f32[32]{0:T(128)}, u32[]{:S(2)}) copy-start(f32[32]{0:T(128)} %param.9) | copy-start | bytes 388
  47.3 7.9 %copy-start.3 = (bf16[27,64,32]{1,2,0:T(8,128)(2,1)S(1)}, bf16[27,64,32]{1,2,0:T(8,128)(2,1)}, u32[]{:S(2)}) copy-start(bf16[27,64,32]{1,2,0:T(8,128)(2,1)} %param.10) | copy-start | bytes 331780
  47.4 4.4 %collective-permute-start.5 = (bf16[32,1,4,64]{0,3,2,1:T(8,128)(2,1)S(1)}, bf16[32,1,4,64]{0,3,2,1:T(8,128)(2,1)S(1)}, u32[]{:S(2)}, u32[]{:S(2)}) collective-permute-start(bf16[32,1,4,64]{0,3,2,1:T(8,128)(2,1)S(1)} %get-tuple-element.99), channel_id=1, source_target_pairs={{8,0},{16,8},{24,16},{0,24},{9,1},{17,9},{25,17},{1,25},{10,2},{18... | collective-permute-start | bytes 49160 | tf_op jit(solution)/shard_map/ppermute | solution.py:16
  49.5 5.2 %collective-permute-start.4 = (bf16[32,1,4,64]{0,3,2,1:T(8,128)(2,1)S(1)}, bf16[32,1,4,64]{0,3,2,1:T(8,128)(2,1)S(1)}, u32[]{:S(2)}, u32[]{:S(2)}) collective-permute-start(bf16[32,1,4,64]{0,3,2,1:T(8,128)(2,1)S(1)} %get-tuple-element.98), channel_id=1, source_target_pairs={{0,8},{8,16},{16,24},{24,0},{1,9},{9,17},{17,25},{25,1},{2,10},{10... | collective-permute-start | bytes 49160 | tf_op jit(solution)/shard_map/ppermute | solution.py:14
  54.7 3.1 %collective-permute-start.7 = (bf16[32,6,1,64]{0,3,2,1:T(8,128)(2,1)S(1)}, bf16[32,6,1,64]{0,3,2,1:T(8,128)(2,1)S(1)}, u32[]{:S(2)}, u32[]{:S(2)}) collective-permute-start(bf16[32,6,1,64]{0,3,2,1:T(8,128)(2,1)S(1)} %get-tuple-element.76), channel_id=1, source_target_pairs={{1,0},{2,1},{3,2},{4,3},{5,4},{6,5},{7,6},{0,7},{9,8},{10,9},{11,1... | collective-permute-start | bytes 73736 | tf_op jit(solution)/shard_map/ppermute | solution.py:16
  54.8 5.9 %collective-permute-start.6 = (bf16[32,6,1,64]{0,3,2,1:T(8,128)(2,1)S(1)}, bf16[32,6,1,64]{0,3,2,1:T(8,128)(2,1)S(1)}, u32[]{:S(2)}, u32[]{:S(2)}) collective-permute-start(bf16[32,6,1,64]{0,3,2,1:T(8,128)(2,1)S(1)} %get-tuple-element.75), channel_id=1, source_target_pairs={{0,1},{1,2},{2,3},{3,4},{4,5},{5,6},{6,7},{7,0},{8,9},{9,10},{10,1... | collective-permute-start | bytes 73736 | tf_op jit(solution)/shard_map/ppermute | solution.py:14
  66.2 0.8 copy-start.11
  67.0 17.6 %copy-start.1 = (bf16[27,128,64]{1,2,0:T(8,128)(2,1)S(1)}, bf16[27,128,64]{1,2,0:T(8,128)(2,1)}, u32[]{:S(2)}) copy-start(bf16[27,128,64]{1,2,0:T(8,128)(2,1)} %param.12) | copy-start | bytes 1327108
  84.5 6.1 %collective-permute-start.8 = (bf16[64,8,16,1]{0,2,3,1:T(8,128)(2,1)S(1)}, bf16[64,8,16,1]{0,2,3,1:T(8,128)(2,1)S(1)}, u32[]{:S(2)}, u32[]{:S(2)}) collective-permute-start(bf16[64,8,16,1]{0,2,3,1:T(8,128)(2,1)S(1)} %get-tuple-element.131), channel_id=1, source_target_pairs={{0,1},{1,2},{2,3},{3,4},{4,5},{5,6},{6,7},{7,0},{8,9},{9,10},{10,1... | collective-permute-start | bytes 49160 | tf_op jit(solution)/shard_map/ppermute | solution.py:14
  87.1 5.1 %collective-permute-start.9 = (bf16[64,8,16,1]{0,2,3,1:T(8,128)(2,1)S(1)}, bf16[64,8,16,1]{0,2,3,1:T(8,128)(2,1)S(1)}, u32[]{:S(2)}, u32[]{:S(2)}) collective-permute-start(bf16[64,8,16,1]{0,2,3,1:T(8,128)(2,1)S(1)} %get-tuple-element.130), channel_id=1, source_target_pairs={{1,0},{2,1},{3,2},{4,3},{5,4},{6,5},{7,6},{0,7},{9,8},{10,9},{11,1... | collective-permute-start | bytes 49160 | tf_op jit(solution)/shard_map/ppermute | solution.py:16
  92.2 0.6 copy-start.9
  94.2 0.9 copy-start.10
  96.3 1.0 copy-start.8
  96.5 1.0 %copy-start.7 = (bf16[3,128,64]{1,2,0:T(8,128)(2,1)S(1)}, bf16[3,128,64]{1,2,0:T(8,128)(2,1)}, u32[]{:S(2)}) copy-start(bf16[3,128,64]{1,2,0:T(8,128)(2,1)} %get-tuple-element.70) | copy-start | bytes 147460
  96.8 0.9 copy-start.6
  97.0 1.0 %copy-start.5 = (bf16[3,128,64]{1,2,0:T(8,128)(2,1)S(1)}, bf16[3,128,64]{1,2,0:T(8,128)(2,1)}, u32[]{:S(2)}) copy-start(bf16[3,128,64]{1,2,0:T(8,128)(2,1)} %get-tuple-element.68) | copy-start | bytes 147460
  97.3 0.9 copy-start.4
  98.2 0.9 copy-start.12
where the time goes:
time: 100 us
  local copies, waits for them, and re-layouts  21.7 us (22%)
  waiting for transfers between devices  19.9 us (20%)
  blocking collectives  16.5 us (16%)
  matrix products  14.8 us (15%)
  other arithmetic  12.9 us (13%)
  starting transfers between devices  12.6 us (13%)
  between operations  1.59 us (2%)
    dot_general x27, matrix products, convolve(): jnp.dot(mixing, stacked, preferred_element_type=jnp.float32)  14.8 us
    ppermute x5, waiting for transfers between devices, extended(): lax.ppermute(tail, axis, [(i, (i + 1) % count) for i in range(count)])  11.6 us
    ppermute x5, starting transfers between devices, extended(): lax.ppermute(head, axis, [((i + 1) % count, i) for i in range(count)])  8.9 us
    all_gather x1, blocking collectives, shards(): slab_rows = lax.all_gather(pieces, 'gx', axis=1, tiled=True)  8.49 us
    ppermute x5, waiting for transfers between devices, extended(): lax.ppermute(head, axis, [((i + 1) % count, i) for i in range(count)])  8.26 us
    all_to_all x1, blocking collectives, shards(): lax.all_to_all(coarse, 'gy', split_axis=3, concat_axis=2, tiled=True)  8.02 us
    concatenate x18, local copies, waits for them, and re-layouts, convolve(): jnp.concatenate([padded[:, offset_x:offset_x + extent_x, offset_y:offset_...  6.73 us
    reduce_sum x2, other arithmetic, average_pool(): return blocks.mean(axis=(2, 4, 6)).astype(jnp.bfloat16)  5.15 us
  transfers between devices with their start and end apart: 10, of which 9 were waited for; matrix products, arithmetic and copies ran while one was open for 4% of the time, Pallas kernels for 0%

commit v1 on v0

v1 whole, which is shorter than its diff:
```python
import functools

import jax
import jax.numpy as jnp
from jax import lax
from jax.experimental import pallas as pl
from jax.experimental.pallas import tpu as pltpu
from jax.sharding import PartitionSpec as P

VMEM = pl.BlockSpec(memory_space=pltpu.VMEM)


def leaky(t):
    return jnp.where(t >= 0, t, 0.1 * t)


def shift_exchange(low, high, axis):
    count = lax.axis_size(axis)
    below = lax.ppermute(high, axis, [(i, (i + 1) % count) for i in range(count)])
    above = lax.ppermute(low, axis, [((i + 1) % count, i) for i in range(count)])
    return below, above


def pair_exchange(low, high, axis):
    count = lax.axis_size(axis)
    if count % 2:
        return shift_exchange(low, high, axis)
    even = lax.axis_index(axis) % 2 == 0
    inner = [(i, i + 1 if i % 2 == 0 else i - 1) for i in range(count)]
    outer = [(i, (i - 1) % count if i % 2 == 0 else (i + 1) % count) for i in range(count)]
    from_outer = lax.ppermute(jnp.where(even, low, high), axis, outer)
    from_inner = lax.ppermute(jnp.where(even, high, low), axis, inner)
    below = jnp.where(even, from_outer, from_inner)
    above = jnp.where(even, from_inner, from_outer)
    return below, above


def level_two_kernel(cells, left, right, below, above, mix, bias, pool, out, pooled, rolled):
    extent_x, extent_y, channels, depth = cells.shape

    def fill(value, x, y):
        rolled[1, x, y] = value
        wide = value.astype(jnp.float32)
        rolled[0, x, y] = pltpu.roll(wide, 1, 1).astype(value.dtype)
        rolled[2, x, y] = pltpu.roll(wide, depth - 1, 1).astype(value.dtype)

    for y in range(extent_y):
        fill(left[y], 0, y + 1)
        fill(right[y], extent_x + 1, y + 1)
        for x in range(extent_x):
            fill(cells[x, y], x + 1, y + 1)
    for x in range(extent_x + 2):
        fill(below[x], x, 0)
        fill(above[x], x, extent_y + 1)
    offset = bias[...]
    for bx in range(0, extent_x, 2):
        for by in range(0, extent_y, 4):
            stacked = jnp.concatenate(
                [
                    rolled[:, bx : bx + 4, y : y + 4].reshape(48 * channels, depth)
                    for y in (by, by + 2)
                ],
                axis=1,
            )
            result = jnp.dot(mix[...], stacked, preferred_element_type=jnp.float32)
            result = leaky(result + offset).astype(jnp.bfloat16)
            for half in range(2):
                parts = []
                for dx in range(2):
                    for dy in range(2):
                        row = (2 * dx + dy) * channels
                        part = result[row : row + channels, half * depth : (half + 1) * depth]
                        out[bx + dx, by + 2 * half + dy] = part
                        parts.append(part)
                mean = jnp.dot(
                    jnp.concatenate(parts, axis=1), pool[...], preferred_element_type=jnp.float32
                )
                pooled[bx // 2, by // 2 + half] = mean.astype(jnp.bfloat16)


def level_two_conv(cells, left, right, below, above, weights, bias_values):
    extent_x, extent_y, channels, depth = cells.shape
    taps = weights.reshape(3, 3, 3, channels, channels)
    blocks = [
        jnp.pad(taps, ((dx, 1 - dx), (dy, 1 - dy), (0, 0), (0, 0), (0, 0)))
        .transpose(3, 2, 0, 1, 4)
        .reshape(channels, 48 * channels)
        for dx in range(2)
        for dy in range(2)
    ]
    mix = jnp.concatenate(blocks, axis=0)
    bias = jnp.tile(bias_values, 4)[:, None]
    source = lax.broadcasted_iota(jnp.int32, (4 * depth, depth), 0) % depth // 2
    target = lax.broadcasted_iota(jnp.int32, (4 * depth, depth), 1) % (depth // 2)
    pool = jnp.where(source == target, 0.125, 0.0).astype(jnp.bfloat16)
    return pl.pallas_call(
        level_two_kernel,
        name="conv_two",
        out_shape=(
            jax.ShapeDtypeStruct(cells.shape, jnp.bfloat16),
            jax.ShapeDtypeStruct((extent_x // 2, extent_y // 2, channels, depth), jnp.bfloat16),
        ),
        in_specs=[VMEM] * 8,
        out_specs=(VMEM, VMEM),
        scratch_shapes=[
            pltpu.VMEM((3, extent_x + 2, extent_y + 2, channels, depth), jnp.bfloat16)
        ],
    )(cells, left, right, below, above, mix, bias, pool)


def level_three_kernel(cells, left, right, below, above, mix, bias, pool, out, pooled, paired):
    extent_x, extent_y, channels, lanes = cells.shape
    depth = lanes // 2
    out_channels = mix.shape[1]

    def column(x, y):
        if y == 0:
            return below[x]
        if y == extent_y + 1:
            return above[x]
        if x == 0:
            return left[y - 1]
        if x == extent_x + 1:
            return right[y - 1]
        return cells[x - 1, y - 1]

    first = lax.broadcasted_iota(jnp.int32, (channels, lanes), 1) < depth
    for x in range(extent_x + 2):
        for y in range(extent_y + 1):
            both = jnp.where(
                first, column(x, y).astype(jnp.float32), column(x, y + 1).astype(jnp.float32)
            )
            place = lax.broadcasted_iota(jnp.int32, (channels, lanes), 1) % depth
            up = jnp.where(place == 0, pltpu.roll(both, lanes - depth + 1, 1), pltpu.roll(both, 1, 1))
            down = jnp.where(
                place == depth - 1, pltpu.roll(both, depth - 1, 1), pltpu.roll(both, lanes - 1, 1)
            )
            paired[x, y, 0] = up.astype(jnp.bfloat16)
            paired[x, y, 1] = both.astype(jnp.bfloat16)
            paired[x, y, 2] = down.astype(jnp.bfloat16)
    offset = bias[...]
    for py in range(extent_y // 2):
        for px in range(extent_x // 2):
            stacked = jnp.concatenate(
                [
                    jnp.concatenate(
                        [
                            paired[x + a, 2 * py + c].reshape(3 * channels, lanes)
                            for a in range(3)
                            for c in range(3)
                        ],
                        axis=0,
                    )
                    for x in (2 * px, 2 * px + 1)
                ],
                axis=1,
            )
            result = lax.dot_general(
                mix[...], stacked, (((0,), (0,)), ((), ())), preferred_element_type=jnp.float32
            )
            result = leaky(result + offset).astype(jnp.bfloat16)
            out[2 * px, py] = result[:, :lanes]
            out[2 * px + 1, py] = result[:, lanes:]
            mean = lax.dot_general(
                pool[...], result, (((1,), (1,)), ((), ())), preferred_element_type=jnp.float32
            )
            pooled[px, py] = mean.astype(jnp.bfloat16)


def level_three_conv(cells, left, right, below, above, weights, bias_values):
    extent_x, extent_y, channels, lanes = cells.shape
    depth = lanes // 2
    out_channels = weights.shape[1]
    mix = weights.transpose(0, 2, 1).reshape(27 * channels, out_channels)
    target = lax.broadcasted_iota(jnp.int32, (depth // 2, 2 * lanes), 0)
    source = lax.broadcasted_iota(jnp.int32, (depth // 2, 2 * lanes), 1) % depth // 2
    pool = jnp.where(source == target, 0.125, 0.0).astype(jnp.bfloat16)
    return pl.pallas_call(
        level_three_kernel,
        name="conv_three",
        out_shape=(
            jax.ShapeDtypeStruct((extent_x, extent_y // 2, out_channels, lanes), jnp.bfloat16),
            jax.ShapeDtypeStruct(
                (extent_x // 2, extent_y // 2, depth // 2, out_channels), jnp.bfloat16
            ),
        ),
        in_specs=[VMEM] * 8,
        out_specs=(VMEM, VMEM),
        scratch_shapes=[
            pltpu.VMEM((extent_x + 2, extent_y + 1, 3, channels, lanes), jnp.bfloat16)
        ],
    )(cells, left, right, below, above, mix, bias_values[:, None], pool)


def level_four_kernel(layers, cells, mix, bias, out, rolled):
    extent_x, rows, width = cells.shape
    for x in range(extent_x):
        value = cells[x]
        wide = value.astype(jnp.float32)
        rolled[0, x + 1] = pltpu.roll(wide, layers, 0).astype(value.dtype)
        rolled[1, x + 1] = value
        rolled[2, x + 1] = pltpu.roll(wide, rows - layers, 0).astype(value.dtype)
    for c in range(3):
        rolled[c, 0] = rolled[c, extent_x]
        rolled[c, extent_x + 1] = rolled[c, 1]
    total = jnp.zeros((extent_x * rows, out.shape[1]), jnp.float32)
    for a in range(3):
        for c in range(3):
            total = total + jnp.dot(
                rolled[c, a : a + extent_x].reshape(extent_x * rows, width),
                mix[3 * a + c],
                preferred_element_type=jnp.float32,
            )
    out[...] = leaky(total + bias[...]).astype(jnp.bfloat16)


def level_four_conv(slabs, weights, bias_values):
    extent_x, extent_y, depth, channels = slabs.shape
    layers = depth - 2
    out_channels = weights.shape[1]
    cells = jnp.concatenate([slabs[:, :, e : e + layers] for e in range(3)], axis=3)
    rows = extent_y * layers
    cells = cells.reshape(extent_x, rows, 3 * channels)
    mix = weights.transpose(0, 2, 1).reshape(9, 3 * channels, out_channels)
    out = pl.pallas_call(
        functools.partial(level_four_kernel, layers),
        name="conv_four",
        out_shape=jax.ShapeDtypeStruct((extent_x * rows, out_channels), jnp.bfloat16),
        in_specs=[VMEM] * 3,
        out_specs=VMEM,
        scratch_shapes=[pltpu.VMEM((3, extent_x + 2, rows, 3 * channels), jnp.bfloat16)],
    )(cells, mix, bias_values[None, :])
    return out.reshape(extent_x, extent_y, layers, out_channels).transpose(3, 0, 1, 2)


def shards(features, weight_two, bias_two, weight_three, bias_three, weight_four, bias_four):
    count_x, count_y = lax.axis_size("gx"), lax.axis_size("gy")
    cells = features.transpose(1, 2, 0, 3)
    left, right = shift_exchange(cells[0], cells[-1], "gx")
    low = jnp.concatenate([left[:1], cells[:, 0], right[:1]], axis=0)
    high = jnp.concatenate([left[-1:], cells[:, -1], right[-1:]], axis=0)
    below, above = pair_exchange(low, high, "gy")
    level_two, pooled = level_two_conv(cells, left, right, below, above, weight_two, bias_two)

    left, right = shift_exchange(pooled[0], pooled[-1], "gx")
    low = jnp.concatenate([left[:1], pooled[:, 0], right[:1]], axis=0)
    high = jnp.concatenate([left[-1:], pooled[:, -1], right[-1:]], axis=0)
    below, above = pair_exchange(low, high, "gy")
    level_three, coarse = level_three_conv(
        pooled, left, right, below, above, weight_three, bias_three
    )

    extent_x, extent_y, depth, channels = coarse.shape
    layers = depth // count_y
    ringed = jnp.concatenate([coarse[:, :, -1:], coarse, coarse[:, :, :1]], axis=2)
    windows = jnp.stack(
        [ringed[:, :, layers * d : layers * (d + 1) + 2] for d in range(count_y)], axis=0
    )
    windows = jnp.broadcast_to(windows, (count_x,) + windows.shape)
    windows = windows.reshape((count_x * count_y,) + windows.shape[2:])
    slabs = lax.all_to_all(windows, ("gx", "gy"), 0, 0, tiled=True)
    slabs = slabs.reshape(count_x, count_y, extent_x, extent_y, layers + 2, channels)
    slabs = slabs.transpose(0, 2, 1, 3, 4, 5).reshape(
        count_x * extent_x, count_y * extent_y, layers + 2, channels
    )
    bottleneck = level_four_conv(slabs, weight_four, bias_four)
    out_three = level_three.reshape(level_three.shape[:3] + (2, level_three.shape[3] // 2))
    out_three = out_three.transpose(2, 0, 1, 3, 4)
    out_three = out_three.reshape(out_three.shape[:2] + (-1, out_three.shape[4]))
    return level_two.transpose(2, 0, 1, 3), out_three, bottleneck


def solution(mesh):
    return jax.shard_map(
        shards,
        mesh=mesh,
        in_specs=(P(None, "gx", "gy", None), P(), P(), P(), P(), P(), P()),
        out_specs=(
            P(None, "gx", "gy", None),
            P(None, "gx", "gy", None),
            P(None, None, None, "gy"),
        ),
        check_vma=False,
    )
```

time: 100 us -> 58 us (0.58)
  blocking collectives: 16.5 us -> 0 us
  matrix products: 14.8 us -> 0 us
  Pallas kernels: 0 us -> 10.3 us
  local copies, waits for them, and re-layouts: 21.7 us -> 13.3 us
  other arithmetic: 12.9 us -> 4.67 us
  waiting for transfers between devices: 19.9 us -> 13.4 us
  starting transfers between devices: 12.6 us -> 15 us
    dot_general x27 -> x0, matrix products: 14.8 us -> none  [convolve(): jnp.dot(mixing, stacked, preferred_element_type=jnp.float32)]
    ppermute x10 -> x8, waiting for transfers between devices: 19.9 us -> 7.67 us  [the longest x2 4.61 us: pair_exchange(): from_outer = lax.ppermute(jnp.where(even, low, high), axis, outer)]
    pallas_call x0 -> x3, Pallas kernels: none -> 10.3 us  [the longest x1 4.79 us: level_two_conv(): pl.pallas_call(level_two_kernel, name='conv_two', out_shape=(jax.ShapeDty...]
    all_gather x1 -> x0, blocking collectives: 8.49 us -> none  [shards(): slab_rows = lax.all_gather(pieces, 'gx', axis=1, tiled=True)]
    all_to_all x1 -> x0, blocking collectives: 8.02 us -> none  [shards(): lax.all_to_all(coarse, 'gy', split_axis=3, concat_axis=2, tiled=True)]
    concatenate x29 -> x2, other arithmetic: 7.67 us -> 0.94 us  [the longest x1 0.79 us: level_two_conv(): mix = jnp.concatenate(blocks, axis=0)]
    concatenate x20 -> x1, local copies, waits for them, and re-layouts: 6.75 us -> 0.14 us  [level_four_conv(): jnp.concatenate([slabs[:, :, e:e + layers] for e in range(3)], axis=3)]
    all_to_all x0 -> x1, waiting for transfers between devices: none -> 5.7 us  [shards(): slabs = lax.all_to_all(windows, ('gx', 'gy'), 0, 0, tiled=True)]
  transfers between devices with their start and end apart: 10 -> 9, of which waited for: 9 -> 5; matrix products, arithmetic and copies ran while one was open for 4% -> 14% of each run, Pallas kernels for 0% -> 0%
where the time goes in v1:
time: 58 us; the launch traced here: 57.6 us
  starting transfers between devices  15 us (26%)
  waiting for transfers between devices  13.4 us (23%)
  local copies, waits for them, and re-layouts  13.3 us (23%)
  Pallas kernels  10.3 us (18%)
  other arithmetic  4.67 us (8%)
  between operations  0.97 us (2%)
    all_to_all x1, waiting for transfers between devices, shards(): slabs = lax.all_to_all(windows, ('gx', 'gy'), 0, 0, tiled=True)  5.7 us
    unnamed x34, local copies, waits for them, and re-layouts  5.61 us
    pallas_call x1, Pallas kernels, level_two_conv(): pl.pallas_call(level_two_kernel, name='conv_two', out_shape=(jax.ShapeDty...  4.79 us
    ppermute x2, waiting for transfers between devices, pair_exchange(): from_outer = lax.ppermute(jnp.where(even, low, high), axis, outer)  4.61 us
    ppermute x2, starting transfers between devices, pair_exchange(): from_outer = lax.ppermute(jnp.where(even, low, high), axis, outer)  4.5 us
    ppermute x2, starting transfers between devices, shift_exchange(): lax.ppermute(high, axis, [(i, (i + 1) % count) for i in range(count)])  4.44 us
    all_to_all x1, starting transfers between devices, shards(): slabs = lax.all_to_all(windows, ('gx', 'gy'), 0, 0, tiled=True)  3.43 us
    pallas_call x1, Pallas kernels, level_three_conv(): pl.pallas_call(level_three_kernel, name='conv_three', out_shape=(jax.Shap...  3.02 us
  transfers between devices with their start and end apart: 9, of which 5 were waited for; matrix products, arithmetic and copies ran while one was open for 14% of the time, Pallas kernels for 0%

profile of v1, /device:TPU:0, one launch (start us, length us, event | category | flops | bytes accessed | tf_op | source)
XLA Modules:
  0.0 57.6 jit_solution(18259029159007960182)
XLA Ops:
  0.6 1.4 %copy.80 = bf16[32,8,8,128]{3,0,2,1:T(8,128)(2,1)S(1)} copy(bf16[32,8,8,128]{3,2,1,0:T(8,128)(2,1)} %param.7) | data formatting | bytes 1048576 | tf_op args[0]
  2.1 3.0 %collective-permute-start = (bf16[8,32,128]{2,1,0:T(8,128)(2,1)S(1)}, bf16[8,32,128]{2,1,0:T(8,128)(2,1)S(1)}, u32[]{:S(2)}, u32[]{:S(2)}) collective-permute-start(bf16[8,32,128]{2,1,0:T(8,128)(2,1)S(1)} %get-tuple-element.29), channel_id=1, source_target_pairs={{0,8},{8,16},{16,24},{24,0},{1,9},{9,17},{17,25},{25,1},{2,10},{10... | collective-permute-start | bytes 196616 | tf_op jit(solution)/shard_map/ppermute | solution.py:19
  5.1 1.0 %collective-permute-start.1 = (bf16[8,32,128]{2,1,0:T(8,128)(2,1)S(1)}, bf16[8,32,128]{2,1,0:T(8,128)(2,1)S(1)}, u32[]{:S(2)}, u32[]{:S(2)}) collective-permute-start(bf16[8,32,128]{2,1,0:T(8,128)(2,1)S(1)} %get-tuple-element.28), channel_id=1, source_target_pairs={{8,0},{16,8},{24,16},{0,24},{9,1},{17,9},{25,17},{1,25},{10,2},{18... | collective-permute-start | bytes 196616 | tf_op jit(solution)/shard_map/ppermute | solution.py:20
  6.3 0.8 %pad_bitcast_fusion.3 = (bf16[32,3,4,4,32]{4,3,2,1,0:T(4,128)(2,1)S(1)}, bf16[32,3,4,4,32]{4,3,2,1,0:T(4,128)(2,1)S(1)}, bf16[32,3,4,4,32]{4,3,2,1,0:T(4,128)(2,1)S(1)}, bf16[32,3,4,4,32]{4,3,2,1,0:T(4,128)(2,1)S(1)}) fusion(bf16[3,3,3,32,32]{4,1,0,2,3:T(4,128)(2,1)S(1)} %copy.62), kind=kLoop, calls=%fused_computation.12 | loop fusion | bytes 448512 | tf_op jit(solution)/shard_map/transpose | solution.py:86
  8.7 0.7 %broadcast_in_dim_tile.4.bias = f32[128,1]{1,0:T(8,128)} reshape(f32[4,32]{1,0:T(4,128)S(1)} %tile.2) | data formatting | bytes 1024 | tf_op jit(solution)/shard_map/broadcast_in_dim;tile | solution.py:92
  9.4 0.8 %pad_maximum_fusion.mix = bf16[128,1536]{1,0:T(8,128)(2,1)} fusion(bf16[32,1536]{1,0:T(8,128)(2,1)S(1)} %reshape.53, bf16[32,1536]{1,0:T(8,128)(2,1)S(1)} %reshape.52, bf16[32,1536]{1,0:T(8,128)(2,1)S(1)} %reshape.51, bf16[32,1536]{1,0:T(8,128)(2,1)S(1)} %reshape.50), kind=kLoop, calls=%fused_computation.5 | loop fusion | flops 1572864 | bytes 786432 | tf_op jit(solution)/shard_map/concatenate | solution.py:91
  10.2 0.9 %select_convert_fusion.pool = bf16[512,128]{1,0:T(8,128)(2,1)} fusion(s32[128]{0:T(128)S(1)} %get-tuple-element.61, s32[128]{0:T(128)S(1)} %get-tuple-element.62, s32[512]{0:T(512)S(1)} %get-tuple-element.59, s32[512]{0:T(512)S(1)} %get-tuple-element.60, pred[512]{0:T(512)(128)(4,1)S(1)} %fusion.17, pred[128]{0:T(512)(128)(4,1)S(1)} %compare_and_fusion.1), kind=kLoop, calls=%fused_computation.19 | loop fusion | flops 1310720 | bytes 136832 | tf_op jit(solution)/shard_map/convert_element_type | solution.py:95
  11.8 2.9 %collective-permute-start.2 = (bf16[10,32,128]{2,1,0:T(8,128)(2,1)S(1)}, bf16[10,32,128]{2,1,0:T(8,128)(2,1)S(1)}, u32[]{:S(2)}, u32[]{:S(2)}) collective-permute-start(bf16[10,32,128]{2,1,0:T(8,128)(2,1)S(1)} %get-tuple-element.40), channel_id=1, source_target_pairs={{0,7},{1,2},{2,1},{3,4},{4,3},{5,6},{6,5},{7,0},{8,15},{9,10},{10,... | collective-permute-start | bytes 245768 | tf_op jit(solution)/shard_map/ppermute | solution.py:31
  14.7 2.9 %collective-permute-done.2 = bf16[10,32,128]{2,1,0:T(8,128)(2,1)S(1)} collective-permute-done((bf16[10,32,128]{2,1,0:T(8,128)(2,1)S(1)}, bf16[10,32,128]{2,1,0:T(8,128)(2,1)S(1)}, u32[]{:S(2)}, u32[]{:S(2)}) %collective-permute-start.2) | collective-permute-done | bytes 81952 | tf_op jit(solution)/shard_map/ppermute | solution.py:31
  17.6 0.7 %broadcast_select_fusion = (bf16[10,32,128]{2,1,0:T(8,128)(2,1)}, bf16[10,32,128]{2,1,0:T(8,128)(2,1)}) fusion(bf16[10,32,128]{2,1,0:T(8,128)(2,1)S(1)} %collective-permute-done.3, bf16[10,32,128]{2,1,0:T(8,128)(2,1)S(1)} %collective-permute-done.2, pred[]{:T(512)S(6)} %eq.18), kind=kLoop, calls=%fused_computation.24 | loop fusion | flops 81920 | bytes 327681 | tf_op jit(solution)/shard_map/jit(_where)/select_n | solution.py:34
  18.3 4.8 %conv_two.1 = (bf16[8,8,32,128]{3,2,1,0:T(8,128)(2,1)}, bf16[4,4,32,128]{3,2,1,0:T(8,128)(2,1)}) custom-call(bf16[8,8,32,128]{3,2,1,0:T(8,128)(2,1)} %bitcast.75, bf16[8,32,128]{2,1,0:T(8,128)(2,1)} %copy-done.6, bf16[8,32,128]{2,1,0:T(8,128)(2,1)} %copy-done.7, bf16[10,32,128]{2,1,0:T(8,128)(2,1)} %get-tuple-element.38.below, ...), custom_call_target="tpu_custom_call" | custom-call | tf_op jit(solution)/shard_map/conv_two/pallas_call | solution.py:96
  23.1 0.8 %slice_bitcast_fusion.6 = (bf16[4,32,128]{2,1,0:T(8,128)(2,1)S(1)}, bf16[4,32,128]{2,1,0:T(8,128)(2,1)S(1)}) fusion(bf16[4,4,32,128]{3,2,1,0:T(8,128)(2,1)} %get-tuple-element.8.cells), kind=kLoop, calls=%fused_computation.53 | loop fusion | bytes 131072 | tf_op jit(solution)/shard_map/squeeze | solution.py:245
  23.9 1.4 %collective-permute-start.4 = (bf16[4,32,128]{2,1,0:T(8,128)(2,1)S(1)}, bf16[4,32,128]{2,1,0:T(8,128)(2,1)S(1)}, u32[]{:S(2)}, u32[]{:S(2)}) collective-permute-start(bf16[4,32,128]{2,1,0:T(8,128)(2,1)S(1)} %get-tuple-element.44), channel_id=1, source_target_pairs={{0,8},{8,16},{16,24},{24,0},{1,9},{9,17},{17,25},{25,1},{2,10},{10... | collective-permute-start | bytes 98312 | tf_op jit(solution)/shard_map/ppermute | solution.py:19
  25.4 1.6 %collective-permute-start.5 = (bf16[4,32,128]{2,1,0:T(8,128)(2,1)S(1)}, bf16[4,32,128]{2,1,0:T(8,128)(2,1)S(1)}, u32[]{:S(2)}, u32[]{:S(2)}) collective-permute-start(bf16[4,32,128]{2,1,0:T(8,128)(2,1)S(1)} %get-tuple-element.43), channel_id=1, source_target_pairs={{8,0},{16,8},{24,16},{0,24},{9,1},{17,9},{25,17},{1,25},{10,2},{18... | collective-permute-start | bytes 98312 | tf_op jit(solution)/shard_map/ppermute | solution.py:20
  26.9 1.8 %collective-permute-done.4.left = bf16[4,32,128]{2,1,0:T(8,128)(2,1)S(1)} collective-permute-done((bf16[4,32,128]{2,1,0:T(8,128)(2,1)S(1)}, bf16[4,32,128]{2,1,0:T(8,128)(2,1)S(1)}, u32[]{:S(2)}, u32[]{:S(2)}) %collective-permute-start.4) | collective-permute-done | bytes 32800 | tf_op jit(solution)/shard_map/ppermute | solution.py:19
  28.7 1.2 %collective-permute-done.5.right = bf16[4,32,128]{2,1,0:T(8,128)(2,1)S(1)} collective-permute-done((bf16[4,32,128]{2,1,0:T(8,128)(2,1)S(1)}, bf16[4,32,128]{2,1,0:T(8,128)(2,1)S(1)}, u32[]{:S(2)}, u32[]{:S(2)}) %collective-permute-start.5) | collective-permute-done | bytes 32800 | tf_op jit(solution)/shard_map/ppermute | solution.py:20
  30.6 1.6 %collective-permute-start.6 = (bf16[6,32,128]{2,1,0:T(8,128)(2,1)S(1)}, bf16[6,32,128]{2,1,0:T(8,128)(2,1)S(1)}, u32[]{:S(2)}, u32[]{:S(2)}) collective-permute-start(bf16[6,32,128]{2,1,0:T(8,128)(2,1)S(1)} %get-tuple-element.48), channel_id=1, source_target_pairs={{0,7},{1,2},{2,1},{3,4},{4,3},{5,6},{6,5},{7,0},{8,15},{9,10},{10,... | collective-permute-start | bytes 147464 | tf_op jit(solution)/shard_map/ppermute | solution.py:31
  32.2 0.6 %select_convert_fusion.1.pool = bf16[32,256]{1,0:T(8,128)(2,1)} fusion(s32[256]{0:T(256)S(1)} %get-tuple-element.63, s32[256]{0:T(256)S(1)} %get-tuple-element.64, pred[256]{0:T(512)(128)(4,1)S(1)} %compare_and_fusion), kind=kLoop, calls=%fused_computation.52 | loop fusion | flops 155648 | bytes 18688 | tf_op jit(solution)/shard_map/convert_element_type | solution.py:177
  32.8 0.7 %copy-done.10 = f32[64]{0:T(128)S(1)} copy-done((f32[64]{0:T(128)S(1)}, f32[64]{0:T(128)}, u32[]{:S(2)}) %copy-start.10) | copy-done | bytes 280
  33.4 0.7 %copy.69.bias = f32[64,1]{1,0:T(8,128)} copy(f32[64,1]{0,1:T(1,128)S(1)} %bitcast.87) | data formatting | bytes 512 | tf_op jit(solution)/shard_map/broadcast_in_dim | solution.py:192
  34.1 1.7 %collective-permute-done.6 = bf16[6,32,128]{2,1,0:T(8,128)(2,1)S(1)} collective-permute-done((bf16[6,32,128]{2,1,0:T(8,128)(2,1)S(1)}, bf16[6,32,128]{2,1,0:T(8,128)(2,1)S(1)}, u32[]{:S(2)}, u32[]{:S(2)}) %collective-permute-start.6) | collective-permute-done | bytes 49184 | tf_op jit(solution)/shard_map/ppermute | solution.py:31
  35.9 0.6 %broadcast_select_fusion.4 = (bf16[6,32,128]{2,1,0:T(8,128)(2,1)}, bf16[6,32,128]{2,1,0:T(8,128)(2,1)}) fusion(bf16[6,32,128]{2,1,0:T(8,128)(2,1)S(1)} %collective-permute-done.7, bf16[6,32,128]{2,1,0:T(8,128)(2,1)S(1)} %collective-permute-done.6, pred[]{:T(512)S(6)} %eq.18), kind=kLoop, calls=%fused_computation.41 | loop fusion | flops 49152 | bytes 196609 | tf_op jit(solution)/shard_map/jit(_where)/select_n | solution.py:34
  36.5 3.0 %conv_three.1 = (bf16[4,2,64,128]{3,2,1,0:T(8,128)(2,1)}, bf16[2,2,32,64]{3,2,1,0:T(8,128)(2,1)}) custom-call(bf16[4,4,32,128]{3,2,1,0:T(8,128)(2,1)} %get-tuple-element.8.cells, bf16[4,32,128]{2,1,0:T(8,128)(2,1)} %copy-done.8, bf16[4,32,128]{2,1,0:T(8,128)(2,1)} %copy-done.9, bf16[6,32,128]{2,1,0:T(8,128)(2,1)} %get-tuple-element.46.below, ...), custom_call_target="tpu_custom_call" | custom-call | tf_op jit(solution)/shard_map/conv_three/pallas_call | solution.py:178
  39.6 0.8 %fusion.22 = (bf16[2,2,1,64]{3,2,1,0:T(2,128)(2,1)S(1)}, bf16[2,2,1,64]{3,2,1,0:T(2,128)(2,1)S(1)}) fusion(bf16[2,2,32,64]{3,2,1,0:T(8,128)(2,1)} %get-tuple-element.10), kind=kLoop, calls=%fused_computation.82 | loop fusion | bytes 2048 | tf_op jit(solution)/shard_map/slice | solution.py:255
  40.3 0.8 %constant_dynamic-update-slice_fusion.7 = bf16[8,2,2,6,64]{4,3,2,1,0:T(8,128)(2,1)S(1)} fusion(bf16[2,2,32,64]{3,2,1,0:T(8,128)(2,1)} %get-tuple-element.10, bf16[2,2,1,64]{3,2,1,0:T(2,128)(2,1)S(1)} %get-tuple-element.54), kind=kLoop, calls=%fused_computation.63 | loop fusion | flops 6143 | bytes 25088
  41.4 0.8 %reshape.63 = bf16[32,2,768]{2,1,0:T(2,128)(2,1)} reshape(bf16[32,2,6,2,64]{4,3,2,1,0:T(2,128)(2,1)S(1)} %bitcast.80) | data formatting | bytes 196608
  42.2 3.4 %all-to-all-start = ((bf16[32,2,768]{2,1,0:T(2,128)(2,1)}), bf16[32,2,768]{2,1,0:T(2,128)(2,1)S(1)}, u32[]{:S(2)}, u32[]{:S(2)}) async-start(bf16[32,2,768]{2,1,0:T(2,128)(2,1)} %reshape.63), calls=%async_computation | async-start | bytes 196608 | tf_op jit(solution)/shard_map/all_to_all | solution.py:261
  45.7 1.0 %copy.75 = bf16[32,8,8,128]{3,2,1,0:T(8,128)(2,1)} copy(bf16[32,8,8,128]{3,0,2,1:T(8,128)(2,1)S(1)} %bitcast.81) | data formatting | bytes 1048576
  46.8 0.9 %copy.70 = bf16[64,4,2,2,64]{4,3,2,1,0:T(2,128)(2,1)} copy(bf16[64,4,2,2,64]{4,3,0,2,1:T(2,128)(2,1)S(1)} %bitcast.77) | data formatting | bytes 262144 | tf_op jit(solution)/shard_map/transpose | solution.py:268
  47.7 5.7 %all-to-all-done = bf16[32,2,768]{2,1,0:T(2,128)(2,1)S(1)} async-done(((bf16[32,2,768]{2,1,0:T(2,128)(2,1)}), bf16[32,2,768]{2,1,0:T(2,128)(2,1)S(1)}, u32[]{:S(2)}, u32[]{:S(2)}) %all-to-all-start) | async-done | bytes 98336 | tf_op jit(solution)/shard_map/all_to_all | solution.py:261
  54.2 0.9 %reshape.60.cells = bf16[8,64,192]{2,1,0:T(8,128)(2,1)} reshape(bf16[8,16,4,192]{3,2,1,0:T(4,128)(2,1)S(1)} %copy.74) | data formatting | bytes 393216 | tf_op jit(solution)/shard_map/reshape | solution.py:223
  55.1 2.5 %conv_four.1 = bf16[512,128]{1,0:T(8,128)(2,1)} custom-call(bf16[8,64,192]{2,1,0:T(8,128)(2,1)} %reshape.60.cells, bf16[9,192,128]{2,1,0:T(8,128)(2,1)} %bitcast.82, f32[1,128]{1,0:T(1,128)} %bitcast.88), custom_call_target="tpu_custom_call" | custom-call | tf_op jit(solution)/shard_map/conv_four/pallas_call | solution.py:225
  (66 shorter events, 4.1 us)
Async XLA Ops:
  2.0 4.3 %copy-start = (bf16[32,8,8,128]{3,0,2,1:T(8,128)(2,1)}, bf16[32,8,8,128]{3,0,2,1:T(8,128)(2,1)S(1)}, u32[]{:S(2)}) copy-start(bf16[32,8,8,128]{3,0,2,1:T(8,128)(2,1)S(1)} %copy.80) | copy-start | bytes 1572868
  2.0 4.1 %copy-start.4 = (bf16[27,32,32]{2,1,0:T(8,128)(2,1)S(1)}, bf16[27,32,32]{2,1,0:T(8,128)(2,1)}, u32[]{:S(2)}) copy-start(bf16[27,32,32]{2,1,0:T(8,128)(2,1)} %param.8) | copy-start | bytes 165892
  2.1 9.1 %collective-permute-start = (bf16[8,32,128]{2,1,0:T(8,128)(2,1)S(1)}, bf16[8,32,128]{2,1,0:T(8,128)(2,1)S(1)}, u32[]{:S(2)}, u32[]{:S(2)}) collective-permute-start(bf16[8,32,128]{2,1,0:T(8,128)(2,1)S(1)} %get-tuple-element.29), channel_id=1, source_target_pairs={{0,8},{8,16},{16,24},{24,0},{1,9},{9,17},{17,25},{25,1},{2,10},{10... | collective-permute-start | bytes 196616 | tf_op jit(solution)/shard_map/ppermute | solution.py:19
  5.1 6.1 %collective-permute-start.1 = (bf16[8,32,128]{2,1,0:T(8,128)(2,1)S(1)}, bf16[8,32,128]{2,1,0:T(8,128)(2,1)S(1)}, u32[]{:S(2)}, u32[]{:S(2)}) collective-permute-start(bf16[8,32,128]{2,1,0:T(8,128)(2,1)S(1)} %get-tuple-element.28), channel_id=1, source_target_pairs={{8,0},{16,8},{24,16},{0,24},{9,1},{17,9},{25,17},{1,25},{10,2},{18... | collective-permute-start | bytes 196616 | tf_op jit(solution)/shard_map/ppermute | solution.py:20
  8.1 0.7 %copy-start.11 = (f32[32]{0:T(128)S(1)}, f32[32]{0:T(128)}, u32[]{:S(2)}) copy-start(f32[32]{0:T(128)} %param.9) | copy-start | bytes 388
  11.2 0.6 %copy-start.6 = (bf16[8,32,128]{2,1,0:T(8,128)(2,1)}, bf16[8,32,128]{2,1,0:T(8,128)(2,1)S(1)}, u32[]{:S(2)}) copy-start(bf16[8,32,128]{2,1,0:T(8,128)(2,1)S(1)} %collective-permute-done.left) | copy-start | bytes 196612
  11.2 0.6 %copy-start.7 = (bf16[8,32,128]{2,1,0:T(8,128)(2,1)}, bf16[8,32,128]{2,1,0:T(8,128)(2,1)S(1)}, u32[]{:S(2)}) copy-start(bf16[8,32,128]{2,1,0:T(8,128)(2,1)S(1)} %collective-permute-done.1.right) | copy-start | bytes 196612
  11.8 5.8 %collective-permute-start.2 = (bf16[10,32,128]{2,1,0:T(8,128)(2,1)S(1)}, bf16[10,32,128]{2,1,0:T(8,128)(2,1)S(1)}, u32[]{:S(2)}, u32[]{:S(2)}) collective-permute-start(bf16[10,32,128]{2,1,0:T(8,128)(2,1)S(1)} %get-tuple-element.40), channel_id=1, source_target_pairs={{0,7},{1,2},{2,1},{3,4},{4,3},{5,6},{6,5},{7,0},{8,15},{9,10},{10,... | collective-permute-start | bytes 245768 | tf_op jit(solution)/shard_map/ppermute | solution.py:31
  14.7 2.9 %collective-permute-start.3 = (bf16[10,32,128]{2,1,0:T(8,128)(2,1)S(1)}, bf16[10,32,128]{2,1,0:T(8,128)(2,1)S(1)}, u32[]{:S(2)}, u32[]{:S(2)}) collective-permute-start(bf16[10,32,128]{2,1,0:T(8,128)(2,1)S(1)} %get-tuple-element.39), channel_id=1, source_target_pairs={{0,1},{1,0},{2,3},{3,2},{4,5},{5,4},{6,7},{7,6},{8,9},{9,8},{10,11... | collective-permute-start | bytes 245768 | tf_op jit(solution)/shard_map/ppermute | solution.py:32
  23.1 2.3 %copy-start.1 = (bf16[4,4,32,128]{3,2,1,0:T(8,128)(2,1)S(1)}, bf16[4,4,32,128]{3,2,1,0:T(8,128)(2,1)}, u32[]{:S(2)}) copy-start(bf16[4,4,32,128]{3,2,1,0:T(8,128)(2,1)} %get-tuple-element.8.cells) | copy-start | bytes 393220
  23.9 4.8 %collective-permute-start.4 = (bf16[4,32,128]{2,1,0:T(8,128)(2,1)S(1)}, bf16[4,32,128]{2,1,0:T(8,128)(2,1)S(1)}, u32[]{:S(2)}, u32[]{:S(2)}) collective-permute-start(bf16[4,32,128]{2,1,0:T(8,128)(2,1)S(1)} %get-tuple-element.44), channel_id=1, source_target_pairs={{0,8},{8,16},{16,24},{24,0},{1,9},{9,17},{17,25},{25,1},{2,10},{10... | collective-permute-start | bytes 98312 | tf_op jit(solution)/shard_map/ppermute | solution.py:19
  25.4 4.6 %collective-permute-start.5 = (bf16[4,32,128]{2,1,0:T(8,128)(2,1)S(1)}, bf16[4,32,128]{2,1,0:T(8,128)(2,1)S(1)}, u32[]{:S(2)}, u32[]{:S(2)}) collective-permute-start(bf16[4,32,128]{2,1,0:T(8,128)(2,1)S(1)} %get-tuple-element.43), channel_id=1, source_target_pairs={{8,0},{16,8},{24,16},{0,24},{9,1},{17,9},{25,17},{1,25},{10,2},{18... | collective-permute-start | bytes 98312 | tf_op jit(solution)/shard_map/ppermute | solution.py:20
  28.7 1.2 %copy-start.8 = (bf16[4,32,128]{2,1,0:T(8,128)(2,1)}, bf16[4,32,128]{2,1,0:T(8,128)(2,1)S(1)}, u32[]{:S(2)}) copy-start(bf16[4,32,128]{2,1,0:T(8,128)(2,1)S(1)} %collective-permute-done.4.left) | copy-start | bytes 98308
  30.0 0.6 %copy-start.9 = (bf16[4,32,128]{2,1,0:T(8,128)(2,1)}, bf16[4,32,128]{2,1,0:T(8,128)(2,1)S(1)}, u32[]{:S(2)}) copy-start(bf16[4,32,128]{2,1,0:T(8,128)(2,1)S(1)} %collective-permute-done.5.right) | copy-start | bytes 98308
  30.6 5.3 %collective-permute-start.6 = (bf16[6,32,128]{2,1,0:T(8,128)(2,1)S(1)}, bf16[6,32,128]{2,1,0:T(8,128)(2,1)S(1)}, u32[]{:S(2)}, u32[]{:S(2)}) collective-permute-start(bf16[6,32,128]{2,1,0:T(8,128)(2,1)S(1)} %get-tuple-element.48), channel_id=1, source_target_pairs={{0,7},{1,2},{2,1},{3,4},{4,3},{5,6},{6,5},{7,0},{8,15},{9,10},{10,... | collective-permute-start | bytes 147464 | tf_op jit(solution)/shard_map/ppermute | solution.py:31
  32.2 3.7 %collective-permute-start.7 = (bf16[6,32,128]{2,1,0:T(8,128)(2,1)S(1)}, bf16[6,32,128]{2,1,0:T(8,128)(2,1)S(1)}, u32[]{:S(2)}, u32[]{:S(2)}) collective-permute-start(bf16[6,32,128]{2,1,0:T(8,128)(2,1)S(1)} %get-tuple-element.47), channel_id=1, source_target_pairs={{0,1},{1,0},{2,3},{3,2},{4,5},{5,4},{6,7},{7,6},{8,9},{9,8},{10,11... | collective-permute-start | bytes 147464 | tf_op jit(solution)/shard_map/ppermute | solution.py:32
  32.8 0.7 %copy-start.10 = (f32[64]{0:T(128)S(1)}, f32[64]{0:T(128)}, u32[]{:S(2)}) copy-start(f32[64]{0:T(128)} %param.11) | copy-start | bytes 772
  39.6 1.6 %copy-start.3 = (bf16[2,2,32,64]{3,2,1,0:T(8,128)(2,1)S(1)}, bf16[2,2,32,64]{3,2,1,0:T(8,128)(2,1)}, u32[]{:S(2)}) copy-start(bf16[2,2,32,64]{3,2,1,0:T(8,128)(2,1)} %get-tuple-element.10) | copy-start | bytes 49156
  40.3 5.3 %copy-start.2 = (bf16[8,8,32,128]{3,2,1,0:T(8,128)(2,1)S(1)}, bf16[8,8,32,128]{3,2,1,0:T(8,128)(2,1)}, u32[]{:S(2)}) copy-start(bf16[8,8,32,128]{3,2,1,0:T(8,128)(2,1)} %get-tuple-element.7) | copy-start | bytes 1572868
  42.2 11.2 %all-to-all-start = ((bf16[32,2,768]{2,1,0:T(2,128)(2,1)}), bf16[32,2,768]{2,1,0:T(2,128)(2,1)S(1)}, u32[]{:S(2)}, u32[]{:S(2)}) async-start(bf16[32,2,768]{2,1,0:T(2,128)(2,1)} %reshape.63), calls=%async_computation | async-start | bytes 196608 | tf_op jit(solution)/shard_map/all_to_all | solution.py:261
  45.6 1.0 %copy-start.5 = (bf16[4,2,64,128]{3,2,1,0:T(8,128)(2,1)S(1)}, bf16[4,2,64,128]{3,2,1,0:T(8,128)(2,1)}, u32[]{:S(2)}) copy-start(bf16[4,2,64,128]{3,2,1,0:T(8,128)(2,1)} %get-tuple-element.9) | copy-start | bytes 393220

commit v2 on v0

v2 whole, which is shorter than its diff:
```python
import functools

import jax
import jax.numpy as jnp
from jax import lax
from jax.experimental import pallas as pl
from jax.experimental.pallas import tpu as pltpu
from jax.sharding import PartitionSpec as P

VMEM = pl.BlockSpec(memory_space=pltpu.VMEM)
BF16 = jnp.bfloat16
F32 = jnp.float32
COST = pl.CostEstimate(flops=1 << 30, transcendentals=0, bytes_accessed=1 << 20)


def leaky(t):
    return jnp.where(t >= 0, t, 0.1 * t)


def near(value):
    return pltpu.with_memory_space_constraint(value, pltpu.VMEM)


def local(shape):
    return pltpu.VMEM(shape, BF16)


def column(bias):
    count = bias.shape[1]
    return jnp.broadcast_to(bias[...], (count, count)).T[:, :1]


def shift_exchange(low, high, axis):
    count = lax.axis_size(axis)
    below = lax.ppermute(high, axis, [(i, (i + 1) % count) for i in range(count)])
    above = lax.ppermute(low, axis, [((i + 1) % count, i) for i in range(count)])
    return below, above


def pair_exchange(low, high, axis):
    count = lax.axis_size(axis)
    if count % 2:
        return shift_exchange(low, high, axis)
    even = lax.axis_index(axis) % 2 == 0
    inner = [(i, i + 1 if i % 2 == 0 else i - 1) for i in range(count)]
    outer = [(i, (i - 1) % count if i % 2 == 0 else (i + 1) % count) for i in range(count)]
    from_outer = lax.ppermute(jnp.where(even, low, high), axis, outer)
    from_inner = lax.ppermute(jnp.where(even, high, low), axis, inner)
    below = jnp.where(even, from_outer, from_inner)
    above = jnp.where(even, from_inner, from_outer)
    return below, above


def mix_two(mix, bias, pool, stacked, channels, depth):
    result = jnp.dot(mix, stacked, preferred_element_type=F32)
    result = leaky(result + bias).astype(BF16)
    answers = []
    for half in range(2):
        block = result[:, half * depth : (half + 1) * depth]
        sums = jnp.dot(block, pool, preferred_element_type=F32)
        mean = sums[:channels]
        for part in range(1, 4):
            mean = mean + sums[part * channels : (part + 1) * channels]
        answers.append((block, mean.astype(BF16)))
    return answers


def pool_two(depth):
    source = lax.broadcasted_iota(jnp.int32, (depth, depth), 0) // 2
    target = lax.broadcasted_iota(jnp.int32, (depth, depth), 1) % (depth // 2)
    return jnp.where(source == target, 0.125, 0.0).astype(BF16)


def shifts(value):
    depth = value.shape[1]
    return pltpu.roll(value, 1, 1), value, pltpu.roll(value, depth - 1, 1)


def inner_two_kernel(cells, left, right, weights, bias, out, pooled, rolled, mix):
    extent_x, extent_y, channels, depth = cells.shape
    for y in range(extent_y):
        for x in range(extent_x + 2):
            if x == 0:
                value = left[y]
            elif x == extent_x + 1:
                value = right[y]
            else:
                value = cells[x - 1, y]
            for e, turned in enumerate(shifts(value)):
                rolled[e, x, y] = turned
    blank = jnp.zeros((channels, channels), BF16)
    empty = jnp.zeros((channels, 4 * channels), BF16)
    for e in range(3):
        for dx in range(2):
            for dy in range(2):
                rows = slice((2 * dx + dy) * channels, (2 * dx + dy + 1) * channels)
                for wide_x in range(4):
                    a = wide_x - dx
                    tile = empty
                    if 0 <= a < 3:
                        taps = [weights[9 * a + 3 * c + e] for c in range(3)]
                        tile = jnp.concatenate([blank] * dy + taps + [blank] * (1 - dy), axis=1)
                    at = (4 * e + wide_x) * 4 * channels
                    mix[rows, at : at + 4 * channels] = tile
    offset = jnp.concatenate([column(bias)] * 4, axis=0)
    pool = pool_two(depth)
    matrix = mix[...]
    blocks = [(x, y) for x in range(0, extent_x, 2) for y in range(2, extent_y - 2, 2)]
    for pair in range(0, len(blocks), 2):
        both = blocks[pair : pair + 2]
        stacked = jnp.concatenate(
            [
                rolled[:, x : x + 4, y - 1 : y + 3].reshape(48 * channels, depth)
                for x, y in both
            ],
            axis=1,
        )
        answers = mix_two(matrix, offset, pool, stacked, channels, depth)
        for (x, y), (block, mean) in zip(both, answers):
            for part in range(4):
                out[x + part // 2, y - 2 + part % 2] = block[
                    part * channels : (part + 1) * channels
                ]
            pooled[x // 2, y // 2 - 1] = mean


def rim_two_kernel(rolled, below, above, inner, inner_pooled, mix, bias, out, pooled, rim):
    _, wide_x, extent_y, channels, depth = rolled.shape
    extent_x = wide_x - 2
    for x in range(wide_x):
        for side, source in enumerate((below, above)):
            for e, turned in enumerate(shifts(source[x])):
                rim[side, e, x] = turned
    offset = jnp.concatenate([column(bias)] * 4, axis=0)
    pool = pool_two(depth)
    matrix = mix[...]
    for x in range(0, extent_x, 2):
        low, high = [], []
        for e in range(3):
            for at in range(x, x + 4):
                low.append(rim[0, e, at])
                low.append(rolled[e, at, 0:3].reshape(3 * channels, depth))
                high.append(rolled[e, at, extent_y - 3 : extent_y].reshape(3 * channels, depth))
                high.append(rim[1, e, at])
        stacked = jnp.concatenate(
            [jnp.concatenate(low, axis=0), jnp.concatenate(high, axis=0)], axis=1
        )
        answers = mix_two(matrix, offset, pool, stacked, channels, depth)
        for y, (block, mean) in zip((0, extent_y - 2), answers):
            for part in range(4):
                out[x + part // 2, y + part % 2] = block[part * channels : (part + 1) * channels]
            pooled[x // 2, y // 2] = mean
    out[:, 2 : extent_y - 2] = inner[...]
    pooled[:, 1 : extent_y // 2 - 1] = inner_pooled[...]


def inner_two(cells, left, right, weights, bias):
    extent_x, extent_y, channels, depth = cells.shape
    return pl.pallas_call(
        inner_two_kernel,
        name="inner_two",
        out_shape=(
            local((extent_x, extent_y - 4, channels, depth)),
            local((extent_x // 2, extent_y // 2 - 2, channels, depth)),
            local((3, extent_x + 2, extent_y, channels, depth)),
            local((4 * channels, 48 * channels)),
        ),
        in_specs=[VMEM] * 5,
        out_specs=(VMEM,) * 4,
        cost_estimate=COST,
        compiler_params=pltpu.CompilerParams(vmem_limit_bytes=16 << 20),
    )(near(cells), near(left), near(right), near(weights), near(bias))


def rim_two(rolled, below, above, inner, inner_pooled, mix, bias):
    _, wide_x, extent_y, channels, depth = rolled.shape
    extent_x = wide_x - 2
    return pl.pallas_call(
        rim_two_kernel,
        name="rim_two",
        out_shape=(
            local((extent_x, extent_y, channels, depth)),
            local((extent_x // 2, extent_y // 2, channels, depth)),
        ),
        in_specs=[VMEM] * 7,
        out_specs=(VMEM,) * 2,
        scratch_shapes=[pltpu.VMEM((2, 3, wide_x, channels, depth), BF16)],
        cost_estimate=COST,
        compiler_params=pltpu.CompilerParams(vmem_limit_bytes=16 << 20),
    )(*map(near, (rolled, below, above, inner, inner_pooled, mix, bias)))


def three_kernel(layers, cells, left, right, below, above, mix, bias, out, windows, paired):
    extent_x, extent_y, channels, lanes = cells.shape
    depth = lanes // 2
    out_channels = mix.shape[1]
    senders, slots = windows.shape[:2]

    def place(x, y):
        if y == 0:
            return below[x]
        if y == extent_y + 1:
            return above[x]
        if x == 0:
            return left[y - 1]
        if x == extent_x + 1:
            return right[y - 1]
        return cells[x - 1, y - 1]

    first = lax.broadcasted_iota(jnp.int32, (channels, lanes), 1) < depth
    for x in range(extent_x + 2):
        turned = [shifts(place(x, y)) for y in range(extent_y + 2)]
        for y in range(extent_y + 1):
            for e in range(3):
                paired[x, y, e] = jnp.where(first, turned[y][e], turned[y + 1][e])
    offset = column(bias)
    rows = lax.broadcasted_iota(jnp.int32, (slots * 8, 2 * lanes), 0)
    layer = rows % 8
    wanted = (layers * (rows // 8) + layer + depth // 2 - 1) % (depth // 2)
    source = lax.broadcasted_iota(jnp.int32, (slots * 8, 2 * lanes), 1) % depth // 2
    pool = jnp.where((source == wanted) & (layer < layers + 2), 0.125, 0.0).astype(BF16)
    matrix = mix[...]
    for px in range(extent_x // 2):
        results = []
        for py in range(extent_y // 2):
            stacked = jnp.concatenate(
                [
                    jnp.concatenate(
                        [
                            paired[x + a, 2 * py + c].reshape(3 * channels, lanes)
                            for a in range(3)
                            for c in range(3)
                        ],
                        axis=0,
                    )
                    for x in (2 * px, 2 * px + 1)
                ],
                axis=1,
            )
            result = lax.dot_general(
                matrix, stacked, (((0,), (0,)), ((), ())), preferred_element_type=F32
            )
            result = leaky(result + offset).astype(BF16)
            out[2 * px, py] = result[:, :lanes]
            out[2 * px + 1, py] = result[:, lanes:]
            results.append(result)
        means = lax.dot_general(
            pool,
            jnp.concatenate(results, axis=0),
            (((1,), (1,)), ((), ())),
            preferred_element_type=F32,
        ).astype(BF16)
        for slot in range(slots):
            for sender in range(senders):
                windows[sender, slot, 8 * px : 8 * px + 8] = means[8 * slot : 8 * slot + 8]


def three(cells, left, right, below, above, weights, bias_values, count_x, count_y):
    extent_x, extent_y, channels, lanes = cells.shape
    depth = lanes // 2
    out_channels = weights.shape[1]
    layers = depth // 2 // count_y
    mix = weights.transpose(0, 2, 1).reshape(27 * channels, out_channels)
    return pl.pallas_call(
        functools.partial(three_kernel, layers),
        name="three",
        out_shape=(
            local((extent_x, extent_y // 2, out_channels, lanes)),
            local((count_x, count_y, extent_x // 2 * 8, extent_y // 2 * out_channels)),
        ),
        in_specs=[VMEM] * 7,
        out_specs=(VMEM, VMEM),
        scratch_shapes=[pltpu.VMEM((extent_x + 2, extent_y + 1, 3, channels, lanes), BF16)],
        cost_estimate=COST,
        compiler_params=pltpu.CompilerParams(vmem_limit_bytes=16 << 20),
    )(*map(near, (cells, left, right, below, above, mix, bias_values)))


def four_kernel(count_y, tiles, mix, bias, out, rolled):
    sources, parts, lanes = tiles.shape
    extent_x, extent_y, layers, out_channels = out.shape
    rows = count_y * 8
    inner_x = parts // 8
    half = lanes // 2
    upper = lax.broadcasted_iota(jnp.int32, (rows, lanes), 1) >= half
    for x in range(extent_x):
        start = x // inner_x * count_y
        at = x % inner_x * 8
        value = tiles[start : start + count_y, at : at + 8].reshape(rows, lanes).astype(F32)
        before = pltpu.roll(value, 8, 0)
        after = pltpu.roll(value, rows - 8, 0)
        around = pltpu.roll(jnp.where(upper, before, after), half, 1)
        whole = jnp.concatenate([value, around], axis=1)
        for e in range(3):
            turned = whole if e == 0 else pltpu.roll(whole, rows - e, 0)
            rolled[x + 1, :, e * 2 * lanes : (e + 1) * 2 * lanes] = turned.astype(BF16)
    rolled[0] = rolled[extent_x]
    rolled[extent_x + 1] = rolled[1]
    offset = jnp.concatenate([bias[...], bias[...]], axis=1)
    matrix = mix[...]
    for x in range(0, extent_x, 2):
        stacked = jnp.concatenate(
            [rolled[x + a : x + a + 2].reshape(2 * rows, 6 * lanes) for a in range(3)], axis=1
        )
        result = jnp.dot(stacked, matrix, preferred_element_type=F32)
        result = leaky(result + offset).astype(BF16)
        for dx in range(2):
            for y in range(extent_y):
                row = dx * rows + y // 2 * 8
                lane = y % 2 * out_channels
                out[x + dx, y] = result[row : row + layers, lane : lane + out_channels]


def mix_four(weights):
    channels, out_channels = weights.shape[2], weights.shape[1]
    taps = weights.transpose(0, 2, 1).reshape(3, 3, 3, channels, out_channels)
    blank = jnp.zeros_like(taps[:, 0])
    bands = [
        jnp.concatenate(pair, axis=3)
        for pair in (
            (taps[:, 1], taps[:, 0]),
            (taps[:, 2], taps[:, 1]),
            (taps[:, 0], blank),
            (blank, taps[:, 2]),
        )
    ]
    return jnp.concatenate(bands, axis=2).reshape(36 * channels, 2 * out_channels)


def four(tiles, mix, bias, extents, count_y):
    extent_x, extent_y, layers = extents
    out_channels = mix.shape[1] // 2
    return pl.pallas_call(
        functools.partial(four_kernel, count_y),
        name="four",
        out_shape=jax.ShapeDtypeStruct((extent_x, extent_y, layers, out_channels), BF16),
        in_specs=[VMEM] * 3,
        out_specs=VMEM,
        scratch_shapes=[pltpu.VMEM((extent_x + 2, count_y * 8, 6 * tiles.shape[2]), BF16)],
        cost_estimate=COST,
        compiler_params=pltpu.CompilerParams(vmem_limit_bytes=16 << 20),
    )(near(tiles), near(mix), near(bias))


def rows_of(left, cells, right):
    low = jnp.concatenate([left[:1], cells[:, 0], right[:1]], axis=0)
    high = jnp.concatenate([left[-1:], cells[:, -1], right[-1:]], axis=0)
    return low, high


def shards(features, weight_two, bias_two, weight_three, bias_three, weight_four, bias_four):
    count_x, count_y = lax.axis_size("gx"), lax.axis_size("gy")
    left, right = shift_exchange(
        features[:, 0].transpose(1, 0, 2), features[:, -1].transpose(1, 0, 2), "gx"
    )
    cells = features.transpose(1, 2, 0, 3)
    below, above = pair_exchange(*rows_of(left, cells, right), "gy")
    inner, inner_pooled, rolled, mix = inner_two(
        cells, left, right, weight_two, bias_two[None, :]
    )
    level_two, pooled = rim_two(rolled, below, above, inner, inner_pooled, mix, bias_two[None, :])

    left, right = shift_exchange(pooled[0], pooled[-1], "gx")
    below, above = pair_exchange(*rows_of(left, pooled, right), "gy")
    level_three, windows = three(
        pooled, left, right, below, above, weight_three, bias_three[None, :], count_x, count_y
    )
    slots = count_x * count_y
    tiles = lax.all_to_all(
        windows.reshape((slots,) + windows.shape[2:]), ("gx", "gy"), 0, 0, tiled=True
    )
    extent_x, extent_y, channels, depth = level_two.shape
    extents = (count_x * extent_x // 4, count_y * extent_y // 4, depth // 4 // count_y)
    bottleneck = four(tiles, mix_four(weight_four), bias_four[None, :], extents, count_y)
    out_three = level_three.reshape(level_three.shape[:3] + (2, level_three.shape[3] // 2))
    out_three = out_three.transpose(2, 0, 1, 3, 4)
    out_three = out_three.reshape(out_three.shape[:2] + (-1, out_three.shape[4]))
    return level_two.transpose(2, 0, 1, 3), out_three, bottleneck.transpose(3, 0, 1, 2)


def solution(mesh):
    return jax.shard_map(
        shards,
        mesh=mesh,
        in_specs=(P(None, "gx", "gy", None), P(), P(), P(), P(), P(), P()),
        out_specs=(
            P(None, "gx", "gy", None),
            P(None, "gx", "gy", None),
            P(None, None, None, "gy"),
        ),
        check_vma=False,
    )
```

time: 100 us -> 42.7 us (0.43)
  local copies, waits for them, and re-layouts: 21.7 us -> 4.82 us
  blocking collectives: 16.5 us -> 0 us
  matrix products: 14.8 us -> 0 us
  other arithmetic: 12.9 us -> 0.19 us
  Pallas kernels: 0 us -> 6.15 us
  waiting for transfers between devices: 19.9 us -> 18.2 us
    dot_general x27 -> x0, matrix products: 14.8 us -> none  [convolve(): jnp.dot(mixing, stacked, preferred_element_type=jnp.float32)]
    all_gather x1 -> x0, blocking collectives: 8.49 us -> none  [shards(): slab_rows = lax.all_gather(pieces, 'gx', axis=1, tiled=True)]
    all_to_all x1 -> x0, blocking collectives: 8.02 us -> none  [shards(): lax.all_to_all(coarse, 'gy', split_axis=3, concat_axis=2, tiled=True)]
    ppermute x10 -> x8, waiting for transfers between devices: 19.9 us -> 12.2 us  [the longest x2 7.32 us: pair_exchange(): from_outer = lax.ppermute(jnp.where(even, low, high), axis, outer)]
    concatenate x29 -> x1, other arithmetic: 7.67 us -> 0.12 us  [mix_four(): jnp.concatenate(bands, axis=2).reshape(36 * channels, 2 * out_channels)]
    concatenate x20 -> x0, local copies, waits for them, and re-layouts: 6.75 us -> none  [the longest x18 6.73 us: convolve(): jnp.concatenate([padded[:, offset_x:offset_x + extent_x, offset_y:offset_...]
    pallas_call x0 -> x4, Pallas kernels: none -> 6.15 us  [the longest x1 1.65 us: inner_two(): pl.pallas_call(inner_two_kernel, name='inner_two', out_shape=(local((exte...]
    all_to_all x0 -> x1, waiting for transfers between devices: none -> 6.01 us  [shards(): lax.all_to_all(windows.reshape((slots,) + windows.shape[2:]), ('gx', 'gy'...]
  transfers between devices with their start and end apart: 10 -> 9, of which waited for: 9 -> 7; matrix products, arithmetic and copies ran while one was open for 4% -> 9% of each run, Pallas kernels for 0% -> 4%
where the time goes in v2:
time: 42.7 us; the launch traced here: 42.5 us
  waiting for transfers between devices  18.2 us (43%)
  starting transfers between devices  12.3 us (29%)
  Pallas kernels  6.15 us (14%)
  local copies, waits for them, and re-layouts  4.82 us (11%)
  between operations  0.81 us (2%)
    ppermute x2, waiting for transfers between devices, pair_exchange(): from_outer = lax.ppermute(jnp.where(even, low, high), axis, outer)  7.32 us
    all_to_all x1, waiting for transfers between devices, shards(): lax.all_to_all(windows.reshape((slots,) + windows.shape[2:]), ('gx', 'gy'...  6.01 us
    ppermute x2, starting transfers between devices, shift_exchange(): lax.ppermute(high, axis, [(i, (i + 1) % count) for i in range(count)])  5.09 us
    all_to_all x1, starting transfers between devices, shards(): lax.all_to_all(windows.reshape((slots,) + windows.shape[2:]), ('gx', 'gy'...  2.71 us
    ppermute x2, starting transfers between devices, pair_exchange(): from_outer = lax.ppermute(jnp.where(even, low, high), axis, outer)  2.6 us
    ppermute x2, waiting for transfers between devices, shift_exchange(): lax.ppermute(low, axis, [((i + 1) % count, i) for i in range(count)])  2.59 us
    unnamed x18, local copies, waits for them, and re-layouts  2.44 us
    ppermute x2, waiting for transfers between devices, shift_exchange(): lax.ppermute(high, axis, [(i, (i + 1) % count) for i in range(count)])  2.29 us
  transfers between devices with their start and end apart: 9, of which 7 were waited for; matrix products, arithmetic and copies ran while one was open for 9% of the time, Pallas kernels for 4%

profile of v2, /device:TPU:0, one launch (start us, length us, event | category | flops | bytes accessed | tf_op | source)
XLA Modules:
  0.0 42.5 jit_solution(5022091836881787183)
XLA Ops:
  0.6 0.0 copy-start.5
  0.7 1.0 %fusion.5 = (bf16[32,1,8,128]{3,2,1,0:T(8,128)(2,1)S(1)}, bf16[32,1,8,128]{3,2,1,0:T(8,128)(2,1)S(1)}) fusion(bf16[32,8,8,128]{3,2,1,0:T(8,128)(2,1)} %param.7), kind=kLoop, calls=%fused_computation.32 | loop fusion | bytes 262144 | tf_op jit(solution)/shard_map/slice | solution.py:354
  1.6 3.0 %collective-permute-start = (bf16[8,32,128]{2,1,0:T(8,128)(2,1)S(1)}, bf16[8,32,128]{2,1,0:T(8,128)(2,1)S(1)}, u32[]{:S(2)}, u32[]{:S(2)}) collective-permute-start(bf16[8,32,128]{2,1,0:T(8,128)(2,1)S(1)} %bitcast.67), channel_id=1, source_target_pairs={{0,8},{8,16},{16,24},{24,0},{1,9},{9,17},{17,25},{25,1},{2,10},{10... | collective-permute-start | bytes 196616 | tf_op jit(solution)/shard_map/ppermute | solution.py:35
  4.7 1.0 %collective-permute-start.1 = (bf16[8,32,128]{2,1,0:T(8,128)(2,1)S(1)}, bf16[8,32,128]{2,1,0:T(8,128)(2,1)S(1)}, u32[]{:S(2)}, u32[]{:S(2)}) collective-permute-start(bf16[8,32,128]{2,1,0:T(8,128)(2,1)S(1)} %bitcast.68), channel_id=1, source_target_pairs={{8,0},{16,8},{24,16},{0,24},{9,1},{17,9},{25,17},{1,25},{10,2},{18... | collective-permute-start | bytes 196616 | tf_op jit(solution)/shard_map/ppermute | solution.py:36
  5.7 1.4 %copy.32 = bf16[32,8,8,128]{3,0,1,2:T(8,128)(2,1)S(1)} copy(bf16[32,8,8,128]{3,2,1,0:T(8,128)(2,1)} %param.7) | data formatting | bytes 1048576 | tf_op args[0]
  7.1 0.3 copy.13.cells
  7.5 0.4 collective-permute-done.left
  7.9 1.5 %collective-permute-done.1.right = bf16[8,32,128]{2,1,0:T(8,128)(2,1)S(1)} collective-permute-done((bf16[8,32,128]{2,1,0:T(8,128)(2,1)S(1)}, bf16[8,32,128]{2,1,0:T(8,128)(2,1)S(1)}, u32[]{:S(2)}, u32[]{:S(2)}) %collective-permute-start.1) | collective-permute-done | bytes 65568 | tf_op jit(solution)/shard_map/ppermute | solution.py:36
  9.4 2.3 %collective-permute-start.2 = (bf16[10,32,128]{2,1,0:T(8,128)(2,1)S(1)}, bf16[10,32,128]{2,1,0:T(8,128)(2,1)S(1)}, u32[]{:S(2)}, u32[]{:S(2)}) collective-permute-start(bf16[10,32,128]{2,1,0:T(8,128)(2,1)S(1)} %get-tuple-element.32), channel_id=1, source_target_pairs={{0,7},{1,2},{2,1},{3,4},{4,3},{5,6},{6,5},{7,0},{8,15},{9,10},{10,... | collective-permute-start | bytes 245768 | tf_op jit(solution)/shard_map/ppermute | solution.py:47
  11.6 0.0 collective-permute-start.3
  11.7 1.7 %inner_two.1 = (bf16[8,4,32,128]{3,2,1,0:T(8,128)(2,1)S(1)}, bf16[4,2,32,128]{3,2,1,0:T(8,128)(2,1)S(1)}, bf16[3,10,8,32,128]{4,3,2,1,0:T(8,128)(2,1)S(1)}, bf16[128,1536]{1,0:T(8,128)(2,1)S(1)}) custom-call(bf16[8,8,32,128]{3,2,1,0:T(8,128)(2,1)S(1)} %copy.13.cells, bf16[8,32,128]{2,1,0:T(8,128)(2,1)S(1)} %collective-permute-done.left, ...), custom_call_target="tpu_custom_call" | custom-call | flops 1073741824 | bytes 1048576 | tf_op jit(solution)/shard_map/inner_two/pallas_call | solution.py:159
  13.3 2.3 %collective-permute-done.2 = bf16[10,32,128]{2,1,0:T(8,128)(2,1)S(1)} collective-permute-done((bf16[10,32,128]{2,1,0:T(8,128)(2,1)S(1)}, bf16[10,32,128]{2,1,0:T(8,128)(2,1)S(1)}, u32[]{:S(2)}, u32[]{:S(2)}) %collective-permute-start.2) | collective-permute-done | bytes 81952 | tf_op jit(solution)/shard_map/ppermute | solution.py:47
  15.7 0.0 copy-start.6
  15.7 0.0 copy-start.1
  15.7 0.0 copy-start.3
  15.7 1.5 %rim_two.1 = (bf16[8,8,32,128]{3,2,1,0:T(8,128)(2,1)S(1)}, bf16[4,4,32,128]{3,2,1,0:T(8,128)(2,1)S(1)}) custom-call(bf16[3,10,8,32,128]{4,3,2,1,0:T(8,128)(2,1)S(1)} %get-tuple-element.11.rolled, bf16[10,32,128]{2,1,0:T(8,128)(2,1)S(1)} %get-tuple-element.30.below, bf16[10,32,128]{2,1,0:T(8,128)(2,1)S(1)} %get-tuple-element.29.above, ...), custom_call_target="tpu_custom_call" | custom-call | flops 1073741824 | bytes 1048576 | tf_op jit(solution)/shard_map/rim_two/pallas_call | solution.py:178
  17.2 2.1 %collective-permute-start.4 = (bf16[4,32,128]{2,1,0:T(8,128)(2,1)S(1)}, bf16[4,32,128]{2,1,0:T(8,128)(2,1)S(1)}, u32[]{:S(2)}, u32[]{:S(2)}) collective-permute-start(bf16[4,32,128]{2,1,0:T(8,128)(2,1)S(1)} %get-tuple-element.36), channel_id=1, source_target_pairs={{0,8},{8,16},{16,24},{24,0},{1,9},{9,17},{17,25},{25,1},{2,10},{10... | collective-permute-start | bytes 98312 | tf_op jit(solution)/shard_map/ppermute | solution.py:35
  19.3 0.9 %collective-permute-start.5 = (bf16[4,32,128]{2,1,0:T(8,128)(2,1)S(1)}, bf16[4,32,128]{2,1,0:T(8,128)(2,1)S(1)}, u32[]{:S(2)}, u32[]{:S(2)}) collective-permute-start(bf16[4,32,128]{2,1,0:T(8,128)(2,1)S(1)} %get-tuple-element.35), channel_id=1, source_target_pairs={{8,0},{16,8},{24,16},{0,24},{9,1},{17,9},{25,17},{1,25},{10,2},{18... | collective-permute-start | bytes 98312 | tf_op jit(solution)/shard_map/ppermute | solution.py:36
  20.2 1.9 %collective-permute-done.4.left = bf16[4,32,128]{2,1,0:T(8,128)(2,1)S(1)} collective-permute-done((bf16[4,32,128]{2,1,0:T(8,128)(2,1)S(1)}, bf16[4,32,128]{2,1,0:T(8,128)(2,1)S(1)}, u32[]{:S(2)}, u32[]{:S(2)}) %collective-permute-start.4) | collective-permute-done | bytes 32800 | tf_op jit(solution)/shard_map/ppermute | solution.py:35
  22.1 1.1 %collective-permute-done.5.right = bf16[4,32,128]{2,1,0:T(8,128)(2,1)S(1)} collective-permute-done((bf16[4,32,128]{2,1,0:T(8,128)(2,1)S(1)}, bf16[4,32,128]{2,1,0:T(8,128)(2,1)S(1)}, u32[]{:S(2)}, u32[]{:S(2)}) %collective-permute-start.5) | collective-permute-done | bytes 32800 | tf_op jit(solution)/shard_map/ppermute | solution.py:36
  23.2 0.3 collective-permute-start.6
  23.6 0.0 collective-permute-start.7
  23.6 5.0 %collective-permute-done.6 = bf16[6,32,128]{2,1,0:T(8,128)(2,1)S(1)} collective-permute-done((bf16[6,32,128]{2,1,0:T(8,128)(2,1)S(1)}, bf16[6,32,128]{2,1,0:T(8,128)(2,1)S(1)}, u32[]{:S(2)}, u32[]{:S(2)}) %collective-permute-start.6) | collective-permute-done | bytes 49184 | tf_op jit(solution)/shard_map/ppermute | solution.py:47
  28.6 0.0 collective-permute-done.7
  28.6 1.5 %three.1 = (bf16[4,2,64,128]{3,2,1,0:T(8,128)(2,1)S(1)}, bf16[4,8,16,128]{3,2,1,0:T(8,128)(2,1)}) custom-call(bf16[4,4,32,128]{3,2,1,0:T(8,128)(2,1)S(1)} %get-tuple-element.16.cells, bf16[4,32,128]{2,1,0:T(8,128)(2,1)S(1)} %collective-permute-done.4.left, bf16[4,32,128]{2,1,0:T(8,128)(2,1)S(1)} %collective-permute-done.5.right, ...), custom_call_target="tpu_custom_call" | custom-call | flops 1073741824 | bytes 1048576 | tf_op jit(solution)/shard_map/three/pallas_call | solution.py:264
  30.1 2.7 %all-to-all-start = ((bf16[32,16,128]{2,1,0:T(8,128)(2,1)}), bf16[32,16,128]{2,1,0:T(8,128)(2,1)S(1)}, u32[]{:S(2)}, u32[]{:S(2)}) async-start(bf16[32,16,128]{2,1,0:T(8,128)(2,1)} %bitcast.19), calls=%async_computation | async-start | bytes 262144 | tf_op jit(solution)/shard_map/all_to_all | solution.py:369
  32.8 0.1 fusion.4
  33.0 1.0 %copy.20 = bf16[32,8,8,128]{3,2,1,0:T(8,128)(2,1)} copy(bf16[32,8,8,128]{3,0,2,1:T(8,128)(2,1)S(1)} %bitcast.56) | data formatting | bytes 1048576
  34.0 0.1 reshape.25
  34.1 0.9 %copy.16 = bf16[64,4,2,2,64]{4,3,2,1,0:T(2,128)(2,1)} copy(bf16[64,4,2,2,64]{4,3,0,2,1:T(2,128)(2,1)S(1)} %bitcast.63) | data formatting | bytes 262144 | tf_op jit(solution)/shard_map/transpose | solution.py:376
  35.0 6.0 %all-to-all-done.tiles = bf16[32,16,128]{2,1,0:T(8,128)(2,1)S(1)} async-done(((bf16[32,16,128]{2,1,0:T(8,128)(2,1)}), bf16[32,16,128]{2,1,0:T(8,128)(2,1)S(1)}, u32[]{:S(2)}, u32[]{:S(2)}) %all-to-all-start) | async-done | bytes 131104 | tf_op jit(solution)/shard_map/all_to_all | solution.py:369
  41.0 1.5 %four.1 = bf16[8,16,4,128]{3,2,1,0:T(4,128)(2,1)} custom-call(bf16[32,16,128]{2,1,0:T(8,128)(2,1)S(1)} %all-to-all-done.tiles, bf16[2304,256]{1,0:T(8,128)(2,1)S(1)} %bitcast.55, f32[1,128]{1,0:T(1,128)S(1)} %bitcast.61), custom_call_target="tpu_custom_call" | custom-call | flops 1073741824 | bytes 1048576 | tf_op jit(solution)/shard_map/four/pallas_call | solution.py:333
  (25 shorter events, 0.2 us)
Async XLA Ops:
  0.6 6.5 %copy-start.5 = (bf16[32,8,8,128]{3,2,1,0:T(8,128)(2,1)S(1)}, bf16[32,8,8,128]{3,2,1,0:T(8,128)(2,1)}, u32[]{:S(2)}) copy-start(bf16[32,8,8,128]{3,2,1,0:T(8,128)(2,1)} %param.7) | copy-start | bytes 1572868
  0.6 11.0 %copy-start.2 = (f32[32]{0:T(128)S(1)}, f32[32]{0:T(128)}, u32[]{:S(2)}) copy-start(f32[32]{0:T(128)} %param.9) | copy-start | bytes 388
  0.7 11.0 %copy-start = (bf16[27,32,32]{2,1,0:T(8,128)(2,1)S(1)}, bf16[27,32,32]{2,1,0:T(8,128)(2,1)}, u32[]{:S(2)}) copy-start(bf16[27,32,32]{2,1,0:T(8,128)(2,1)} %weights.1) | copy-start | bytes 165892
  1.6 6.2 %collective-permute-start = (bf16[8,32,128]{2,1,0:T(8,128)(2,1)S(1)}, bf16[8,32,128]{2,1,0:T(8,128)(2,1)S(1)}, u32[]{:S(2)}, u32[]{:S(2)}) collective-permute-start(bf16[8,32,128]{2,1,0:T(8,128)(2,1)S(1)} %bitcast.67), channel_id=1, source_target_pairs={{0,8},{8,16},{16,24},{24,0},{1,9},{9,17},{17,25},{25,1},{2,10},{10... | collective-permute-start | bytes 196616 | tf_op jit(solution)/shard_map/ppermute | solution.py:35
  4.7 4.7 %collective-permute-start.1 = (bf16[8,32,128]{2,1,0:T(8,128)(2,1)S(1)}, bf16[8,32,128]{2,1,0:T(8,128)(2,1)S(1)}, u32[]{:S(2)}, u32[]{:S(2)}) collective-permute-start(bf16[8,32,128]{2,1,0:T(8,128)(2,1)S(1)} %bitcast.68), channel_id=1, source_target_pairs={{8,0},{16,8},{24,16},{0,24},{9,1},{17,9},{25,17},{1,25},{10,2},{18... | collective-permute-start | bytes 196616 | tf_op jit(solution)/shard_map/ppermute | solution.py:36
  9.4 6.2 %collective-permute-start.2 = (bf16[10,32,128]{2,1,0:T(8,128)(2,1)S(1)}, bf16[10,32,128]{2,1,0:T(8,128)(2,1)S(1)}, u32[]{:S(2)}, u32[]{:S(2)}) collective-permute-start(bf16[10,32,128]{2,1,0:T(8,128)(2,1)S(1)} %get-tuple-element.32), channel_id=1, source_target_pairs={{0,7},{1,2},{2,1},{3,4},{4,3},{5,6},{6,5},{7,0},{8,15},{9,10},{10,... | collective-permute-start | bytes 245768 | tf_op jit(solution)/shard_map/ppermute | solution.py:47
  11.6 4.0 %collective-permute-start.3 = (bf16[10,32,128]{2,1,0:T(8,128)(2,1)S(1)}, bf16[10,32,128]{2,1,0:T(8,128)(2,1)S(1)}, u32[]{:S(2)}, u32[]{:S(2)}) collective-permute-start(bf16[10,32,128]{2,1,0:T(8,128)(2,1)S(1)} %get-tuple-element.31), channel_id=1, source_target_pairs={{0,1},{1,0},{2,3},{3,2},{4,5},{5,4},{6,7},{7,6},{8,9},{9,8},{10,11... | collective-permute-start | bytes 245768 | tf_op jit(solution)/shard_map/ppermute | solution.py:48
  15.7 7.9 %copy-start.6 = (bf16[27,128,64]{1,2,0:T(8,128)(2,1)S(1)}, bf16[27,128,64]{1,2,0:T(8,128)(2,1)}, u32[]{:S(2)}) copy-start(bf16[27,128,64]{1,2,0:T(8,128)(2,1)} %param.12) | copy-start | bytes 1327108
  15.7 12.9 %copy-start.1 = (bf16[27,64,32]{1,2,0:T(8,128)(2,1)S(1)}, bf16[27,64,32]{1,2,0:T(8,128)(2,1)}, u32[]{:S(2)}) copy-start(bf16[27,64,32]{1,2,0:T(8,128)(2,1)} %param.10) | copy-start | bytes 331780
  15.7 12.9 %copy-start.3 = (f32[64]{0:T(128)S(1)}, f32[64]{0:T(128)}, u32[]{:S(2)}) copy-start(f32[64]{0:T(128)} %param.11) | copy-start | bytes 772
  17.2 4.9 %collective-permute-start.4 = (bf16[4,32,128]{2,1,0:T(8,128)(2,1)S(1)}, bf16[4,32,128]{2,1,0:T(8,128)(2,1)S(1)}, u32[]{:S(2)}, u32[]{:S(2)}) collective-permute-start(bf16[4,32,128]{2,1,0:T(8,128)(2,1)S(1)} %get-tuple-element.36), channel_id=1, source_target_pairs={{0,8},{8,16},{16,24},{24,0},{1,9},{9,17},{17,25},{25,1},{2,10},{10... | collective-permute-start | bytes 98312 | tf_op jit(solution)/shard_map/ppermute | solution.py:35
  19.3 3.9 %collective-permute-start.5 = (bf16[4,32,128]{2,1,0:T(8,128)(2,1)S(1)}, bf16[4,32,128]{2,1,0:T(8,128)(2,1)S(1)}, u32[]{:S(2)}, u32[]{:S(2)}) collective-permute-start(bf16[4,32,128]{2,1,0:T(8,128)(2,1)S(1)} %get-tuple-element.35), channel_id=1, source_target_pairs={{8,0},{16,8},{24,16},{0,24},{9,1},{17,9},{25,17},{1,25},{10,2},{18... | collective-permute-start | bytes 98312 | tf_op jit(solution)/shard_map/ppermute | solution.py:36
  23.2 5.4 %collective-permute-start.6 = (bf16[6,32,128]{2,1,0:T(8,128)(2,1)S(1)}, bf16[6,32,128]{2,1,0:T(8,128)(2,1)S(1)}, u32[]{:S(2)}, u32[]{:S(2)}) collective-permute-start(bf16[6,32,128]{2,1,0:T(8,128)(2,1)S(1)} %get-tuple-element.40), channel_id=1, source_target_pairs={{0,7},{1,2},{2,1},{3,4},{4,3},{5,6},{6,5},{7,0},{8,15},{9,10},{10,... | collective-permute-start | bytes 147464 | tf_op jit(solution)/shard_map/ppermute | solution.py:47
  23.6 5.0 %collective-permute-start.7 = (bf16[6,32,128]{2,1,0:T(8,128)(2,1)S(1)}, bf16[6,32,128]{2,1,0:T(8,128)(2,1)S(1)}, u32[]{:S(2)}, u32[]{:S(2)}) collective-permute-start(bf16[6,32,128]{2,1,0:T(8,128)(2,1)S(1)} %get-tuple-element.39), channel_id=1, source_target_pairs={{0,1},{1,0},{2,3},{3,2},{4,5},{5,4},{6,7},{7,6},{8,9},{9,8},{10,11... | collective-permute-start | bytes 147464 | tf_op jit(solution)/shard_map/ppermute | solution.py:48
  30.1 10.9 %copy-start.4 = (f32[128]{0:T(128)S(1)}, f32[128]{0:T(128)}, u32[]{:S(2)}) copy-start(f32[128]{0:T(128)} %param.13) | copy-start | bytes 1540
  30.1 10.9 %all-to-all-start = ((bf16[32,16,128]{2,1,0:T(8,128)(2,1)}), bf16[32,16,128]{2,1,0:T(8,128)(2,1)S(1)}, u32[]{:S(2)}, u32[]{:S(2)}) async-start(bf16[32,16,128]{2,1,0:T(8,128)(2,1)} %bitcast.19), calls=%async_computation | async-start | bytes 262144 | tf_op jit(solution)/shard_map/all_to_all | solution.py:369

commit v3 on v2

--- a/solution.py
+++ b/solution.py
@@ -7,6 +7,7 @@
 from jax.experimental.pallas import tpu as pltpu
 from jax.sharding import PartitionSpec as P
 
+
 VMEM = pl.BlockSpec(memory_space=pltpu.VMEM)
 BF16 = jnp.bfloat16
 F32 = jnp.float32
@@ -40,22 +41,21 @@
 def pair_exchange(low, high, axis):
     count = lax.axis_size(axis)
     if count % 2:
-        return shift_exchange(low, high, axis)
+        far, near_rim = shift_exchange(low, high, axis)
+        return near_rim, far, jnp.bool_(True)
     even = lax.axis_index(axis) % 2 == 0
     inner = [(i, i + 1 if i % 2 == 0 else i - 1) for i in range(count)]
     outer = [(i, (i - 1) % count if i % 2 == 0 else (i + 1) % count) for i in range(count)]
-    from_outer = lax.ppermute(jnp.where(even, low, high), axis, outer)
-    from_inner = lax.ppermute(jnp.where(even, high, low), axis, inner)
-    below = jnp.where(even, from_outer, from_inner)
-    above = jnp.where(even, from_inner, from_outer)
-    return below, above
+    far = lax.ppermute(jnp.where(even, low, high), axis, outer)
+    near_rim = lax.ppermute(jnp.where(even, high, low), axis, inner)
+    return near_rim, far, even
 
 
 def mix_two(mix, bias, pool, stacked, channels, depth):
     result = jnp.dot(mix, stacked, preferred_element_type=F32)
     result = leaky(result + bias).astype(BF16)
     answers = []
-    for half in range(2):
+    for half in range(result.shape[1] // depth):
         block = result[:, half * depth : (half + 1) * depth]
         sums = jnp.dot(block, pool, preferred_element_type=F32)
         mean = sums[:channels]
@@ -106,8 +106,8 @@
     pool = pool_two(depth)
     matrix = mix[...]
     blocks = [(x, y) for x in range(0, extent_x, 2) for y in range(2, extent_y - 2, 2)]
-    for pair in range(0, len(blocks), 2):
-        both = blocks[pair : pair + 2]
+    for pair in range(0, len(blocks), 4):
+        both = blocks[pair : pair + 4]
         stacked = jnp.concatenate(
             [
                 rolled[:, x : x + 4, y - 1 : y + 3].reshape(48 * channels, depth)
@@ -124,34 +124,64 @@
             pooled[x // 2, y // 2 - 1] = mean
 
 
-def rim_two_kernel(rolled, below, above, inner, inner_pooled, mix, bias, out, pooled, rim):
+def rim_two_kernel(side, rolled, halo, mix, bias, out, pooled, band):
     _, wide_x, extent_y, channels, depth = rolled.shape
-    extent_x = wide_x - 2
-    for x in range(wide_x):
-        for side, source in enumerate((below, above)):
-            for e, turned in enumerate(shifts(source[x])):
-                rim[side, e, x] = turned
+    extent_x, width = wide_x - 2, halo.shape[1]
     offset = jnp.concatenate([column(bias)] * 4, axis=0)
     pool = pool_two(depth)
     matrix = mix[...]
-    for x in range(0, extent_x, 2):
-        low, high = [], []
-        for e in range(3):
-            for at in range(x, x + 4):
-                low.append(rim[0, e, at])
-                low.append(rolled[e, at, 0:3].reshape(3 * channels, depth))
-                high.append(rolled[e, at, extent_y - 3 : extent_y].reshape(3 * channels, depth))
-                high.append(rim[1, e, at])
-        stacked = jnp.concatenate(
-            [jnp.concatenate(low, axis=0), jnp.concatenate(high, axis=0)], axis=1
-        )
-        answers = mix_two(matrix, offset, pool, stacked, channels, depth)
-        for y, (block, mean) in zip((0, extent_y - 2), answers):
-            for part in range(4):
-                out[x + part // 2, y + part % 2] = block[part * channels : (part + 1) * channels]
-            pooled[x // 2, y // 2] = mean
-    out[:, 2 : extent_y - 2] = inner[...]
-    pooled[:, 1 : extent_y // 2 - 1] = inner_pooled[...]
+
+    def fill(x):
+        for row in range(width):
+            for e, turned in enumerate(shifts(halo[x, row])):
+                band[e, x, row] = turned
+
+    def edge(above):
+        def rows(e, x, first):
+            if above:
+                start = extent_y - width + first
+                pieces = [rolled[e, x, start:extent_y], band[e, x, : first + 4 - width]]
+            else:
+                pieces = [band[e, x, first:], rolled[e, x, : first + 4 - width]]
+            return [piece.reshape(-1, depth) for piece in pieces]
+
+        for x in range(wide_x):
+            fill(x)
+        blocks = [(x, first) for x in range(0, extent_x, 2) for first in (0, 2)]
+        for group in range(0, len(blocks), 4):
+            some = blocks[group : group + 4]
+            stacked = jnp.concatenate(
+                [
+                    jnp.concatenate(
+                        [
+                            piece
+                            for e in range(3)
+                            for at in range(x, x + 4)
+                            for piece in rows(e, at, first)
+                        ],
+                        axis=0,
+                    )
+                    for x, first in some
+                ],
+                axis=1,
+            )
+            answers = mix_two(matrix, offset, pool, stacked, channels, depth)
+            for (x, first), (block, mean) in zip(some, answers):
+                own = (first == 0) == above
+                if own:
+                    for part in range(4):
+                        out[x + part // 2, part % 2] = block[
+                            part * channels : (part + 1) * channels
+                        ]
+                pooled[0 if own else 1, x // 2] = mean
+
+    @pl.when(side[0] == 1)
+    def _():
+        edge(True)
+
+    @pl.when(side[0] == 0)
+    def _():
+        edge(False)
 
 
 def inner_two(cells, left, right, weights, bias):
@@ -172,40 +202,35 @@
     )(near(cells), near(left), near(right), near(weights), near(bias))
 
 
-def rim_two(rolled, below, above, inner, inner_pooled, mix, bias):
-    _, wide_x, extent_y, channels, depth = rolled.shape
-    extent_x = wide_x - 2
+def rim_two(side, rolled, halo, mix, bias):
+    _, wide_x, _, channels, depth = rolled.shape
+    extent_x, width = wide_x - 2, halo.shape[1]
     return pl.pallas_call(
         rim_two_kernel,
         name="rim_two",
         out_shape=(
-            local((extent_x, extent_y, channels, depth)),
-            local((extent_x // 2, extent_y // 2, channels, depth)),
+            local((extent_x, 2, channels, depth)),
+            local((2, extent_x // 2, channels, depth)),
         ),
-        in_specs=[VMEM] * 7,
+        in_specs=[pl.BlockSpec(memory_space=pltpu.SMEM)] + [VMEM] * 4,
         out_specs=(VMEM,) * 2,
-        scratch_shapes=[pltpu.VMEM((2, 3, wide_x, channels, depth), BF16)],
+        scratch_shapes=[pltpu.VMEM((3, wide_x, width, channels, depth), BF16)],
         cost_estimate=COST,
         compiler_params=pltpu.CompilerParams(vmem_limit_bytes=16 << 20),
-    )(*map(near, (rolled, below, above, inner, inner_pooled, mix, bias)))
-
-
-def three_kernel(layers, cells, left, right, below, above, mix, bias, out, windows, paired):
-    extent_x, extent_y, channels, lanes = cells.shape
+    )(side, *map(near, (rolled, halo, mix, bias)))
+
+
+def three_kernel(layers, cells, left, right, mix, bias, out, windows, paired):
+    extent_x, wide_y, channels, lanes = cells.shape
+    extent_y = wide_y - 2
     depth = lanes // 2
-    out_channels = mix.shape[1]
     senders, slots = windows.shape[:2]
 
     def place(x, y):
-        if y == 0:
-            return below[x]
-        if y == extent_y + 1:
-            return above[x]
-        if x == 0:
-            return left[y - 1]
-        if x == extent_x + 1:
-            return right[y - 1]
-        return cells[x - 1, y - 1]
+        if 0 < x < extent_x + 1:
+            return cells[x - 1, y]
+        both = (left if x == 0 else right)[y // 2]
+        return jnp.where(first == (y % 2 == 0), both, pltpu.roll(both, depth, 1))
 
     first = lax.broadcasted_iota(jnp.int32, (channels, lanes), 1) < depth
     for x in range(extent_x + 2):
@@ -237,9 +262,7 @@
                 ],
                 axis=1,
             )
-            result = lax.dot_general(
-                matrix, stacked, (((0,), (0,)), ((), ())), preferred_element_type=F32
-            )
+            result = jnp.dot(matrix, stacked, preferred_element_type=F32)
             result = leaky(result + offset).astype(BF16)
             out[2 * px, py] = result[:, :lanes]
             out[2 * px + 1, py] = result[:, lanes:]
@@ -255,12 +278,13 @@
                 windows[sender, slot, 8 * px : 8 * px + 8] = means[8 * slot : 8 * slot + 8]
 
 
-def three(cells, left, right, below, above, weights, bias_values, count_x, count_y):
-    extent_x, extent_y, channels, lanes = cells.shape
+def three(cells, left, right, weights, bias_values, count_x, count_y):
+    extent_x, wide_y, channels, lanes = cells.shape
+    extent_y = wide_y - 2
     depth = lanes // 2
     out_channels = weights.shape[1]
     layers = depth // 2 // count_y
-    mix = weights.transpose(0, 2, 1).reshape(27 * channels, out_channels)
+    mix = weights.transpose(1, 0, 2).reshape(out_channels, 27 * channels)
     return pl.pallas_call(
         functools.partial(three_kernel, layers),
         name="three",
@@ -268,21 +292,22 @@
             local((extent_x, extent_y // 2, out_channels, lanes)),
             local((count_x, count_y, extent_x // 2 * 8, extent_y // 2 * out_channels)),
         ),
-        in_specs=[VMEM] * 7,
+        in_specs=[VMEM] * 5,
         out_specs=(VMEM, VMEM),
         scratch_shapes=[pltpu.VMEM((extent_x + 2, extent_y + 1, 3, channels, lanes), BF16)],
         cost_estimate=COST,
         compiler_params=pltpu.CompilerParams(vmem_limit_bytes=16 << 20),
-    )(*map(near, (cells, left, right, below, above, mix, bias_values)))
-
-
-def four_kernel(count_y, tiles, mix, bias, out, rolled):
-    sources, parts, lanes = tiles.shape
+    )(*map(near, (cells, left, right, mix, bias_values)))
+
+
+def four_kernel(count_y, tiles, weights, bias, out, rolled, mix):
+    _, parts, lanes = tiles.shape
     extent_x, extent_y, layers, out_channels = out.shape
     rows = count_y * 8
     inner_x = parts // 8
     half = lanes // 2
     upper = lax.broadcasted_iota(jnp.int32, (rows, lanes), 1) >= half
+    short = count_y * layers
     for x in range(extent_x):
         start = x // inner_x * count_y
         at = x % inner_x * 8
@@ -293,85 +318,103 @@
         whole = jnp.concatenate([value, around], axis=1)
         for e in range(3):
             turned = whole if e == 0 else pltpu.roll(whole, rows - e, 0)
+            turned = turned.reshape(count_y, 8, 2 * lanes)[:, :layers].reshape(short, 2 * lanes)
             rolled[x + 1, :, e * 2 * lanes : (e + 1) * 2 * lanes] = turned.astype(BF16)
     rolled[0] = rolled[extent_x]
     rolled[extent_x + 1] = rolled[1]
+    bands = ((1, 0), (2, 1), (0, None), (None, 2))
+    for a in range(3):
+        for e in range(3):
+            for band, taps in enumerate(bands):
+                row = ((3 * a + e) * 4 + band) * half
+                for index, c in enumerate(taps):
+                    lane = index * out_channels
+                    if c is None:
+                        tap = jnp.zeros((half, out_channels), BF16)
+                    else:
+                        tap = weights[9 * a + 3 * c + e]
+                    mix[row : row + half, lane : lane + out_channels] = tap
     offset = jnp.concatenate([bias[...], bias[...]], axis=1)
     matrix = mix[...]
-    for x in range(0, extent_x, 2):
+    group = min(extent_x, 4)
+    for x in range(0, extent_x, group):
         stacked = jnp.concatenate(
-            [rolled[x + a : x + a + 2].reshape(2 * rows, 6 * lanes) for a in range(3)], axis=1
+            [rolled[x + a : x + a + group].reshape(group * short, 6 * lanes) for a in range(3)],
+            axis=1,
         )
         result = jnp.dot(stacked, matrix, preferred_element_type=F32)
         result = leaky(result + offset).astype(BF16)
-        for dx in range(2):
+        for dx in range(group):
             for y in range(extent_y):
-                row = dx * rows + y // 2 * 8
+                row = dx * short + y // 2 * layers
                 lane = y % 2 * out_channels
                 out[x + dx, y] = result[row : row + layers, lane : lane + out_channels]
 
 
-def mix_four(weights):
-    channels, out_channels = weights.shape[2], weights.shape[1]
-    taps = weights.transpose(0, 2, 1).reshape(3, 3, 3, channels, out_channels)
-    blank = jnp.zeros_like(taps[:, 0])
-    bands = [
-        jnp.concatenate(pair, axis=3)
-        for pair in (
-            (taps[:, 1], taps[:, 0]),
-            (taps[:, 2], taps[:, 1]),
-            (taps[:, 0], blank),
-            (blank, taps[:, 2]),
-        )
-    ]
-    return jnp.concatenate(bands, axis=2).reshape(36 * channels, 2 * out_channels)
-
-
-def four(tiles, mix, bias, extents, count_y):
+def four(tiles, weights, bias, extents, count_y):
     extent_x, extent_y, layers = extents
-    out_channels = mix.shape[1] // 2
+    _, channels, out_channels = weights.shape
     return pl.pallas_call(
         functools.partial(four_kernel, count_y),
         name="four",
         out_shape=jax.ShapeDtypeStruct((extent_x, extent_y, layers, out_channels), BF16),
         in_specs=[VMEM] * 3,
         out_specs=VMEM,
-        scratch_shapes=[pltpu.VMEM((extent_x + 2, count_y * 8, 6 * tiles.shape[2]), BF16)],
+        scratch_shapes=[
+            pltpu.VMEM((extent_x + 2, count_y * layers, 6 * tiles.shape[2]), BF16),
+            pltpu.VMEM((36 * channels, 2 * out_channels), BF16),
+        ],
         cost_estimate=COST,
         compiler_params=pltpu.CompilerParams(vmem_limit_bytes=16 << 20),
-    )(near(tiles), near(mix), near(bias))
-
-
-def rows_of(left, cells, right):
-    low = jnp.concatenate([left[:1], cells[:, 0], right[:1]], axis=0)
-    high = jnp.concatenate([left[-1:], cells[:, -1], right[-1:]], axis=0)
+    )(near(tiles), near(weights), near(bias))
+
+
+def rows_of(left, cells, right, width):
+    low = jnp.concatenate([left[None, :width], cells[:, :width], right[None, :width]], axis=0)
+    high = jnp.concatenate([left[None, -width:], cells[:, -width:], right[None, -width:]], axis=0)
     return low, high
 
 
 def shards(features, weight_two, bias_two, weight_three, bias_three, weight_four, bias_four):
     count_x, count_y = lax.axis_size("gx"), lax.axis_size("gy")
-    left, right = shift_exchange(
-        features[:, 0].transpose(1, 0, 2), features[:, -1].transpose(1, 0, 2), "gx"
+    low, high, features = lax.optimization_barrier((features[:, 0], features[:, -1], features))
+    left, right = shift_exchange(low.transpose(1, 0, 2), high.transpose(1, 0, 2), "gx")
+    cells = features.transpose(1, 2, 0, 3)
+    near_rim, far_rim, even = pair_exchange(*rows_of(left, cells, right, 3), "gy")
+    bias = bias_two[None, :]
+    inner, inner_pooled, rolled, mix = inner_two(cells, left, right, weight_two, bias)
+    side = even.astype(jnp.int32)[None]
+    near_out, near_pooled = rim_two(side, rolled, near_rim, mix, bias)
+    far_out, far_pooled = rim_two(1 - side, rolled, far_rim, mix, bias)
+    low_pooled = jnp.where(even, far_pooled, near_pooled)
+    high_pooled = jnp.where(even, near_pooled, far_pooled)
+    pooled = jnp.concatenate(
+        [
+            low_pooled[1][:, None],
+            low_pooled[0][:, None],
+            inner_pooled,
+            high_pooled[0][:, None],
+            high_pooled[1][:, None],
+        ],
+        axis=1,
     )
-    cells = features.transpose(1, 2, 0, 3)
-    below, above = pair_exchange(*rows_of(left, cells, right), "gy")
-    inner, inner_pooled, rolled, mix = inner_two(
-        cells, left, right, weight_two, bias_two[None, :]
-    )
-    level_two, pooled = rim_two(rolled, below, above, inner, inner_pooled, mix, bias_two[None, :])
-
-    left, right = shift_exchange(pooled[0], pooled[-1], "gx")
-    below, above = pair_exchange(*rows_of(left, pooled, right), "gy")
+    low_out = jnp.where(even, far_out, near_out)
+    high_out = jnp.where(even, near_out, far_out)
+    level_two = jnp.concatenate([low_out, inner, high_out], axis=1)
+
+    first = jnp.arange(pooled.shape[3]) < pooled.shape[3] // 2
+    low, high = [jnp.where(first, face[0::2], face[1::2]) for face in (pooled[0], pooled[-1])]
+    left, right = shift_exchange(low, high, "gx")
     level_three, windows = three(
-        pooled, left, right, below, above, weight_three, bias_three[None, :], count_x, count_y
+        pooled, left, right, weight_three, bias_three[None, :], count_x, count_y
     )
     slots = count_x * count_y
     tiles = lax.all_to_all(
         windows.reshape((slots,) + windows.shape[2:]), ("gx", "gy"), 0, 0, tiled=True
     )
-    extent_x, extent_y, channels, depth = level_two.shape
+    extent_x, extent_y, _, depth = level_two.shape
     extents = (count_x * extent_x // 4, count_y * extent_y // 4, depth // 4 // count_y)
-    bottleneck = four(tiles, mix_four(weight_four), bias_four[None, :], extents, count_y)
+    bottleneck = four(tiles, weight_four.transpose(0, 2, 1), bias_four[None, :], extents, count_y)
     out_three = level_three.reshape(level_three.shape[:3] + (2, level_three.shape[3] // 2))
     out_three = out_three.transpose(2, 0, 1, 3, 4)
     out_three = out_three.reshape(out_three.shape[:2] + (-1, out_three.shape[4]))

time: 42.7 us -> 41.4 us (0.970)
  waiting for transfers between devices: 18.2 us -> 14.5 us
  starting transfers between devices: 12.3 us -> 14.9 us
    ppermute x4 -> x2, waiting for transfers between devices: 7.32 us -> 3.48 us  [the longest x1 3.48 us: pair_exchange(): far = lax.ppermute(jnp.where(even, low, high), axis, outer)]
    all_to_all x1, starting transfers between devices: 2.71 us -> 4.13 us  [shards(): lax.all_to_all(windows.reshape((slots,) + windows.shape[2:]), ('gx', 'gy'...]
    optimization_barrier x0 -> x1, local copies, waits for them, and re-layouts: none -> 1.38 us  [shards(): lax.optimization_barrier((features[:, 0], features[:, -1], features))]
    unnamed x18 -> x17, local copies, waits for them, and re-layouts: 2.44 us -> 1.07 us
    ppermute x4 -> x2, starting transfers between devices: 2.61 us -> 3.77 us  [the longest x1 3.7 us: pair_exchange(): far = lax.ppermute(jnp.where(even, low, high), axis, outer)]
    ppermute x2, waiting for transfers between devices: 2.59 us -> 3.3 us  [shift_exchange(): lax.ppermute(low, axis, [((i + 1) % count, i) for i in range(count)])]
    ppermute x2, waiting for transfers between devices: 2.29 us -> 1.66 us  [shift_exchange(): lax.ppermute(high, axis, [(i, (i + 1) % count) for i in range(count)])]
    pallas_call x1 -> x2, Pallas kernels: 1.5 us -> 2.09 us  [rim_two(): pl.pallas_call(rim_two_kernel, name='rim_two', out_shape=(local((extent_x...]
  transfers between devices with their start and end apart: 9 -> 7, of which waited for: 7 -> 5; matrix products, arithmetic and copies ran while one was open for 9% -> 9% of each run, Pallas kernels for 4% -> 5%
where the time goes in v3:
time: 41.4 us; the launch traced here: 41.2 us
  starting transfers between devices  14.9 us (36%)
  waiting for transfers between devices  14.5 us (35%)
  Pallas kernels  6.13 us (15%)
  local copies, waits for them, and re-layouts  4.61 us (11%)
  between operations  0.82 us (2%)
    all_to_all x1, waiting for transfers between devices, shards(): lax.all_to_all(windows.reshape((slots,) + windows.shape[2:]), ('gx', 'gy'...  6.03 us
    ppermute x2, starting transfers between devices, shift_exchange(): lax.ppermute(high, axis, [(i, (i + 1) % count) for i in range(count)])  5.02 us
    all_to_all x1, starting transfers between devices, shards(): lax.all_to_all(windows.reshape((slots,) + windows.shape[2:]), ('gx', 'gy'...  4.13 us
    ppermute x1, starting transfers between devices, pair_exchange(): far = lax.ppermute(jnp.where(even, low, high), axis, outer)  3.7 us
    ppermute x1, waiting for transfers between devices, pair_exchange(): far = lax.ppermute(jnp.where(even, low, high), axis, outer)  3.48 us
    ppermute x2, waiting for transfers between devices, shift_exchange(): lax.ppermute(low, axis, [((i + 1) % count, i) for i in range(count)])  3.3 us
    pallas_call x2, Pallas kernels, rim_two(): pl.pallas_call(rim_two_kernel, name='rim_two', out_shape=(local((extent_x...  2.09 us
    ppermute x2, starting transfers between devices, shift_exchange(): lax.ppermute(low, axis, [((i + 1) % count, i) for i in range(count)])  2 us
  transfers between devices with their start and end apart: 7, of which 5 were waited for; matrix products, arithmetic and copies ran while one was open for 9% of the time, Pallas kernels for 5%

profile of v3, /device:TPU:0, one launch (start us, length us, event | category | flops | bytes accessed | tf_op | source)
XLA Modules:
  0.0 41.2 jit_solution(1402428367590896411)
XLA Ops:
  0.6 0.0 copy-start.1
  0.6 0.0 copy-start.2
  0.7 0.9 %fusion.5 = (bf16[32,1,8,128]{3,2,1,0:T(8,128)(2,1)S(1)}, bf16[32,1,8,128]{3,2,1,0:T(8,128)(2,1)S(1)}) fusion(bf16[32,8,8,128]{3,2,1,0:T(8,128)(2,1)} %param.7), kind=kLoop, calls=%fused_computation.31 | loop fusion | bytes 262144 | tf_op jit(solution)/shard_map/slice | solution.py:380
  1.6 3.0 %collective-permute-start = (bf16[8,32,128]{2,1,0:T(8,128)(2,1)S(1)}, bf16[8,32,128]{2,1,0:T(8,128)(2,1)S(1)}, u32[]{:S(2)}, u32[]{:S(2)}) collective-permute-start(bf16[8,32,128]{2,1,0:T(8,128)(2,1)S(1)} %bitcast.70), channel_id=1, source_target_pairs={{0,8},{8,16},{16,24},{24,0},{1,9},{9,17},{17,25},{25,1},{2,10},{10... | collective-permute-start | bytes 196616 | tf_op jit(solution)/shard_map/ppermute | solution.py:36
  4.6 1.0 %collective-permute-start.1 = (bf16[8,32,128]{2,1,0:T(8,128)(2,1)S(1)}, bf16[8,32,128]{2,1,0:T(8,128)(2,1)S(1)}, u32[]{:S(2)}, u32[]{:S(2)}) collective-permute-start(bf16[8,32,128]{2,1,0:T(8,128)(2,1)S(1)} %bitcast.71), channel_id=1, source_target_pairs={{8,0},{16,8},{24,16},{0,24},{9,1},{17,9},{25,17},{1,25},{10,2},{18... | collective-permute-start | bytes 196616 | tf_op jit(solution)/shard_map/ppermute | solution.py:37
  5.6 1.4 %copy.33 = bf16[32,8,8,128]{3,0,2,1:T(8,128)(2,1)S(1)} copy(bf16[32,8,8,128]{3,2,1,0:T(8,128)(2,1)} %param.7) | data formatting | bytes 1048576 | tf_op jit(solution)/shard_map/optimization_barrier | solution.py:380
  7.1 2.2 %collective-permute-done.1.right = bf16[8,32,128]{2,1,0:T(8,128)(2,1)S(1)} collective-permute-done((bf16[8,32,128]{2,1,0:T(8,128)(2,1)S(1)}, bf16[8,32,128]{2,1,0:T(8,128)(2,1)S(1)}, u32[]{:S(2)}, u32[]{:S(2)}) %collective-permute-start.1) | collective-permute-done | bytes 65568 | tf_op jit(solution)/shard_map/ppermute | solution.py:37
  9.3 0.0 collective-permute-done.left
  9.4 0.1 broadcast_select_fusion.1
  9.4 0.1 collective-permute-start.3
  9.5 3.7 %collective-permute-start.2 = (bf16[10,3,32,128]{3,2,1,0:T(8,128)(2,1)S(1)}, bf16[10,3,32,128]{3,2,1,0:T(8,128)(2,1)S(1)}, u32[]{:S(2)}, u32[]{:S(2)}) collective-permute-start(bf16[10,3,32,128]{3,2,1,0:T(8,128)(2,1)S(1)} %get-tuple-element.39), channel_id=1, source_target_pairs={{0,7},{1,2},{2,1},{3,4},{4,3},{5,6},{6,5},{7,0},{8,15},{9,10},{10,... | collective-permute-start | bytes 737288 | tf_op jit(solution)/shard_map/ppermute | solution.py:49
  13.2 0.0 copy-done.1
  13.2 0.0 copy-done.2
  13.2 1.2 %inner_two.1 = (bf16[8,4,32,128]{3,2,1,0:T(8,128)(2,1)S(1)}, bf16[4,2,32,128]{3,2,1,0:T(8,128)(2,1)S(1)}, bf16[3,10,8,32,128]{4,3,2,1,0:T(8,128)(2,1)S(1)}, bf16[128,1536]{1,0:T(8,128)(2,1)S(1)}) custom-call(bf16[8,8,32,128]{3,2,1,0:T(8,128)(2,1)S(1)} %bitcast.60, bf16[8,32,128]{2,1,0:T(8,128)(2,1)S(1)} %collective-permute-done.left, ...), custom_call_target="tpu_custom_call" | custom-call | flops 1073741824 | bytes 1048576 | tf_op jit(solution)/shard_map/inner_two/pallas_call | solution.py:189
  14.4 0.0 collective-permute-done.3.halo
  14.4 1.0 %rim_two.3 = (bf16[8,2,32,128]{3,2,1,0:T(8,128)(2,1)S(1)}, bf16[2,4,32,128]{3,2,1,0:T(8,128)(2,1)S(1)}) custom-call(s32[1]{0:T(128)} %bitcast.side, bf16[3,10,8,32,128]{4,3,2,1,0:T(8,128)(2,1)S(1)} %get-tuple-element.19.rolled, bf16[10,3,32,128]{3,2,1,0:T(8,128)(2,1)S(1)} %collective-permute-done.3.halo, bf16[128,1536]{1,0:T(8,128)(2,1)S(1)} %get-tuple-element.20.mix, ...), custom_call_target="tpu_custom_call" | custom-call | flops 1073741824 | bytes 1048576 | tf_op jit(solution)/shard_map/rim_two/pallas_call | solution.py:208
  15.5 0.0 copy-start.3
  15.5 3.5 %collective-permute-done.2.halo = bf16[10,3,32,128]{3,2,1,0:T(8,128)(2,1)S(1)} collective-permute-done((bf16[10,3,32,128]{3,2,1,0:T(8,128)(2,1)S(1)}, bf16[10,3,32,128]{3,2,1,0:T(8,128)(2,1)S(1)}, u32[]{:S(2)}, u32[]{:S(2)}) %collective-permute-start.2) | collective-permute-done | bytes 245792 | tf_op jit(solution)/shard_map/ppermute | solution.py:49
  19.0 1.0 %rim_two.2 = (bf16[8,2,32,128]{3,2,1,0:T(8,128)(2,1)S(1)}, bf16[2,4,32,128]{3,2,1,0:T(8,128)(2,1)S(1)}) custom-call(s32[1]{0:T(128)S(6)} %sub.3.side, bf16[3,10,8,32,128]{4,3,2,1,0:T(8,128)(2,1)S(1)} %get-tuple-element.19.rolled, bf16[10,3,32,128]{3,2,1,0:T(8,128)(2,1)S(1)} %collective-permute-done.2.halo, bf16[128,1536]{1,0:T(8,128)(2,1)S(1)} %get-tuple-element.20.mix, ...), custom_call_target="tpu_custom_call" | custom-call | flops 1073741824 | bytes 1048576 | tf_op jit(solution)/shard_map/rim_two/pallas_call | solution.py:208
  20.2 2.0 %collective-permute-start.4 = (bf16[3,32,128]{2,1,0:T(8,128)(2,1)S(1)}, bf16[3,32,128]{2,1,0:T(8,128)(2,1)S(1)}, u32[]{:S(2)}, u32[]{:S(2)}) collective-permute-start(bf16[3,32,128]{2,1,0:T(8,128)(2,1)S(1)} %get-tuple-element.52), channel_id=1, source_target_pairs={{0,8},{8,16},{16,24},{24,0},{1,9},{9,17},{17,25},{25,1},{2,10},{10... | collective-permute-start | bytes 73736 | tf_op jit(solution)/shard_map/ppermute | solution.py:36
  22.2 1.0 %collective-permute-start.5 = (bf16[3,32,128]{2,1,0:T(8,128)(2,1)S(1)}, bf16[3,32,128]{2,1,0:T(8,128)(2,1)S(1)}, u32[]{:S(2)}, u32[]{:S(2)}) collective-permute-start(bf16[3,32,128]{2,1,0:T(8,128)(2,1)S(1)} %get-tuple-element.51), channel_id=1, source_target_pairs={{8,0},{16,8},{24,16},{0,24},{9,1},{17,9},{25,17},{1,25},{10,2},{18... | collective-permute-start | bytes 73736 | tf_op jit(solution)/shard_map/ppermute | solution.py:37
  23.2 0.1 copy.25.mix
  23.3 1.7 %collective-permute-done.4.left = bf16[3,32,128]{2,1,0:T(8,128)(2,1)S(1)} collective-permute-done((bf16[3,32,128]{2,1,0:T(8,128)(2,1)S(1)}, bf16[3,32,128]{2,1,0:T(8,128)(2,1)S(1)}, u32[]{:S(2)}, u32[]{:S(2)}) %collective-permute-start.4) | collective-permute-done | bytes 24608 | tf_op jit(solution)/shard_map/ppermute | solution.py:36
  25.0 1.1 %collective-permute-done.5.right = bf16[3,32,128]{2,1,0:T(8,128)(2,1)S(1)} collective-permute-done((bf16[3,32,128]{2,1,0:T(8,128)(2,1)S(1)}, bf16[3,32,128]{2,1,0:T(8,128)(2,1)S(1)}, u32[]{:S(2)}, u32[]{:S(2)}) %collective-permute-start.5) | collective-permute-done | bytes 24608 | tf_op jit(solution)/shard_map/ppermute | solution.py:37
  26.0 1.5 %three.1 = (bf16[4,2,64,128]{3,2,1,0:T(8,128)(2,1)S(1)}, bf16[4,8,16,128]{3,2,1,0:T(8,128)(2,1)}) custom-call(bf16[4,6,32,128]{3,2,1,0:T(8,128)(2,1)S(1)} %fusion.cells, bf16[3,32,128]{2,1,0:T(8,128)(2,1)S(1)} %collective-permute-done.4.left, bf16[3,32,128]{2,1,0:T(8,128)(2,1)S(1)} %collective-permute-done.5.right, bf16[64,864]{1,0:T(8,128)(2,1)S(1)} %copy.25.mix, ...), custom_call_target="tpu_custom_call" | custom-call | flops 1073741824 | bytes 1048576 | tf_op jit(solution)/shard_map/three/pallas_call | solution.py:288
  27.6 4.1 %all-to-all-start = ((bf16[32,16,128]{2,1,0:T(8,128)(2,1)}), bf16[32,16,128]{2,1,0:T(8,128)(2,1)S(1)}, u32[]{:S(2)}, u32[]{:S(2)}) async-start(bf16[32,16,128]{2,1,0:T(8,128)(2,1)} %bitcast.26), calls=%async_computation | async-start | bytes 262144 | tf_op jit(solution)/shard_map/all_to_all | solution.py:412
  31.7 0.1 maximum_bitcast_fusion
  31.8 1.0 %copy.27 = bf16[32,8,8,128]{3,2,1,0:T(8,128)(2,1)} copy(bf16[32,8,8,128]{3,0,2,1:T(8,128)(2,1)S(1)} %maximum_bitcast_fusion) | data formatting | bytes 1048576
  32.8 0.1 reshape.19
  32.9 0.9 %copy.26 = bf16[64,4,2,2,64]{4,3,2,1,0:T(2,128)(2,1)} copy(bf16[64,4,2,2,64]{4,3,0,2,1:T(2,128)(2,1)S(1)} %bitcast.67) | data formatting | bytes 262144 | tf_op jit(solution)/shard_map/transpose | solution.py:419
  33.8 6.0 %all-to-all-done.tiles = bf16[32,16,128]{2,1,0:T(8,128)(2,1)S(1)} async-done(((bf16[32,16,128]{2,1,0:T(8,128)(2,1)}), bf16[32,16,128]{2,1,0:T(8,128)(2,1)S(1)}, u32[]{:S(2)}, u32[]{:S(2)}) %all-to-all-start) | async-done | bytes 131104 | tf_op jit(solution)/shard_map/all_to_all | solution.py:412
  39.9 1.3 %four.1 = bf16[8,16,4,128]{3,2,1,0:T(4,128)(2,1)} custom-call(bf16[32,16,128]{2,1,0:T(8,128)(2,1)S(1)} %all-to-all-done.tiles, bf16[27,64,128]{2,1,0:T(8,128)(2,1)S(1)} %bitcast.61, f32[1,128]{1,0:T(1,128)S(1)} %bitcast.66), custom_call_target="tpu_custom_call" | custom-call | flops 1073741824 | bytes 1048576 | tf_op jit(solution)/shard_map/four/pallas_call | solution.py:357
  (21 shorter events, 0.2 us)
Async XLA Ops:
  0.6 12.6 %copy-start.1 = (bf16[27,32,32]{2,1,0:T(8,128)(2,1)S(1)}, bf16[27,32,32]{2,1,0:T(8,128)(2,1)}, u32[]{:S(2)}) copy-start(bf16[27,32,32]{2,1,0:T(8,128)(2,1)} %weights.1) | copy-start | bytes 165892
  0.6 12.6 %copy-start.2 = (f32[32]{0:T(128)S(1)}, f32[32]{0:T(128)}, u32[]{:S(2)}) copy-start(f32[32]{0:T(128)} %param.9) | copy-start | bytes 388
  1.6 7.7 %collective-permute-start = (bf16[8,32,128]{2,1,0:T(8,128)(2,1)S(1)}, bf16[8,32,128]{2,1,0:T(8,128)(2,1)S(1)}, u32[]{:S(2)}, u32[]{:S(2)}) collective-permute-start(bf16[8,32,128]{2,1,0:T(8,128)(2,1)S(1)} %bitcast.70), channel_id=1, source_target_pairs={{0,8},{8,16},{16,24},{24,0},{1,9},{9,17},{17,25},{25,1},{2,10},{10... | collective-permute-start | bytes 196616 | tf_op jit(solution)/shard_map/ppermute | solution.py:36
  4.6 4.7 %collective-permute-start.1 = (bf16[8,32,128]{2,1,0:T(8,128)(2,1)S(1)}, bf16[8,32,128]{2,1,0:T(8,128)(2,1)S(1)}, u32[]{:S(2)}, u32[]{:S(2)}) collective-permute-start(bf16[8,32,128]{2,1,0:T(8,128)(2,1)S(1)} %bitcast.71), channel_id=1, source_target_pairs={{8,0},{16,8},{24,16},{0,24},{9,1},{17,9},{25,17},{1,25},{10,2},{18... | collective-permute-start | bytes 196616 | tf_op jit(solution)/shard_map/ppermute | solution.py:37
  9.4 5.0 %collective-permute-start.3 = (bf16[10,3,32,128]{3,2,1,0:T(8,128)(2,1)S(1)}, bf16[10,3,32,128]{3,2,1,0:T(8,128)(2,1)S(1)}, u32[]{:S(2)}, u32[]{:S(2)}) collective-permute-start(bf16[10,3,32,128]{3,2,1,0:T(8,128)(2,1)S(1)} %get-tuple-element.40), channel_id=1, source_target_pairs={{0,1},{1,0},{2,3},{3,2},{4,5},{5,4},{6,7},{7,6},{8,9},{9,8},{10,11... | collective-permute-start | bytes 737288 | tf_op jit(solution)/shard_map/ppermute | solution.py:50
  9.5 9.5 %collective-permute-start.2 = (bf16[10,3,32,128]{3,2,1,0:T(8,128)(2,1)S(1)}, bf16[10,3,32,128]{3,2,1,0:T(8,128)(2,1)S(1)}, u32[]{:S(2)}, u32[]{:S(2)}) collective-permute-start(bf16[10,3,32,128]{3,2,1,0:T(8,128)(2,1)S(1)} %get-tuple-element.39), channel_id=1, source_target_pairs={{0,7},{1,2},{2,1},{3,4},{4,3},{5,6},{6,5},{7,0},{8,15},{9,10},{10,... | collective-permute-start | bytes 737288 | tf_op jit(solution)/shard_map/ppermute | solution.py:49
  15.5 7.7 %copy-start.5 = (bf16[27,64,32]{1,2,0:T(8,128)(2,1)S(1)}, bf16[27,64,32]{1,2,0:T(8,128)(2,1)}, u32[]{:S(2)}) copy-start(bf16[27,64,32]{1,2,0:T(8,128)(2,1)} %param.10) | copy-start | bytes 331780
  15.5 10.5 %copy-start.3 = (f32[64]{0:T(128)S(1)}, f32[64]{0:T(128)}, u32[]{:S(2)}) copy-start(f32[64]{0:T(128)} %param.11) | copy-start | bytes 772
  20.2 4.8 %collective-permute-start.4 = (bf16[3,32,128]{2,1,0:T(8,128)(2,1)S(1)}, bf16[3,32,128]{2,1,0:T(8,128)(2,1)S(1)}, u32[]{:S(2)}, u32[]{:S(2)}) collective-permute-start(bf16[3,32,128]{2,1,0:T(8,128)(2,1)S(1)} %get-tuple-element.52), channel_id=1, source_target_pairs={{0,8},{8,16},{16,24},{24,0},{1,9},{9,17},{17,25},{25,1},{2,10},{10... | collective-permute-start | bytes 73736 | tf_op jit(solution)/shard_map/ppermute | solution.py:36
  22.2 3.8 %collective-permute-start.5 = (bf16[3,32,128]{2,1,0:T(8,128)(2,1)S(1)}, bf16[3,32,128]{2,1,0:T(8,128)(2,1)S(1)}, u32[]{:S(2)}, u32[]{:S(2)}) collective-permute-start(bf16[3,32,128]{2,1,0:T(8,128)(2,1)S(1)} %get-tuple-element.51), channel_id=1, source_target_pairs={{8,0},{16,8},{24,16},{0,24},{9,1},{17,9},{25,17},{1,25},{10,2},{18... | collective-permute-start | bytes 73736 | tf_op jit(solution)/shard_map/ppermute | solution.py:37
  27.5 12.3 %copy-start = (bf16[27,128,64]{1,2,0:T(8,128)(2,1)S(1)}, bf16[27,128,64]{1,2,0:T(8,128)(2,1)}, u32[]{:S(2)}) copy-start(bf16[27,128,64]{1,2,0:T(8,128)(2,1)} %param.12) | copy-start | bytes 1327108
  27.6 12.3 %copy-start.4 = (f32[128]{0:T(128)S(1)}, f32[128]{0:T(128)}, u32[]{:S(2)}) copy-start(f32[128]{0:T(128)} %param.13) | copy-start | bytes 1540
  27.6 12.3 %all-to-all-start = ((bf16[32,16,128]{2,1,0:T(8,128)(2,1)}), bf16[32,16,128]{2,1,0:T(8,128)(2,1)S(1)}, u32[]{:S(2)}, u32[]{:S(2)}) async-start(bf16[32,16,128]{2,1,0:T(8,128)(2,1)} %bitcast.26), calls=%async_computation | async-start | bytes 262144 | tf_op jit(solution)/shard_map/all_to_all | solution.py:412

commit v4 on v3

v4 whole, which is shorter than its diff:
```python
import functools

import jax
import jax.numpy as jnp
from jax import lax
from jax.experimental import pallas as pl
from jax.experimental.pallas import tpu as pltpu
from jax.sharding import PartitionSpec as P


VMEM = pl.BlockSpec(memory_space=pltpu.VMEM)
BF16 = jnp.bfloat16
F32 = jnp.float32
COST = pl.CostEstimate(flops=1 << 30, transcendentals=0, bytes_accessed=1 << 20)


def leaky(t):
    return jnp.where(t >= 0, t, 0.1 * t)


def near_memory(value):
    return pltpu.with_memory_space_constraint(value, pltpu.VMEM)


def local(shape):
    return pltpu.VMEM(shape, BF16)


def column(bias):
    count = bias.shape[1]
    return jnp.broadcast_to(bias[...], (count, count)).T[:, :1]


def shift_exchange(low, high, axis):
    count = lax.axis_size(axis)
    below = lax.ppermute(high, axis, [(i, (i + 1) % count) for i in range(count)])
    above = lax.ppermute(low, axis, [((i + 1) % count, i) for i in range(count)])
    return below, above


def pairings(axis):
    count = lax.axis_size(axis)
    near = [(i, i + 1 if i % 2 == 0 else i - 1) for i in range(count)]
    far = [(i, (i - 1) % count if i % 2 == 0 else (i + 1) % count) for i in range(count)]
    return near, far


def mix_two(mix, bias, pool, stacked, channels, depth):
    result = jnp.dot(mix, stacked, preferred_element_type=F32)
    result = leaky(result + bias).astype(BF16)
    answers = []
    for half in range(result.shape[1] // depth):
        block = result[:, half * depth : (half + 1) * depth]
        sums = jnp.dot(block, pool, preferred_element_type=F32)
        mean = sums[:channels]
        for part in range(1, 4):
            mean = mean + sums[part * channels : (part + 1) * channels]
        answers.append((block, mean.astype(BF16)))
    return answers


def pool_two(depth):
    source = lax.broadcasted_iota(jnp.int32, (depth, depth), 0) // 2
    target = lax.broadcasted_iota(jnp.int32, (depth, depth), 1) % (depth // 2)
    return jnp.where(source == target, 0.125, 0.0).astype(BF16)


def shifts(value):
    depth = value.shape[1]
    return pltpu.roll(value, 1, 1), value, pltpu.roll(value, depth - 1, 1)


def mix_kernel(flip, weights, *refs):
    count = len(refs) // 2
    mix = refs[count]
    for source, target in zip(refs[:count], refs[count + 1 :]):
        target[...] = source[...]
    channels = weights.shape[1]
    blank = jnp.zeros((channels, channels), BF16)
    empty = jnp.zeros((channels, 4 * channels), BF16)
    turn = flip[0]
    for e in range(3):
        for a in range(3):
            taps = [weights[9 * a + e + 3 * (c + turn * (2 - 2 * c))] for c in range(3)]
            for dy in range(2):
                tile = jnp.concatenate([blank] * dy + taps + [blank] * (1 - dy), axis=1)
                for dx in range(2):
                    row = (2 * dx + dy) * channels
                    at = (4 * e + a + dx) * 4 * channels
                    mix[row : row + channels, at : at + 4 * channels] = tile
        for dy in range(2):
            for dx in range(2):
                row = (2 * dx + dy) * channels
                at = (4 * e + 3 * (1 - dx)) * 4 * channels
                mix[row : row + channels, at : at + 4 * channels] = empty


def store_block(block, target, x, y, turn, channels):
    for part in range(4):
        dx, dy = part // 2, part % 2
        target[x + dx, y + dy + turn * (1 - 2 * dy)] = block[
            part * channels : (part + 1) * channels
        ]


def frames(blocks):
    return sorted({at for start in blocks for at in range(start, start + 4)})


def main_two(blocks, fetch, extent_y, mix, bias, turn, out, pooled, edge, rolled):
    width, channels, depth = edge.shape[2:]
    columns = frames(blocks)
    for slot, x in enumerate(columns):
        for y in range(extent_y + width):
            for e, turned in enumerate(shifts(fetch(x, y))):
                if y < width:
                    edge[e, slot, y] = turned
                if y:
                    rolled[e, slot, y - 1] = turned
    offset = jnp.concatenate([column(bias)] * 4, axis=0)
    pool = pool_two(depth)
    matrix = mix[...]
    for index, x in enumerate(blocks):
        slot = columns.index(x)
        rows = list(range(2, extent_y + 1, 2))
        stacked = jnp.concatenate(
            [
                rolled[:, slot : slot + 4, y - 2 : y + 2].reshape(48 * channels, depth)
                for y in rows
            ],
            axis=1,
        )
        answers = mix_two(matrix, offset, pool, stacked, channels, depth)
        for y, (block, mean) in zip(rows, answers):
            if y < extent_y:
                at = y - 2 + turn * (extent_y - 2 * y)
                store_block(block, out, 2 * index, at, turn, channels)
            pooled[index, y // 2 - 1 + turn * (extent_y // 2 + 1 - y)] = mean


def mirrored(y, extent_y, turn):
    return y + turn * (extent_y - 1 - 2 * y) if y < extent_y else y


def center_two_kernel(flip, cells, near, mix, bias, out, pooled, edge, rolled):
    extent_x, extent_y = cells.shape[:2]

    def fetch(x, y):
        if y < extent_y:
            return cells[x - 1, mirrored(y, extent_y, flip[0])]
        return near[x - 1, y - extent_y]

    blocks = list(range(2, extent_x - 2, 2))
    main_two(blocks, fetch, extent_y, mix, bias, flip[0], out, pooled, edge, rolled)


def sides_two_kernel(flip, cells, near, left, right, mix, bias, out, pooled, edge, rolled):
    extent_x, extent_y = cells.shape[:2]

    def fetch(x, y):
        at = mirrored(y, extent_y, flip[0])
        if x == 0:
            return left[at]
        if x == extent_x + 1:
            return right[at]
        if y < extent_y:
            return cells[x - 1, at]
        return near[x - 1, y - extent_y]

    blocks = [0, extent_x - 2]
    main_two(blocks, fetch, extent_y, mix, bias, flip[0], out, pooled, edge, rolled)


def far_two(blocks, fetch, edge, mix, bias, turn, out, pooled, shift, rim):
    _, _, width, channels, depth = edge.shape
    columns = frames(blocks)
    for x in columns:
        for row in range(width):
            for e, turned in enumerate(shifts(fetch(x, row))):
                rim[e, x, width - 1 - row] = turned
    offset = jnp.concatenate([column(bias)] * 4, axis=0)
    pool = pool_two(depth)
    starts = [(x, first) for x in blocks for first in (0, 2)]
    stacked = jnp.concatenate(
        [
            jnp.concatenate(
                [
                    piece.reshape(-1, depth)
                    for e in range(3)
                    for at in range(x, x + 4)
                    for piece in (
                        rim[e, at, first:],
                        edge[e, columns.index(at), : first + 4 - width],
                    )
                ],
                axis=0,
            )
            for x, first in starts
        ],
        axis=1,
    )
    answers = mix_two(mix[...], offset, pool, stacked, channels, depth)
    for (x, first), (block, mean) in zip(starts, answers):
        if first:
            store_block(block, out, x - shift, 0, turn, channels)
        own = first // 2
        pooled[(x - shift) // 2, own + turn * (1 - 2 * own)] = mean


def middle_two_kernel(flip, far, edge, mix, bias, out, pooled, rim):
    extent_x = far.shape[0]
    far_two(
        list(range(2, extent_x - 2, 2)),
        lambda x, row: far[x - 1, row],
        edge,
        mix,
        bias,
        flip[0],
        out,
        pooled,
        2,
        rim,
    )


def corner_two_kernel(
    flip, far, left, right, edge, mix, bias, middle, middle_pooled, center_pooled, sides_pooled,
    out, pooled, low, high, rim, means,
):
    extent_x = far.shape[0]
    turn = flip[0]

    def fetch(x, row):
        if x == 0:
            return left[row]
        if x == extent_x + 1:
            return right[row]
        return far[x - 1, row]

    far_two([0, extent_x - 2], fetch, edge, mix, bias, turn, out, means, 0, rim)
    out[2 : extent_x - 2] = middle[...]
    means[1 : extent_x // 2 - 1] = middle_pooled[...]
    rest = center_pooled.shape[1]
    pooled[:, pl.ds(turn * rest, 2)] = means[...]
    main = pl.ds(2 - 2 * turn, rest)
    last = extent_x // 2 - 1
    pooled[0:1, main] = sides_pooled[0:1]
    pooled[1:last, main] = center_pooled[...]
    pooled[last : last + 1, main] = sides_pooled[1:2]
    channels, depth = low.shape[1:]
    first = lax.broadcasted_iota(jnp.int32, (channels, depth), 1) < depth // 2
    for target, x in ((low, 0), (high, extent_x // 2 - 1)):
        for pair in range(target.shape[0]):
            target[pair] = jnp.where(first, pooled[x, 2 * pair], pooled[x, 2 * pair + 1])


SCALAR = pl.BlockSpec(memory_space=pltpu.SMEM)


def kernel_call(body, flip, operands, results, scratch):
    return pl.pallas_call(
        body,
        out_shape=tuple(
            local(result) if isinstance(result, tuple) else result for result in results
        ),
        in_specs=[SCALAR] + [VMEM] * len(operands),
        out_specs=(VMEM,) * len(results),
        scratch_shapes=[pltpu.VMEM(shape, BF16) for shape in scratch],
        cost_estimate=COST,
        compiler_params=pltpu.CompilerParams(vmem_limit_bytes=16 << 20),
    )(flip, *map(near_memory, operands))


def three_kernel(layers, cells, left, right, mix, bias, out, windows, paired):
    extent_x, wide_y, channels, lanes = cells.shape
    extent_y = wide_y - 2
    depth = lanes // 2
    senders, slots = windows.shape[:2]

    def place(x, y):
        if 0 < x < extent_x + 1:
            return cells[x - 1, y]
        both = (left if x == 0 else right)[y // 2]
        return jnp.where(first == (y % 2 == 0), both, pltpu.roll(both, depth, 1))

    first = lax.broadcasted_iota(jnp.int32, (channels, lanes), 1) < depth
    for x in range(extent_x + 2):
        turned = [shifts(place(x, y)) for y in range(extent_y + 2)]
        for y in range(extent_y + 1):
            for e in range(3):
                paired[x, y, e] = jnp.where(first, turned[y][e], turned[y + 1][e])
    offset = column(bias)
    rows = lax.broadcasted_iota(jnp.int32, (slots * 8, 2 * lanes), 0)
    layer = rows % 8
    wanted = (layers * (rows // 8) + layer + depth // 2 - 1) % (depth // 2)
    source = lax.broadcasted_iota(jnp.int32, (slots * 8, 2 * lanes), 1) % depth // 2
    pool = jnp.where((source == wanted) & (layer < layers + 2), 0.125, 0.0).astype(BF16)
    matrix = mix[...]
    for px in range(extent_x // 2):
        results = []
        for py in range(extent_y // 2):
            stacked = jnp.concatenate(
                [
                    jnp.concatenate(
                        [
                            paired[x + a, 2 * py + c].reshape(3 * channels, lanes)
                            for a in range(3)
                            for c in range(3)
                        ],
                        axis=0,
                    )
                    for x in (2 * px, 2 * px + 1)
                ],
                axis=1,
            )
            result = jnp.dot(matrix, stacked, preferred_element_type=F32)
            result = leaky(result + offset).astype(BF16)
            out[2 * px, py] = result[:, :lanes]
            out[2 * px + 1, py] = result[:, lanes:]
            results.append(result)
        means = lax.dot_general(
            pool,
            jnp.concatenate(results, axis=0),
            (((1,), (1,)), ((), ())),
            preferred_element_type=F32,
        ).astype(BF16)
        for slot in range(slots):
            for sender in range(senders):
                windows[sender, slot, 8 * px : 8 * px + 8] = means[8 * slot : 8 * slot + 8]


def three(cells, left, right, weights, bias_values, count_x, count_y):
    extent_x, wide_y, channels, lanes = cells.shape
    extent_y = wide_y - 2
    depth = lanes // 2
    out_channels = weights.shape[1]
    layers = depth // 2 // count_y
    mix = weights.transpose(1, 0, 2).reshape(out_channels, 27 * channels)
    return pl.pallas_call(
        functools.partial(three_kernel, layers),
        name="three",
        out_shape=(
            local((extent_x, extent_y // 2, out_channels, lanes)),
            local((count_x, count_y, extent_x // 2 * 8, extent_y // 2 * out_channels)),
        ),
        in_specs=[VMEM] * 5,
        out_specs=(VMEM, VMEM),
        scratch_shapes=[pltpu.VMEM((extent_x + 2, extent_y + 1, 3, channels, lanes), BF16)],
        cost_estimate=COST,
        compiler_params=pltpu.CompilerParams(vmem_limit_bytes=16 << 20),
    )(*map(near_memory, (cells, left, right, mix, bias_values)))


def four_kernel(count_y, tiles, weights, bias, out, rolled, mix):
    _, parts, lanes = tiles.shape
    extent_x, extent_y, layers, out_channels = out.shape
    rows = count_y * 8
    inner_x = parts // 8
    half = lanes // 2
    upper = lax.broadcasted_iota(jnp.int32, (rows, lanes), 1) >= half
    short = count_y * layers
    for x in range(extent_x):
        start = x // inner_x * count_y
        at = x % inner_x * 8
        value = tiles[start : start + count_y, at : at + 8].reshape(rows, lanes).astype(F32)
        before = pltpu.roll(value, 8, 0)
        after = pltpu.roll(value, rows - 8, 0)
        around = pltpu.roll(jnp.where(upper, before, after), half, 1)
        whole = jnp.concatenate([value, around], axis=1)
        for e in range(3):
            turned = whole if e == 0 else pltpu.roll(whole, rows - e, 0)
            turned = turned.reshape(count_y, 8, 2 * lanes)[:, :layers].reshape(short, 2 * lanes)
            rolled[x + 1, :, e * 2 * lanes : (e + 1) * 2 * lanes] = turned.astype(BF16)
    rolled[0] = rolled[extent_x]
    rolled[extent_x + 1] = rolled[1]
    bands = ((1, 0), (2, 1), (0, None), (None, 2))
    for a in range(3):
        for e in range(3):
            for band, taps in enumerate(bands):
                row = ((3 * a + e) * 4 + band) * half
                for index, c in enumerate(taps):
                    lane = index * out_channels
                    if c is None:
                        tap = jnp.zeros((half, out_channels), BF16)
                    else:
                        tap = weights[9 * a + 3 * c + e]
                    mix[row : row + half, lane : lane + out_channels] = tap
    offset = jnp.concatenate([bias[...], bias[...]], axis=1)
    matrix = mix[...]
    group = min(extent_x, 4)
    for x in range(0, extent_x, group):
        stacked = jnp.concatenate(
            [rolled[x + a : x + a + group].reshape(group * short, 6 * lanes) for a in range(3)],
            axis=1,
        )
        result = jnp.dot(stacked, matrix, preferred_element_type=F32)
        result = leaky(result + offset).astype(BF16)
        for dx in range(group):
            for y in range(extent_y):
                row = dx * short + y // 2 * layers
                lane = y % 2 * out_channels
                out[x + dx, y] = result[row : row + layers, lane : lane + out_channels]


def four(tiles, weights, bias, extents, count_y):
    extent_x, extent_y, layers = extents
    _, channels, out_channels = weights.shape
    return pl.pallas_call(
        functools.partial(four_kernel, count_y),
        name="four",
        out_shape=jax.ShapeDtypeStruct((extent_x, extent_y, layers, out_channels), BF16),
        in_specs=[VMEM] * 3,
        out_specs=VMEM,
        scratch_shapes=[
            pltpu.VMEM((extent_x + 2, count_y * layers, 6 * tiles.shape[2]), BF16),
            pltpu.VMEM((36 * channels, 2 * out_channels), BF16),
        ],
        cost_estimate=COST,
        compiler_params=pltpu.CompilerParams(vmem_limit_bytes=16 << 20),
    )(near_memory(tiles), near_memory(weights), near_memory(bias))


def shards(features, weight_two, bias_two, weight_three, bias_three, weight_four, bias_four):
    count_x, count_y = lax.axis_size("gx"), lax.axis_size("gy")
    width = 3
    cells = features.transpose(1, 2, 0, 3)
    extent_x, extent_y, channels, depth = cells.shape
    even = lax.axis_index("gy") % 2 == 0
    flip = 1 - even.astype(jnp.int32)[None]
    head, tail = cells[:, :width], cells[:, : -width - 1 : -1]
    near_pairs, far_pairs = pairings("gy")
    far = lax.ppermute(jnp.where(even, head, tail), "gy", far_pairs)
    near = lax.ppermute(jnp.where(even, tail, head), "gy", near_pairs)
    left, right = shift_exchange(
        jnp.concatenate([cells[0], near[0]], axis=0),
        jnp.concatenate([cells[-1], near[-1]], axis=0),
        "gx",
    )
    far_left, far_right = shift_exchange(far[0], far[-1], "gx")
    biases = [bias[None, :] for bias in (bias_two, bias_three, bias_four)]
    mix, bias, bias_three, bias_four = kernel_call(
        mix_kernel,
        flip,
        [weight_two, *biases],
        [local((4 * channels, 48 * channels))] + [pltpu.VMEM(row.shape, F32) for row in biases],
        [],
    )
    rest = extent_y // 2
    deep = extent_y + width - 1

    def main_call(body, name, operands, blocks):
        read = 2 * blocks + 2 if name == "center_two" else 8
        return kernel_call(
            body,
            flip,
            [cells, near, *operands, mix, bias],
            [
                (2 * blocks, extent_y - 2, channels, depth),
                (blocks, rest, channels, depth),
                (3, read, width, channels, depth),
            ],
            [(3, read, deep, channels, depth)],
        )

    center, center_pooled, center_edge = main_call(
        center_two_kernel, "center_two", [], extent_x // 2 - 2
    )
    sides, sides_pooled, sides_edge = main_call(
        sides_two_kernel, "sides_two", [left, right], 2
    )
    rim = (3, extent_x + 2, width, channels, depth)
    middle, middle_pooled = kernel_call(
        middle_two_kernel,
        flip,
        [far, center_edge, mix, bias],
        [(extent_x - 4, 2, channels, depth), (extent_x // 2 - 2, 2, channels, depth)],
        [rim],
    )
    far_out, pooled, low, high = kernel_call(
        corner_two_kernel,
        flip,
        [
            far, far_left, far_right, sides_edge, mix, bias,
            middle, middle_pooled, center_pooled, sides_pooled,
        ],
        [
            (extent_x, 2, channels, depth),
            (extent_x // 2, rest + 2, channels, depth),
            (rest // 2 + 1, channels, depth),
            (rest // 2 + 1, channels, depth),
        ],
        [rim, (extent_x // 2, 2, channels, depth)],
    )
    main = jnp.concatenate([sides[:2], center, sides[2:]], axis=0)
    level_two = jnp.where(
        even,
        jnp.concatenate([far_out, main], axis=1),
        jnp.concatenate([main, far_out], axis=1),
    ).transpose(2, 0, 1, 3)

    left, right = shift_exchange(low, high, "gx")
    level_three, windows = three(
        pooled, left, right, weight_three, bias_three, count_x, count_y
    )
    slots = count_x * count_y
    tiles = lax.all_to_all(
        windows.reshape((slots,) + windows.shape[2:]), ("gx", "gy"), 0, 0, tiled=True
    )
    extents = (count_x * extent_x // 4, count_y * extent_y // 4, depth // 4 // count_y)
    bottleneck = four(tiles, weight_four.transpose(0, 2, 1), bias_four, extents, count_y)
    out_three = level_three.reshape(level_three.shape[:3] + (2, level_three.shape[3] // 2))
    out_three = out_three.transpose(2, 0, 1, 3, 4)
    out_three = out_three.reshape(out_three.shape[:2] + (-1, out_three.shape[4]))
    return level_two, out_three, bottleneck.transpose(3, 0, 1, 2)


def solution(mesh):
    return jax.shard_map(
        shards,
        mesh=mesh,
        in_specs=(P(None, "gx", "gy", None), P(), P(), P(), P(), P(), P()),
        out_specs=(
            P(None, "gx", "gy", None),
            P(None, "gx", "gy", None),
            P(None, None, None, "gy"),
        ),
        check_vma=False,
    )
```

time: 41.4 us -> 38.2 us (0.923)
  waiting for transfers between devices: 14.5 us -> 10.1 us
  starting transfers between devices: 14.9 us -> 16.3 us
    ppermute x2 -> x3, starting transfers between devices: 2 us -> 4.77 us  [shift_exchange(): lax.ppermute(low, axis, [((i + 1) % count, i) for i in range(count)])]
    ppermute x2, waiting for transfers between devices: 3.48 us -> 1.22 us  [the longest x1 1.22 us: shards(): far = lax.ppermute(jnp.where(even, head, tail), 'gy', far_pairs)]
    ppermute x2 -> x3, waiting for transfers between devices: 3.3 us -> 1.19 us  [shift_exchange(): lax.ppermute(low, axis, [((i + 1) % count, i) for i in range(count)])]
    unnamed x17 -> x14, local copies, waits for them, and re-layouts: 1.07 us -> 3.08 us
    all_to_all x1, starting transfers between devices: 4.13 us -> 2.58 us  [shards(): lax.all_to_all(windows.reshape((slots,) + windows.shape[2:]), ('gx', 'gy'...]
    ppermute x2, starting transfers between devices: 3.77 us -> 5.26 us  [the longest x1 4.7 us: shards(): far = lax.ppermute(jnp.where(even, head, tail), 'gy', far_pairs)]
    optimization_barrier x1 -> x0, local copies, waits for them, and re-layouts: 1.38 us -> none  [shards(): lax.optimization_barrier((features[:, 0], features[:, -1], features))]
    ppermute x2 -> x3, starting transfers between devices: 5.02 us -> 3.69 us  [shift_exchange(): lax.ppermute(high, axis, [(i, (i + 1) % count) for i in range(count)])]
  transfers between devices with their start and end apart: 7 -> 9, of which waited for: 5 -> 4; matrix products, arithmetic and copies ran while one was open for 9% -> 6% of each run, Pallas kernels for 5% -> 7%
where the time goes in v4:
time: 38.2 us; the launch traced here: 38 us
  starting transfers between devices  16.3 us (43%)
  waiting for transfers between devices  10.1 us (26%)
  Pallas kernels  6.27 us (16%)
  local copies, waits for them, and re-layouts  4.29 us (11%)
  between operations  0.81 us (2%)
    all_to_all x1, waiting for transfers between devices, shards(): lax.all_to_all(windows.reshape((slots,) + windows.shape[2:]), ('gx', 'gy'...  6.03 us
    ppermute x3, starting transfers between devices, shift_exchange(): lax.ppermute(low, axis, [((i + 1) % count, i) for i in range(count)])  4.77 us
    ppermute x1, starting transfers between devices, shards(): far = lax.ppermute(jnp.where(even, head, tail), 'gy', far_pairs)  4.7 us
    ppermute x3, starting transfers between devices, shift_exchange(): lax.ppermute(high, axis, [(i, (i + 1) % count) for i in range(count)])  3.69 us
    pallas_call x5, Pallas kernels, kernel_call(): pl.pallas_call(body, out_shape=tuple((local(result) if isinstance(result,...  3.44 us
    unnamed x14, local copies, waits for them, and re-layouts  3.08 us
    all_to_all x1, starting transfers between devices, shards(): lax.all_to_all(windows.reshape((slots,) + windows.shape[2:]), ('gx', 'gy'...  2.58 us
    ppermute x3, waiting for transfers between devices, shift_exchange(): lax.ppermute(high, axis, [(i, (i + 1) % count) for i in range(count)])  1.67 us
  transfers between devices with their start and end apart: 9, of which 4 were waited for; matrix products, arithmetic and copies ran while one was open for 6% of the time, Pallas kernels for 7%

profile of v4, /device:TPU:0, one launch (start us, length us, event | category | flops | bytes accessed | tf_op | source)
XLA Modules:
  0.0 38.0 jit_solution(1908491389193112503)
XLA Ops:
  0.6 1.4 %copy.19 = bf16[32,8,8,128]{3,0,2,1:T(8,128)(2,1)S(1)} copy(bf16[32,8,8,128]{3,2,1,0:T(8,128)(2,1)} %param.7) | data formatting | bytes 1048576 | tf_op args[0]
  2.1 0.0 copy-start.1
  2.1 0.1 broadcast_select_fusion.1
  2.2 0.6 %collective-permute-start.3 = (bf16[8,3,32,128]{3,2,1,0:T(8,128)(2,1)S(1)}, bf16[8,3,32,128]{3,2,1,0:T(8,128)(2,1)S(1)}, u32[]{:S(2)}, u32[]{:S(2)}) collective-permute-start(bf16[8,3,32,128]{3,2,1,0:T(8,128)(2,1)S(1)} %get-tuple-element.46), channel_id=1, source_target_pairs={{0,1},{1,0},{2,3},{3,2},{4,5},{5,4},{6,7},{7,6},{8,9},{9,8},{10,11... | collective-permute-start | bytes 589832 | tf_op jit(solution)/shard_map/ppermute | solution.py:433
  2.7 4.7 %collective-permute-start = (bf16[8,3,32,128]{3,2,1,0:T(8,128)(2,1)S(1)}, bf16[8,3,32,128]{3,2,1,0:T(8,128)(2,1)S(1)}, u32[]{:S(2)}, u32[]{:S(2)}) collective-permute-start(bf16[8,3,32,128]{3,2,1,0:T(8,128)(2,1)S(1)} %get-tuple-element.45), channel_id=1, source_target_pairs={{0,7},{1,2},{2,1},{3,4},{4,3},{5,6},{6,5},{7,0},{8,15},{9,10},{10,... | collective-permute-start | bytes 589832 | tf_op jit(solution)/shard_map/ppermute | solution.py:432
  7.4 0.6 %copy-done.2 = f32[32]{0:T(128)S(1)} copy-done((f32[32]{0:T(128)S(1)}, f32[32]{0:T(128)}, u32[]{:S(2)}) %copy-start.2) | copy-done | bytes 152
  8.1 0.0 copy-done.3
  8.1 0.0 copy-done.4
  8.1 0.2 shard_map.94
  8.3 2.5 %collective-permute-start.5 = (bf16[11,32,128]{2,1,0:T(8,128)(2,1)S(1)}, bf16[11,32,128]{2,1,0:T(8,128)(2,1)S(1)}, u32[]{:S(2)}, u32[]{:S(2)}) collective-permute-start(bf16[11,32,128]{2,1,0:T(8,128)(2,1)S(1)} %pad_maximum_fusion.1), channel_id=1, source_target_pairs={{8,0},{16,8},{24,16},{0,24},{9,1},{17,9},{25,17},{1,25},{10,2},{18... | collective-permute-start | bytes 270344 | tf_op jit(solution)/shard_map/ppermute | solution.py:37
  10.8 0.1 collective-permute-start.4
  10.9 1.2 %collective-permute-done.far = bf16[8,3,32,128]{3,2,1,0:T(8,128)(2,1)S(1)} collective-permute-done((bf16[8,3,32,128]{3,2,1,0:T(8,128)(2,1)S(1)}, bf16[8,3,32,128]{3,2,1,0:T(8,128)(2,1)S(1)}, u32[]{:S(2)}, u32[]{:S(2)}) %collective-permute-start) | collective-permute-done | bytes 196640 | tf_op jit(solution)/shard_map/ppermute | solution.py:432
  12.1 1.5 %collective-permute-start.1 = (bf16[3,32,128]{2,1,0:T(8,128)(2,1)S(1)}, bf16[3,32,128]{2,1,0:T(8,128)(2,1)S(1)}, u32[]{:S(2)}, u32[]{:S(2)}) collective-permute-start(bf16[3,32,128]{2,1,0:T(8,128)(2,1)S(1)} %get-tuple-element.50), channel_id=1, source_target_pairs={{0,8},{8,16},{16,24},{24,0},{1,9},{9,17},{17,25},{25,1},{2,10},{10... | collective-permute-start | bytes 73736 | tf_op jit(solution)/shard_map/ppermute | solution.py:36
  13.6 1.4 %collective-permute-start.2 = (bf16[3,32,128]{2,1,0:T(8,128)(2,1)S(1)}, bf16[3,32,128]{2,1,0:T(8,128)(2,1)S(1)}, u32[]{:S(2)}, u32[]{:S(2)}) collective-permute-start(bf16[3,32,128]{2,1,0:T(8,128)(2,1)S(1)} %get-tuple-element.49), channel_id=1, source_target_pairs={{8,0},{16,8},{24,16},{0,24},{9,1},{17,9},{25,17},{1,25},{10,2},{18... | collective-permute-start | bytes 73736 | tf_op jit(solution)/shard_map/ppermute | solution.py:37
  15.1 1.0 %shard_map.96 = (bf16[4,6,32,128]{3,2,1,0:T(8,128)(2,1)S(1)}, bf16[2,4,32,128]{3,2,1,0:T(8,128)(2,1)S(1)}, bf16[3,6,3,32,128]{4,3,2,1,0:T(8,128)(2,1)S(1)}) custom-call(s32[1]{0:T(128)} %bitcast.flip, bf16[8,8,32,128]{3,2,1,0:T(8,128)(2,1)S(1)} %bitcast.34, bf16[8,3,32,128]{3,2,1,0:T(8,128)(2,1)S(1)} %collective-permute-done.3.near, ...), custom_call_target="tpu_custom_call" | custom-call | flops 1073741824 | bytes 1048576 | tf_op jit(solution)/shard_map/pallas_call | solution.py:261
  16.1 0.6 %shard_map.97 = (bf16[4,2,32,128]{3,2,1,0:T(8,128)(2,1)S(1)}, bf16[2,2,32,128]{3,2,1,0:T(8,128)(2,1)S(1)}) custom-call(s32[1]{0:T(128)} %bitcast.flip, bf16[8,3,32,128]{3,2,1,0:T(8,128)(2,1)S(1)} %collective-permute-done.far, bf16[3,6,3,32,128]{4,3,2,1,0:T(8,128)(2,1)S(1)} %get-tuple-element.24.edge, bf16[128,1536]{1,0:T(8,128)(2,1)S(1)} %get-tuple-element.21.mix, ...), custom_call_target="tpu_custom_call" | custom-call | flops 1073741824 | bytes 1048576 | tf_op jit(solution)/shard_map/pallas_call | solution.py:261
  16.7 0.0 collective-permute-done.4.left
  16.7 1.0 %shard_map.95 = (bf16[4,6,32,128]{3,2,1,0:T(8,128)(2,1)S(1)}, bf16[2,4,32,128]{3,2,1,0:T(8,128)(2,1)S(1)}, bf16[3,8,3,32,128]{4,3,2,1,0:T(8,128)(2,1)S(1)}) custom-call(s32[1]{0:T(128)} %bitcast.flip, bf16[8,8,32,128]{3,2,1,0:T(8,128)(2,1)S(1)} %bitcast.35, bf16[8,3,32,128]{3,2,1,0:T(8,128)(2,1)S(1)} %collective-permute-done.3.near, ...), custom_call_target="tpu_custom_call" | custom-call | flops 1073741824 | bytes 1048576 | tf_op jit(solution)/shard_map/pallas_call | solution.py:261
  17.8 0.6 %shard_map.98 = (bf16[8,2,32,128]{3,2,1,0:T(8,128)(2,1)S(1)}, bf16[4,6,32,128]{3,2,1,0:T(8,128)(2,1)S(1)}, bf16[3,32,128]{2,1,0:T(8,128)(2,1)S(1)}, bf16[3,32,128]{2,1,0:T(8,128)(2,1)S(1)}) custom-call(s32[1]{0:T(128)} %bitcast.flip, bf16[8,3,32,128]{3,2,1,0:T(8,128)(2,1)S(1)} %collective-permute-done.far, ...), custom_call_target="tpu_custom_call" | custom-call | flops 1073741824 | bytes 1048576 | tf_op jit(solution)/shard_map/pallas_call | solution.py:261
  18.4 2.1 %collective-permute-start.6 = (bf16[3,32,128]{2,1,0:T(8,128)(2,1)S(1)}, bf16[3,32,128]{2,1,0:T(8,128)(2,1)S(1)}, u32[]{:S(2)}, u32[]{:S(2)}) collective-permute-start(bf16[3,32,128]{2,1,0:T(8,128)(2,1)S(1)} %get-tuple-element.33), channel_id=1, source_target_pairs={{0,8},{8,16},{16,24},{24,0},{1,9},{9,17},{17,25},{25,1},{2,10},{10... | collective-permute-start | bytes 73736 | tf_op jit(solution)/shard_map/ppermute | solution.py:36
  20.5 0.8 %collective-permute-start.7 = (bf16[3,32,128]{2,1,0:T(8,128)(2,1)S(1)}, bf16[3,32,128]{2,1,0:T(8,128)(2,1)S(1)}, u32[]{:S(2)}, u32[]{:S(2)}) collective-permute-start(bf16[3,32,128]{2,1,0:T(8,128)(2,1)S(1)} %get-tuple-element.34), channel_id=1, source_target_pairs={{8,0},{16,8},{24,16},{0,24},{9,1},{17,9},{25,17},{1,25},{10,2},{18... | collective-permute-start | bytes 73736 | tf_op jit(solution)/shard_map/ppermute | solution.py:37
  21.4 0.1 copy.15.mix
  21.5 1.7 %collective-permute-done.6.left = bf16[3,32,128]{2,1,0:T(8,128)(2,1)S(1)} collective-permute-done((bf16[3,32,128]{2,1,0:T(8,128)(2,1)S(1)}, bf16[3,32,128]{2,1,0:T(8,128)(2,1)S(1)}, u32[]{:S(2)}, u32[]{:S(2)}) %collective-permute-start.6) | collective-permute-done | bytes 24608 | tf_op jit(solution)/shard_map/ppermute | solution.py:36
  23.2 1.2 %collective-permute-done.7.right = bf16[3,32,128]{2,1,0:T(8,128)(2,1)S(1)} collective-permute-done((bf16[3,32,128]{2,1,0:T(8,128)(2,1)S(1)}, bf16[3,32,128]{2,1,0:T(8,128)(2,1)S(1)}, u32[]{:S(2)}, u32[]{:S(2)}) %collective-permute-start.7) | collective-permute-done | bytes 24608 | tf_op jit(solution)/shard_map/ppermute | solution.py:37
  24.4 1.5 %three.1 = (bf16[4,2,64,128]{3,2,1,0:T(8,128)(2,1)S(1)}, bf16[4,8,16,128]{3,2,1,0:T(8,128)(2,1)}) custom-call(bf16[4,6,32,128]{3,2,1,0:T(8,128)(2,1)S(1)} %get-tuple-element.32.cells, bf16[3,32,128]{2,1,0:T(8,128)(2,1)S(1)} %collective-permute-done.6.left, bf16[3,32,128]{2,1,0:T(8,128)(2,1)S(1)} %collective-permute-done.7.right, ...), custom_call_target="tpu_custom_call" | custom-call | flops 1073741824 | bytes 1048576 | tf_op jit(solution)/shard_map/three/pallas_call | solution.py:339
  25.9 2.6 %all-to-all-start = ((bf16[32,16,128]{2,1,0:T(8,128)(2,1)}), bf16[32,16,128]{2,1,0:T(8,128)(2,1)S(1)}, u32[]{:S(2)}, u32[]{:S(2)}) async-start(bf16[32,16,128]{2,1,0:T(8,128)(2,1)} %bitcast.16), calls=%async_computation | async-start | bytes 262144 | tf_op jit(solution)/shard_map/all_to_all | solution.py:506
  28.5 0.1 fusion
  28.6 1.0 %copy.17 = bf16[32,8,8,128]{3,2,1,0:T(8,128)(2,1)} copy(bf16[32,8,8,128]{3,0,2,1:T(8,128)(2,1)S(1)} %fusion) | data formatting | bytes 1048576
  29.6 0.1 reshape.21
  29.7 0.9 %copy.16 = bf16[64,4,2,2,64]{4,3,2,1,0:T(2,128)(2,1)} copy(bf16[64,4,2,2,64]{4,3,0,2,1:T(2,128)(2,1)S(1)} %bitcast.40) | data formatting | bytes 262144 | tf_op jit(solution)/shard_map/transpose | solution.py:512
  30.6 6.0 %all-to-all-done.tiles = bf16[32,16,128]{2,1,0:T(8,128)(2,1)S(1)} async-done(((bf16[32,16,128]{2,1,0:T(8,128)(2,1)}), bf16[32,16,128]{2,1,0:T(8,128)(2,1)S(1)}, u32[]{:S(2)}, u32[]{:S(2)}) %all-to-all-start) | async-done | bytes 131104 | tf_op jit(solution)/shard_map/all_to_all | solution.py:506
  36.6 1.3 %four.1 = bf16[8,16,4,128]{3,2,1,0:T(4,128)(2,1)} custom-call(bf16[32,16,128]{2,1,0:T(8,128)(2,1)S(1)} %all-to-all-done.tiles, bf16[27,64,128]{2,1,0:T(8,128)(2,1)S(1)} %bitcast.36, f32[1,128]{1,0:T(1,128)S(1)} %get-tuple-element.38.bias), custom_call_target="tpu_custom_call" | custom-call | flops 1073741824 | bytes 1048576 | tf_op jit(solution)/shard_map/four/pallas_call | solution.py:408
  (19 shorter events, 0.1 us)
Async XLA Ops:
  2.1 5.4 %copy-start.1 = (bf16[27,32,32]{2,1,0:T(8,128)(2,1)S(1)}, bf16[27,32,32]{2,1,0:T(8,128)(2,1)}, u32[]{:S(2)}) copy-start(bf16[27,32,32]{2,1,0:T(8,128)(2,1)} %weights.1) | copy-start | bytes 165892
  2.2 6.1 %collective-permute-start.3 = (bf16[8,3,32,128]{3,2,1,0:T(8,128)(2,1)S(1)}, bf16[8,3,32,128]{3,2,1,0:T(8,128)(2,1)S(1)}, u32[]{:S(2)}, u32[]{:S(2)}) collective-permute-start(bf16[8,3,32,128]{3,2,1,0:T(8,128)(2,1)S(1)} %get-tuple-element.46), channel_id=1, source_target_pairs={{0,1},{1,0},{2,3},{3,2},{4,5},{5,4},{6,7},{7,6},{8,9},{9,8},{10,11... | collective-permute-start | bytes 589832 | tf_op jit(solution)/shard_map/ppermute | solution.py:433
  2.7 9.4 %collective-permute-start = (bf16[8,3,32,128]{3,2,1,0:T(8,128)(2,1)S(1)}, bf16[8,3,32,128]{3,2,1,0:T(8,128)(2,1)S(1)}, u32[]{:S(2)}, u32[]{:S(2)}) collective-permute-start(bf16[8,3,32,128]{3,2,1,0:T(8,128)(2,1)S(1)} %get-tuple-element.45), channel_id=1, source_target_pairs={{0,7},{1,2},{2,1},{3,4},{4,3},{5,6},{6,5},{7,0},{8,15},{9,10},{10,... | collective-permute-start | bytes 589832 | tf_op jit(solution)/shard_map/ppermute | solution.py:432
  7.4 0.7 %copy-start.2 = (f32[32]{0:T(128)S(1)}, f32[32]{0:T(128)}, u32[]{:S(2)}) copy-start(f32[32]{0:T(128)} %param.9) | copy-start | bytes 388
  7.4 0.7 %copy-start.3 = (f32[64]{0:T(128)S(1)}, f32[64]{0:T(128)}, u32[]{:S(2)}) copy-start(f32[64]{0:T(128)} %param.11) | copy-start | bytes 772
  7.4 0.7 %copy-start.4 = (f32[128]{0:T(128)S(1)}, f32[128]{0:T(128)}, u32[]{:S(2)}) copy-start(f32[128]{0:T(128)} %param.13) | copy-start | bytes 1540
  8.3 8.3 %collective-permute-start.5 = (bf16[11,32,128]{2,1,0:T(8,128)(2,1)S(1)}, bf16[11,32,128]{2,1,0:T(8,128)(2,1)S(1)}, u32[]{:S(2)}, u32[]{:S(2)}) collective-permute-start(bf16[11,32,128]{2,1,0:T(8,128)(2,1)S(1)} %pad_maximum_fusion.1), channel_id=1, source_target_pairs={{8,0},{16,8},{24,16},{0,24},{9,1},{17,9},{25,17},{1,25},{10,2},{18... | collective-permute-start | bytes 270344 | tf_op jit(solution)/shard_map/ppermute | solution.py:37
  10.8 5.8 %collective-permute-start.4 = (bf16[11,32,128]{2,1,0:T(8,128)(2,1)S(1)}, bf16[11,32,128]{2,1,0:T(8,128)(2,1)S(1)}, u32[]{:S(2)}, u32[]{:S(2)}) collective-permute-start(bf16[11,32,128]{2,1,0:T(8,128)(2,1)S(1)} %pad_maximum_fusion), channel_id=1, source_target_pairs={{0,8},{8,16},{16,24},{24,0},{1,9},{9,17},{17,25},{25,1},{2,10},{10... | collective-permute-start | bytes 270344 | tf_op jit(solution)/shard_map/ppermute | solution.py:36
  12.1 5.6 %collective-permute-start.1 = (bf16[3,32,128]{2,1,0:T(8,128)(2,1)S(1)}, bf16[3,32,128]{2,1,0:T(8,128)(2,1)S(1)}, u32[]{:S(2)}, u32[]{:S(2)}) collective-permute-start(bf16[3,32,128]{2,1,0:T(8,128)(2,1)S(1)} %get-tuple-element.50), channel_id=1, source_target_pairs={{0,8},{8,16},{16,24},{24,0},{1,9},{9,17},{17,25},{25,1},{2,10},{10... | collective-permute-start | bytes 73736 | tf_op jit(solution)/shard_map/ppermute | solution.py:36
  13.6 4.1 %collective-permute-start.2 = (bf16[3,32,128]{2,1,0:T(8,128)(2,1)S(1)}, bf16[3,32,128]{2,1,0:T(8,128)(2,1)S(1)}, u32[]{:S(2)}, u32[]{:S(2)}) collective-permute-start(bf16[3,32,128]{2,1,0:T(8,128)(2,1)S(1)} %get-tuple-element.49), channel_id=1, source_target_pairs={{8,0},{16,8},{24,16},{0,24},{9,1},{17,9},{25,17},{1,25},{10,2},{18... | collective-permute-start | bytes 73736 | tf_op jit(solution)/shard_map/ppermute | solution.py:37
  17.7 3.6 %copy-start.5 = (bf16[27,64,32]{1,2,0:T(8,128)(2,1)S(1)}, bf16[27,64,32]{1,2,0:T(8,128)(2,1)}, u32[]{:S(2)}) copy-start(bf16[27,64,32]{1,2,0:T(8,128)(2,1)} %param.10) | copy-start | bytes 331780
  18.4 4.8 %collective-permute-start.6 = (bf16[3,32,128]{2,1,0:T(8,128)(2,1)S(1)}, bf16[3,32,128]{2,1,0:T(8,128)(2,1)S(1)}, u32[]{:S(2)}, u32[]{:S(2)}) collective-permute-start(bf16[3,32,128]{2,1,0:T(8,128)(2,1)S(1)} %get-tuple-element.33), channel_id=1, source_target_pairs={{0,8},{8,16},{16,24},{24,0},{1,9},{9,17},{17,25},{25,1},{2,10},{10... | collective-permute-start | bytes 73736 | tf_op jit(solution)/shard_map/ppermute | solution.py:36
  20.5 3.8 %collective-permute-start.7 = (bf16[3,32,128]{2,1,0:T(8,128)(2,1)S(1)}, bf16[3,32,128]{2,1,0:T(8,128)(2,1)S(1)}, u32[]{:S(2)}, u32[]{:S(2)}) collective-permute-start(bf16[3,32,128]{2,1,0:T(8,128)(2,1)S(1)} %get-tuple-element.34), channel_id=1, source_target_pairs={{8,0},{16,8},{24,16},{0,24},{9,1},{17,9},{25,17},{1,25},{10,2},{18... | collective-permute-start | bytes 73736 | tf_op jit(solution)/shard_map/ppermute | solution.py:37
  25.9 10.7 %all-to-all-start = ((bf16[32,16,128]{2,1,0:T(8,128)(2,1)}), bf16[32,16,128]{2,1,0:T(8,128)(2,1)S(1)}, u32[]{:S(2)}, u32[]{:S(2)}) async-start(bf16[32,16,128]{2,1,0:T(8,128)(2,1)} %bitcast.16), calls=%async_computation | async-start | bytes 262144 | tf_op jit(solution)/shard_map/all_to_all | solution.py:506
  29.6 7.1 %copy-start = (bf16[27,128,64]{1,2,0:T(8,128)(2,1)S(1)}, bf16[27,128,64]{1,2,0:T(8,128)(2,1)}, u32[]{:S(2)}) copy-start(bf16[27,128,64]{1,2,0:T(8,128)(2,1)} %param.12) | copy-start | bytes 1327108

commit v5 on v4

--- a/solution.py
+++ b/solution.py
@@ -11,6 +11,7 @@
 VMEM = pl.BlockSpec(memory_space=pltpu.VMEM)
 BF16 = jnp.bfloat16
 F32 = jnp.float32
+SCALAR = pl.BlockSpec(memory_space=pltpu.SMEM)
 COST = pl.CostEstimate(flops=1 << 30, transcendentals=0, bytes_accessed=1 << 20)
 
 
@@ -68,6 +69,51 @@
 def shifts(value):
     depth = value.shape[1]
     return pltpu.roll(value, 1, 1), value, pltpu.roll(value, depth - 1, 1)
+
+
+def split_kernel(flip, features, cells, head, tail, parts, arrived):
+    _, extent_y = cells.shape[:2]
+    count, _, step = parts.shape[:3]
+    turn = flip[0]
+    copies = [
+        pltpu.make_async_copy(
+            features.at[:, pl.ds(part * step, step)], parts.at[part], arrived.at[part]
+        )
+        for part in range(count)
+    ]
+    for copy in copies:
+        copy.start()
+    for part in range(count):
+        copies[part].wait()
+        for index in range(step):
+            x = part * step + index
+            cells[x] = jnp.swapaxes(parts[part, :, index], 0, 1)
+            for row in range(head.shape[1]):
+                head[x, row] = cells[x, mirrored(row, extent_y, turn)]
+                tail[x, row] = cells[x, mirrored(extent_y - 1 - row, extent_y, turn)]
+
+
+def split(flip, features, width):
+    channels, extent_x, extent_y, depth = features.shape
+    step = 2
+    count = extent_x // step
+    return pl.pallas_call(
+        split_kernel,
+        name="split",
+        out_shape=(
+            local((extent_x, extent_y, channels, depth)),
+            local((extent_x, width, channels, depth)),
+            local((extent_x, width, channels, depth)),
+        ),
+        in_specs=[SCALAR, pl.BlockSpec(memory_space=pl.ANY)],
+        out_specs=(VMEM,) * 3,
+        scratch_shapes=[
+            pltpu.VMEM((count, channels, step, extent_y, depth), BF16),
+            pltpu.SemaphoreType.DMA((count,)),
+        ],
+        cost_estimate=COST,
+        compiler_params=pltpu.CompilerParams(vmem_limit_bytes=16 << 20),
+    )(flip, pltpu.with_memory_space_constraint(features, pltpu.HBM))
 
 
 def mix_kernel(flip, weights, *refs):
@@ -254,9 +300,6 @@
             target[pair] = jnp.where(first, pooled[x, 2 * pair], pooled[x, 2 * pair + 1])
 
 
-SCALAR = pl.BlockSpec(memory_space=pltpu.SMEM)
-
-
 def kernel_call(body, flip, operands, results, scratch):
     return pl.pallas_call(
         body,
@@ -269,6 +312,35 @@
         cost_estimate=COST,
         compiler_params=pltpu.CompilerParams(vmem_limit_bytes=16 << 20),
     )(flip, *map(near_memory, operands))
+
+
+def store_two_kernel(flip, far, center, sides, out, rows):
+    extent_x = far.shape[0]
+    extent_y = out.shape[2]
+    turn = flip[0]
+    for x in range(extent_x):
+        if 2 <= x < extent_x - 2:
+            main = center[x - 2]
+        else:
+            main = sides[x if x < 2 else x - extent_x + 4]
+        rows[x, pl.ds(turn * (extent_y - 2), 2)] = far[x]
+        rows[x, pl.ds(2 - 2 * turn, extent_y - 2)] = main
+        out[:, x] = jnp.swapaxes(rows[x], 0, 1)
+
+
+def store_two(flip, far, center, sides):
+    extent_x, _, channels, depth = far.shape
+    extent_y = center.shape[1] + 2
+    return pl.pallas_call(
+        store_two_kernel,
+        name="store_two",
+        out_shape=jax.ShapeDtypeStruct((channels, extent_x, extent_y, depth), BF16),
+        in_specs=[SCALAR] + [VMEM] * 3,
+        out_specs=VMEM,
+        scratch_shapes=[pltpu.VMEM((extent_x, extent_y, channels, depth), BF16)],
+        cost_estimate=COST,
+        compiler_params=pltpu.CompilerParams(vmem_limit_bytes=16 << 20),
+    )(flip, *map(near_memory, (far, center, sides)))
 
 
 def three_kernel(layers, cells, left, right, mix, bias, out, windows, paired):
@@ -351,7 +423,7 @@
     )(*map(near_memory, (cells, left, right, mix, bias_values)))
 
 
-def four_kernel(count_y, tiles, weights, bias, out, rolled, mix):
+def four_kernel(count_y, tiles, weights, bias, columns, out, three_out, rolled, mix):
     _, parts, lanes = tiles.shape
     extent_x, extent_y, layers, out_channels = out.shape
     rows = count_y * 8
@@ -385,6 +457,14 @@
                     else:
                         tap = weights[9 * a + 3 * c + e]
                     mix[row : row + half, lane : lane + out_channels] = tap
+    depth = three_out.shape[3]
+    for x in range(columns.shape[0]):
+        rows_of_y = [
+            columns[x, pair][None, :, part * depth : (part + 1) * depth]
+            for pair in range(columns.shape[1])
+            for part in range(2)
+        ]
+        three_out[:, x] = jnp.swapaxes(jnp.concatenate(rows_of_y, axis=0), 0, 1)
     offset = jnp.concatenate([bias[...], bias[...]], axis=1)
     matrix = mix[...]
     group = min(extent_x, 4)
@@ -402,35 +482,38 @@
                 out[x + dx, y] = result[row : row + layers, lane : lane + out_channels]
 
 
-def four(tiles, weights, bias, extents, count_y):
+def four(tiles, weights, bias, columns, extents, count_y):
     extent_x, extent_y, layers = extents
+    three_x, pairs, three_channels, lanes = columns.shape
     _, channels, out_channels = weights.shape
     return pl.pallas_call(
         functools.partial(four_kernel, count_y),
         name="four",
-        out_shape=jax.ShapeDtypeStruct((extent_x, extent_y, layers, out_channels), BF16),
-        in_specs=[VMEM] * 3,
-        out_specs=VMEM,
+        out_shape=(
+            jax.ShapeDtypeStruct((extent_x, extent_y, layers, out_channels), BF16),
+            jax.ShapeDtypeStruct((three_channels, three_x, 2 * pairs, lanes // 2), BF16),
+        ),
+        in_specs=[VMEM] * 4,
+        out_specs=(VMEM, VMEM),
         scratch_shapes=[
             pltpu.VMEM((extent_x + 2, count_y * layers, 6 * tiles.shape[2]), BF16),
             pltpu.VMEM((36 * channels, 2 * out_channels), BF16),
         ],
         cost_estimate=COST,
         compiler_params=pltpu.CompilerParams(vmem_limit_bytes=16 << 20),
-    )(near_memory(tiles), near_memory(weights), near_memory(bias))
+    )(*map(near_memory, (tiles, weights, bias, columns)))
 
 
 def shards(features, weight_two, bias_two, weight_three, bias_three, weight_four, bias_four):
     count_x, count_y = lax.axis_size("gx"), lax.axis_size("gy")
     width = 3
-    cells = features.transpose(1, 2, 0, 3)
-    extent_x, extent_y, channels, depth = cells.shape
+    channels, extent_x, extent_y, depth = features.shape
     even = lax.axis_index("gy") % 2 == 0
     flip = 1 - even.astype(jnp.int32)[None]
-    head, tail = cells[:, :width], cells[:, : -width - 1 : -1]
+    cells, head, tail = split(flip, features, width)
     near_pairs, far_pairs = pairings("gy")
-    far = lax.ppermute(jnp.where(even, head, tail), "gy", far_pairs)
-    near = lax.ppermute(jnp.where(even, tail, head), "gy", near_pairs)
+    far = lax.ppermute(head, "gy", far_pairs)
+    near = lax.ppermute(tail, "gy", near_pairs)
     left, right = shift_exchange(
         jnp.concatenate([cells[0], near[0]], axis=0),
         jnp.concatenate([cells[-1], near[-1]], axis=0),
@@ -491,15 +574,10 @@
         ],
         [rim, (extent_x // 2, 2, channels, depth)],
     )
-    main = jnp.concatenate([sides[:2], center, sides[2:]], axis=0)
-    level_two = jnp.where(
-        even,
-        jnp.concatenate([far_out, main], axis=1),
-        jnp.concatenate([main, far_out], axis=1),
-    ).transpose(2, 0, 1, 3)
+    level_two = store_two(flip, far_out, center, sides)
 
     left, right = shift_exchange(low, high, "gx")
-    level_three, windows = three(
+    columns, windows = three(
         pooled, left, right, weight_three, bias_three, count_x, count_y
     )
     slots = count_x * count_y
@@ -507,11 +585,10 @@
         windows.reshape((slots,) + windows.shape[2:]), ("gx", "gy"), 0, 0, tiled=True
     )
     extents = (count_x * extent_x // 4, count_y * extent_y // 4, depth // 4 // count_y)
-    bottleneck = four(tiles, weight_four.transpose(0, 2, 1), bias_four, extents, count_y)
-    out_three = level_three.reshape(level_three.shape[:3] + (2, level_three.shape[3] // 2))
-    out_three = out_three.transpose(2, 0, 1, 3, 4)
-    out_three = out_three.reshape(out_three.shape[:2] + (-1, out_three.shape[4]))
-    return level_two, out_three, bottleneck.transpose(3, 0, 1, 2)
+    bottleneck, level_three = four(
+        tiles, weight_four.transpose(0, 2, 1), bias_four, columns, extents, count_y
+    )
+    return level_two, level_three, bottleneck.transpose(3, 0, 1, 2)
 
 
 def solution(mesh):

time: 38.2 us -> 38 us (level)
  local copies, waits for them, and re-layouts: 4.29 us -> 0.86 us
  Pallas kernels: 6.27 us -> 8.65 us
  waiting for transfers between devices: 10.1 us -> 11.2 us
    unnamed x14 -> x12, local copies, waits for them, and re-layouts: 3.08 us -> 0.7 us
    pallas_call x0 -> x2, Pallas kernels: none -> 2.29 us  [the longest x1 1.23 us: split(): pl.pallas_call(split_kernel, name='split', out_shape=(local((extent_x, ex...]
    all_to_all x1, waiting for transfers between devices: 6.03 us -> 7.08 us  [shards(): lax.all_to_all(windows.reshape((slots,) + windows.shape[2:]), ('gx', 'gy'...]
    transpose x1 -> x0, local copies, waits for them, and re-layouts: 0.89 us -> none  [shards(): out_three = out_three.transpose(2, 0, 1, 3, 4)]
  transfers between devices with their start and end apart: 9 -> 9, of which waited for: 4 -> 4; matrix products, arithmetic and copies ran while one was open for 6% -> 0% of each run, Pallas kernels for 7% -> 10%
where the time goes in v5:
time: 38 us; the launch traced here: 37.8 us
  starting transfers between devices  16.3 us (43%)
  waiting for transfers between devices  11.2 us (29%)
  Pallas kernels  8.65 us (23%)
  local copies, waits for them, and re-layouts  0.86 us (2%)
  between operations  0.78 us (2%)
    all_to_all x1, waiting for transfers between devices, shards(): lax.all_to_all(windows.reshape((slots,) + windows.shape[2:]), ('gx', 'gy'...  7.08 us
    ppermute x3, starting transfers between devices, shift_exchange(): lax.ppermute(low, axis, [((i + 1) % count, i) for i in range(count)])  4.78 us
    ppermute x1, starting transfers between devices, shards(): far = lax.ppermute(head, 'gy', far_pairs)  4.7 us
    ppermute x3, starting transfers between devices, shift_exchange(): lax.ppermute(high, axis, [(i, (i + 1) % count) for i in range(count)])  3.68 us
    pallas_call x5, Pallas kernels, kernel_call(): pl.pallas_call(body, out_shape=tuple((local(result) if isinstance(result,...  3.45 us
    all_to_all x1, starting transfers between devices, shards(): lax.all_to_all(windows.reshape((slots,) + windows.shape[2:]), ('gx', 'gy'...  2.58 us
    ppermute x3, waiting for transfers between devices, shift_exchange(): lax.ppermute(high, axis, [(i, (i + 1) % count) for i in range(count)])  1.67 us
    pallas_call x1, Pallas kernels, three(): pl.pallas_call(functools.partial(three_kernel, layers), name='three', out...  1.52 us
  transfers between devices with their start and end apart: 9, of which 4 were waited for; matrix products, arithmetic and copies ran while one was open for 0% of the time, Pallas kernels for 10%

profile of v5, /device:TPU:0, one launch (start us, length us, event | category | flops | bytes accessed | tf_op | source)
XLA Modules:
  0.0 37.8 jit_solution(11356801822117325029)
XLA Ops:
  0.7 1.2 %split.1 = (bf16[8,8,32,128]{3,2,1,0:T(8,128)(2,1)S(1)}, bf16[8,3,32,128]{3,2,1,0:T(8,128)(2,1)S(1)}, bf16[8,3,32,128]{3,2,1,0:T(8,128)(2,1)S(1)}) custom-call(s32[1]{0:T(128)} %bitcast.flip, bf16[32,8,8,128]{3,2,1,0:T(8,128)(2,1)} %features.1), custom_call_target="tpu_custom_call" | custom-call | flops 1073741824 | bytes 1048576 | tf_op jit(solution)/shard_map/split/pallas_call | solution.py:100
  1.9 0.6 %collective-permute-start.3 = (bf16[8,3,32,128]{3,2,1,0:T(8,128)(2,1)S(1)}, bf16[8,3,32,128]{3,2,1,0:T(8,128)(2,1)S(1)}, u32[]{:S(2)}, u32[]{:S(2)}) collective-permute-start(bf16[8,3,32,128]{3,2,1,0:T(8,128)(2,1)S(1)} %get-tuple-element.28), channel_id=1, source_target_pairs={{0,1},{1,0},{2,3},{3,2},{4,5},{5,4},{6,7},{7,6},{8,9},{9,8},{10,11... | collective-permute-start | bytes 589832 | tf_op jit(solution)/shard_map/ppermute | solution.py:516
  2.5 4.7 %collective-permute-start = (bf16[8,3,32,128]{3,2,1,0:T(8,128)(2,1)S(1)}, bf16[8,3,32,128]{3,2,1,0:T(8,128)(2,1)S(1)}, u32[]{:S(2)}, u32[]{:S(2)}) collective-permute-start(bf16[8,3,32,128]{3,2,1,0:T(8,128)(2,1)S(1)} %get-tuple-element.26), channel_id=1, source_target_pairs={{0,7},{1,2},{2,1},{3,4},{4,3},{5,6},{6,5},{7,0},{8,15},{9,10},{10,... | collective-permute-start | bytes 589832 | tf_op jit(solution)/shard_map/ppermute | solution.py:515
  7.2 0.6 %copy-done.2 = f32[32]{0:T(128)S(1)} copy-done((f32[32]{0:T(128)S(1)}, f32[32]{0:T(128)}, u32[]{:S(2)}) %copy-start.2) | copy-done | bytes 152
  7.8 0.0 copy-done.3
  7.8 0.0 copy-done.4
  7.8 0.2 shard_map.94
  8.0 0.0 collective-permute-done.3.near
  8.1 2.5 %collective-permute-start.5 = (bf16[11,32,128]{2,1,0:T(8,128)(2,1)S(1)}, bf16[11,32,128]{2,1,0:T(8,128)(2,1)S(1)}, u32[]{:S(2)}, u32[]{:S(2)}) collective-permute-start(bf16[11,32,128]{2,1,0:T(8,128)(2,1)S(1)} %pad_maximum_fusion.1), channel_id=1, source_target_pairs={{8,0},{16,8},{24,16},{0,24},{9,1},{17,9},{25,17},{1,25},{10,2},{18... | collective-permute-start | bytes 270344 | tf_op jit(solution)/shard_map/ppermute | solution.py:38
  10.6 0.1 collective-permute-start.4
  10.6 1.2 %collective-permute-done.far = bf16[8,3,32,128]{3,2,1,0:T(8,128)(2,1)S(1)} collective-permute-done((bf16[8,3,32,128]{3,2,1,0:T(8,128)(2,1)S(1)}, bf16[8,3,32,128]{3,2,1,0:T(8,128)(2,1)S(1)}, u32[]{:S(2)}, u32[]{:S(2)}) %collective-permute-start) | collective-permute-done | bytes 196640 | tf_op jit(solution)/shard_map/ppermute | solution.py:515
  11.9 1.5 %collective-permute-start.1 = (bf16[3,32,128]{2,1,0:T(8,128)(2,1)S(1)}, bf16[3,32,128]{2,1,0:T(8,128)(2,1)S(1)}, u32[]{:S(2)}, u32[]{:S(2)}) collective-permute-start(bf16[3,32,128]{2,1,0:T(8,128)(2,1)S(1)} %get-tuple-element.54), channel_id=1, source_target_pairs={{0,8},{8,16},{16,24},{24,0},{1,9},{9,17},{17,25},{25,1},{2,10},{10... | collective-permute-start | bytes 73736 | tf_op jit(solution)/shard_map/ppermute | solution.py:37
  13.4 1.4 %collective-permute-start.2 = (bf16[3,32,128]{2,1,0:T(8,128)(2,1)S(1)}, bf16[3,32,128]{2,1,0:T(8,128)(2,1)S(1)}, u32[]{:S(2)}, u32[]{:S(2)}) collective-permute-start(bf16[3,32,128]{2,1,0:T(8,128)(2,1)S(1)} %get-tuple-element.53), channel_id=1, source_target_pairs={{8,0},{16,8},{24,16},{0,24},{9,1},{17,9},{25,17},{1,25},{10,2},{18... | collective-permute-start | bytes 73736 | tf_op jit(solution)/shard_map/ppermute | solution.py:38
  14.8 1.0 %shard_map.96 = (bf16[4,6,32,128]{3,2,1,0:T(8,128)(2,1)S(1)}, bf16[2,4,32,128]{3,2,1,0:T(8,128)(2,1)S(1)}, bf16[3,6,3,32,128]{4,3,2,1,0:T(8,128)(2,1)S(1)}) custom-call(s32[1]{0:T(128)} %bitcast.flip, bf16[8,8,32,128]{3,2,1,0:T(8,128)(2,1)S(1)} %get-tuple-element.27.cells, bf16[8,3,32,128]{3,2,1,0:T(8,128)(2,1)S(1)} %collective-permute-done.3.near, ...), custom_call_target="tpu_custom_call" | custom-call | flops 1073741824 | bytes 1048576 | tf_op jit(solution)/shard_map/pallas_call | solution.py:304
  15.8 0.6 %shard_map.97 = (bf16[4,2,32,128]{3,2,1,0:T(8,128)(2,1)S(1)}, bf16[2,2,32,128]{3,2,1,0:T(8,128)(2,1)S(1)}) custom-call(s32[1]{0:T(128)} %bitcast.flip, bf16[8,3,32,128]{3,2,1,0:T(8,128)(2,1)S(1)} %collective-permute-done.far, bf16[3,6,3,32,128]{4,3,2,1,0:T(8,128)(2,1)S(1)} %get-tuple-element.32.edge, bf16[128,1536]{1,0:T(8,128)(2,1)S(1)} %get-tuple-element.29.mix, ...), custom_call_target="tpu_custom_call" | custom-call | flops 1073741824 | bytes 1048576 | tf_op jit(solution)/shard_map/pallas_call | solution.py:304
  16.4 0.0 collective-permute-done.5.right
  16.4 0.0 collective-permute-done.4.left
  16.4 1.0 %shard_map.95 = (bf16[4,6,32,128]{3,2,1,0:T(8,128)(2,1)S(1)}, bf16[2,4,32,128]{3,2,1,0:T(8,128)(2,1)S(1)}, bf16[3,8,3,32,128]{4,3,2,1,0:T(8,128)(2,1)S(1)}) custom-call(s32[1]{0:T(128)} %bitcast.flip, bf16[8,8,32,128]{3,2,1,0:T(8,128)(2,1)S(1)} %get-tuple-element.27.cells, bf16[8,3,32,128]{3,2,1,0:T(8,128)(2,1)S(1)} %collective-permute-done.3.near, ...), custom_call_target="tpu_custom_call" | custom-call | flops 1073741824 | bytes 1048576 | tf_op jit(solution)/shard_map/pallas_call | solution.py:304
  17.5 0.0 collective-permute-done.2.right
  17.5 0.0 copy-start.5
  17.5 0.6 %shard_map.98 = (bf16[8,2,32,128]{3,2,1,0:T(8,128)(2,1)S(1)}, bf16[4,6,32,128]{3,2,1,0:T(8,128)(2,1)S(1)}, bf16[3,32,128]{2,1,0:T(8,128)(2,1)S(1)}, bf16[3,32,128]{2,1,0:T(8,128)(2,1)S(1)}) custom-call(s32[1]{0:T(128)} %bitcast.flip, bf16[8,3,32,128]{3,2,1,0:T(8,128)(2,1)S(1)} %collective-permute-done.far, ...), custom_call_target="tpu_custom_call" | custom-call | flops 1073741824 | bytes 1048576 | tf_op jit(solution)/shard_map/pallas_call | solution.py:304
  18.1 2.1 %collective-permute-start.6 = (bf16[3,32,128]{2,1,0:T(8,128)(2,1)S(1)}, bf16[3,32,128]{2,1,0:T(8,128)(2,1)S(1)}, u32[]{:S(2)}, u32[]{:S(2)}) collective-permute-start(bf16[3,32,128]{2,1,0:T(8,128)(2,1)S(1)} %get-tuple-element.41), channel_id=1, source_target_pairs={{0,8},{8,16},{16,24},{24,0},{1,9},{9,17},{17,25},{25,1},{2,10},{10... | collective-permute-start | bytes 73736 | tf_op jit(solution)/shard_map/ppermute | solution.py:37
  20.3 0.9 %collective-permute-start.7 = (bf16[3,32,128]{2,1,0:T(8,128)(2,1)S(1)}, bf16[3,32,128]{2,1,0:T(8,128)(2,1)S(1)}, u32[]{:S(2)}, u32[]{:S(2)}) collective-permute-start(bf16[3,32,128]{2,1,0:T(8,128)(2,1)S(1)} %get-tuple-element.42), channel_id=1, source_target_pairs={{8,0},{16,8},{24,16},{0,24},{9,1},{17,9},{25,17},{1,25},{10,2},{18... | collective-permute-start | bytes 73736 | tf_op jit(solution)/shard_map/ppermute | solution.py:38
  21.1 0.1 copy.11.mix
  21.3 1.7 %collective-permute-done.6.left = bf16[3,32,128]{2,1,0:T(8,128)(2,1)S(1)} collective-permute-done((bf16[3,32,128]{2,1,0:T(8,128)(2,1)S(1)}, bf16[3,32,128]{2,1,0:T(8,128)(2,1)S(1)}, u32[]{:S(2)}, u32[]{:S(2)}) %collective-permute-start.6) | collective-permute-done | bytes 24608 | tf_op jit(solution)/shard_map/ppermute | solution.py:37
  22.9 1.2 %collective-permute-done.7.right = bf16[3,32,128]{2,1,0:T(8,128)(2,1)S(1)} collective-permute-done((bf16[3,32,128]{2,1,0:T(8,128)(2,1)S(1)}, bf16[3,32,128]{2,1,0:T(8,128)(2,1)S(1)}, u32[]{:S(2)}, u32[]{:S(2)}) %collective-permute-start.7) | collective-permute-done | bytes 24608 | tf_op jit(solution)/shard_map/ppermute | solution.py:38
  24.1 1.5 %three.1 = (bf16[4,2,64,128]{3,2,1,0:T(8,128)(2,1)S(1)}, bf16[4,8,16,128]{3,2,1,0:T(8,128)(2,1)}) custom-call(bf16[4,6,32,128]{3,2,1,0:T(8,128)(2,1)S(1)} %get-tuple-element.40.cells, bf16[3,32,128]{2,1,0:T(8,128)(2,1)S(1)} %collective-permute-done.6.left, bf16[3,32,128]{2,1,0:T(8,128)(2,1)S(1)} %collective-permute-done.7.right, ...), custom_call_target="tpu_custom_call" | custom-call | flops 1073741824 | bytes 1048576 | tf_op jit(solution)/shard_map/three/pallas_call | solution.py:411
  25.6 2.6 %all-to-all-start = ((bf16[32,16,128]{2,1,0:T(8,128)(2,1)}), bf16[32,16,128]{2,1,0:T(8,128)(2,1)S(1)}, u32[]{:S(2)}, u32[]{:S(2)}) async-start(bf16[32,16,128]{2,1,0:T(8,128)(2,1)} %bitcast.12), calls=%async_computation | async-start | bytes 262144 | tf_op jit(solution)/shard_map/all_to_all | solution.py:584
  28.2 0.0 copy-start
  28.2 1.1 %store_two.1 = bf16[32,8,8,128]{3,2,1,0:T(8,128)(2,1)} custom-call(s32[1]{0:T(128)} %bitcast.flip, bf16[8,2,32,128]{3,2,1,0:T(8,128)(2,1)S(1)} %get-tuple-element.37.far, bf16[4,6,32,128]{3,2,1,0:T(8,128)(2,1)S(1)} %get-tuple-element.38.center, bf16[4,6,32,128]{3,2,1,0:T(8,128)(2,1)S(1)} %get-tuple-element.39.sides), custom_call_target="tpu_custom_call" | custom-call | flops 1073741824 | bytes 1048576 | tf_op jit(solution)/shard_map/store_two/pallas_call | solution.py:334
  29.3 7.1 %all-to-all-done.tiles = bf16[32,16,128]{2,1,0:T(8,128)(2,1)S(1)} async-done(((bf16[32,16,128]{2,1,0:T(8,128)(2,1)}), bf16[32,16,128]{2,1,0:T(8,128)(2,1)S(1)}, u32[]{:S(2)}, u32[]{:S(2)}) %all-to-all-start) | async-done | bytes 131104 | tf_op jit(solution)/shard_map/all_to_all | solution.py:584
  36.4 1.4 %four.1 = (bf16[8,16,4,128]{3,2,1,0:T(4,128)(2,1)}, bf16[64,4,4,64]{3,2,1,0:T(4,128)(2,1)}) custom-call(bf16[32,16,128]{2,1,0:T(8,128)(2,1)S(1)} %all-to-all-done.tiles, bf16[27,64,128]{2,1,0:T(8,128)(2,1)S(1)} %bitcast.22, f32[1,128]{1,0:T(1,128)S(1)} %get-tuple-element.45.bias, bf16[4,2,64,128]{3,2,1,0:T(8,128)(2,1)S(1)} %get-tuple-element.46.columns), custom_call_target="tpu_custom_call" | custom-call | flops 1073741824 | bytes 1048576 | tf_op jit(solution)/shard_map/four/pallas_call | solution.py:489
  (13 shorter events, 0.1 us)
Async XLA Ops:
  0.6 6.5 %copy-start.1 = (bf16[27,32,32]{2,1,0:T(8,128)(2,1)S(1)}, bf16[27,32,32]{2,1,0:T(8,128)(2,1)}, u32[]{:S(2)}) copy-start(bf16[27,32,32]{2,1,0:T(8,128)(2,1)} %weights.1) | copy-start | bytes 165892
  1.9 6.1 %collective-permute-start.3 = (bf16[8,3,32,128]{3,2,1,0:T(8,128)(2,1)S(1)}, bf16[8,3,32,128]{3,2,1,0:T(8,128)(2,1)S(1)}, u32[]{:S(2)}, u32[]{:S(2)}) collective-permute-start(bf16[8,3,32,128]{3,2,1,0:T(8,128)(2,1)S(1)} %get-tuple-element.28), channel_id=1, source_target_pairs={{0,1},{1,0},{2,3},{3,2},{4,5},{5,4},{6,7},{7,6},{8,9},{9,8},{10,11... | collective-permute-start | bytes 589832 | tf_op jit(solution)/shard_map/ppermute | solution.py:516
  2.5 9.4 %collective-permute-start = (bf16[8,3,32,128]{3,2,1,0:T(8,128)(2,1)S(1)}, bf16[8,3,32,128]{3,2,1,0:T(8,128)(2,1)S(1)}, u32[]{:S(2)}, u32[]{:S(2)}) collective-permute-start(bf16[8,3,32,128]{3,2,1,0:T(8,128)(2,1)S(1)} %get-tuple-element.26), channel_id=1, source_target_pairs={{0,7},{1,2},{2,1},{3,4},{4,3},{5,6},{6,5},{7,0},{8,15},{9,10},{10,... | collective-permute-start | bytes 589832 | tf_op jit(solution)/shard_map/ppermute | solution.py:515
  7.1 0.7 %copy-start.2 = (f32[32]{0:T(128)S(1)}, f32[32]{0:T(128)}, u32[]{:S(2)}) copy-start(f32[32]{0:T(128)} %param.9) | copy-start | bytes 388
  7.2 0.7 %copy-start.3 = (f32[64]{0:T(128)S(1)}, f32[64]{0:T(128)}, u32[]{:S(2)}) copy-start(f32[64]{0:T(128)} %param.11) | copy-start | bytes 772
  7.2 0.7 %copy-start.4 = (f32[128]{0:T(128)S(1)}, f32[128]{0:T(128)}, u32[]{:S(2)}) copy-start(f32[128]{0:T(128)} %param.13) | copy-start | bytes 1540
  8.1 8.3 %collective-permute-start.5 = (bf16[11,32,128]{2,1,0:T(8,128)(2,1)S(1)}, bf16[11,32,128]{2,1,0:T(8,128)(2,1)S(1)}, u32[]{:S(2)}, u32[]{:S(2)}) collective-permute-start(bf16[11,32,128]{2,1,0:T(8,128)(2,1)S(1)} %pad_maximum_fusion.1), channel_id=1, source_target_pairs={{8,0},{16,8},{24,16},{0,24},{9,1},{17,9},{25,17},{1,25},{10,2},{18... | collective-permute-start | bytes 270344 | tf_op jit(solution)/shard_map/ppermute | solution.py:38
  10.6 5.8 %collective-permute-start.4 = (bf16[11,32,128]{2,1,0:T(8,128)(2,1)S(1)}, bf16[11,32,128]{2,1,0:T(8,128)(2,1)S(1)}, u32[]{:S(2)}, u32[]{:S(2)}) collective-permute-start(bf16[11,32,128]{2,1,0:T(8,128)(2,1)S(1)} %pad_maximum_fusion), channel_id=1, source_target_pairs={{0,8},{8,16},{16,24},{24,0},{1,9},{9,17},{17,25},{25,1},{2,10},{10... | collective-permute-start | bytes 270344 | tf_op jit(solution)/shard_map/ppermute | solution.py:37
  11.9 5.6 %collective-permute-start.1 = (bf16[3,32,128]{2,1,0:T(8,128)(2,1)S(1)}, bf16[3,32,128]{2,1,0:T(8,128)(2,1)S(1)}, u32[]{:S(2)}, u32[]{:S(2)}) collective-permute-start(bf16[3,32,128]{2,1,0:T(8,128)(2,1)S(1)} %get-tuple-element.54), channel_id=1, source_target_pairs={{0,8},{8,16},{16,24},{24,0},{1,9},{9,17},{17,25},{25,1},{2,10},{10... | collective-permute-start | bytes 73736 | tf_op jit(solution)/shard_map/ppermute | solution.py:37
  13.4 4.1 %collective-permute-start.2 = (bf16[3,32,128]{2,1,0:T(8,128)(2,1)S(1)}, bf16[3,32,128]{2,1,0:T(8,128)(2,1)S(1)}, u32[]{:S(2)}, u32[]{:S(2)}) collective-permute-start(bf16[3,32,128]{2,1,0:T(8,128)(2,1)S(1)} %get-tuple-element.53), channel_id=1, source_target_pairs={{8,0},{16,8},{24,16},{0,24},{9,1},{17,9},{25,17},{1,25},{10,2},{18... | collective-permute-start | bytes 73736 | tf_op jit(solution)/shard_map/ppermute | solution.py:38
  17.5 3.6 %copy-start.5 = (bf16[27,64,32]{1,2,0:T(8,128)(2,1)S(1)}, bf16[27,64,32]{1,2,0:T(8,128)(2,1)}, u32[]{:S(2)}) copy-start(bf16[27,64,32]{1,2,0:T(8,128)(2,1)} %param.10) | copy-start | bytes 331780
  18.1 4.8 %collective-permute-start.6 = (bf16[3,32,128]{2,1,0:T(8,128)(2,1)S(1)}, bf16[3,32,128]{2,1,0:T(8,128)(2,1)S(1)}, u32[]{:S(2)}, u32[]{:S(2)}) collective-permute-start(bf16[3,32,128]{2,1,0:T(8,128)(2,1)S(1)} %get-tuple-element.41), channel_id=1, source_target_pairs={{0,8},{8,16},{16,24},{24,0},{1,9},{9,17},{17,25},{25,1},{2,10},{10... | collective-permute-start | bytes 73736 | tf_op jit(solution)/shard_map/ppermute | solution.py:37
  20.3 3.8 %collective-permute-start.7 = (bf16[3,32,128]{2,1,0:T(8,128)(2,1)S(1)}, bf16[3,32,128]{2,1,0:T(8,128)(2,1)S(1)}, u32[]{:S(2)}, u32[]{:S(2)}) collective-permute-start(bf16[3,32,128]{2,1,0:T(8,128)(2,1)S(1)} %get-tuple-element.42), channel_id=1, source_target_pairs={{8,0},{16,8},{24,16},{0,24},{9,1},{17,9},{25,17},{1,25},{10,2},{18... | collective-permute-start | bytes 73736 | tf_op jit(solution)/shard_map/ppermute | solution.py:38
  25.6 10.7 %all-to-all-start = ((bf16[32,16,128]{2,1,0:T(8,128)(2,1)}), bf16[32,16,128]{2,1,0:T(8,128)(2,1)S(1)}, u32[]{:S(2)}, u32[]{:S(2)}) async-start(bf16[32,16,128]{2,1,0:T(8,128)(2,1)} %bitcast.12), calls=%async_computation | async-start | bytes 262144 | tf_op jit(solution)/shard_map/all_to_all | solution.py:584
  28.2 8.2 %copy-start = (bf16[27,128,64]{1,2,0:T(8,128)(2,1)S(1)}, bf16[27,128,64]{1,2,0:T(8,128)(2,1)}, u32[]{:S(2)}) copy-start(bf16[27,128,64]{1,2,0:T(8,128)(2,1)} %param.12) | copy-start | bytes 1327108

commit v6 on v5

--- a/solution.py
+++ b/solution.py
@@ -343,53 +343,75 @@
     )(flip, *map(near_memory, (far, center, sides)))
 
 
-def three_kernel(layers, cells, left, right, mix, bias, out, windows, paired):
-    extent_x, wide_y, channels, lanes = cells.shape
-    extent_y = wide_y - 2
+def pair_columns(turned, target, at):
+    channels, lanes = turned[0][0].shape
+    first = lax.broadcasted_iota(jnp.int32, (channels, lanes), 1) < lanes // 2
+    for y in range(len(turned) - 1):
+        for e in range(3):
+            target[at, y, e] = jnp.where(first, turned[y][e], turned[y + 1][e])
+
+
+def mix_three(matrix, offset, columns, pairs):
+    pieces = []
+    for frame, py in pairs:
+        taps = [
+            source[at, 2 * py + c].reshape(-1, source.shape[4])
+            for source, at in frame
+            for c in range(3)
+        ]
+        pieces.append(jnp.concatenate(taps, axis=0))
+    stacked = jnp.concatenate(pieces, axis=1)
+    result = leaky(jnp.dot(matrix, stacked, preferred_element_type=F32) + offset).astype(BF16)
+    return [result[:, at * columns : (at + 1) * columns] for at in range(len(pairs))]
+
+
+def own_three_kernel(cells, mix, bias, inside, paired):
+    extent_x, wide_y, _, lanes = cells.shape
+    for x in range(extent_x):
+        pair_columns([shifts(cells[x, y]) for y in range(wide_y)], paired, x)
+    offset = column(bias)
+    matrix = mix[...]
+    for py in range((wide_y - 2) // 2):
+        places = range(1, extent_x - 1)
+        pairs = [([(paired, x + a) for a in (-1, 0, 1)], py) for x in places]
+        for x, part in zip(places, mix_three(matrix, offset, lanes, pairs)):
+            inside[x - 1, py] = part
+
+
+def three_kernel(layers, paired, inside, left, right, mix, bias, out, windows, outer):
+    extent_x, wide_y, _, channels, lanes = paired.shape
+    extent_y = wide_y - 1
     depth = lanes // 2
     senders, slots = windows.shape[:2]
-
-    def place(x, y):
-        if 0 < x < extent_x + 1:
-            return cells[x - 1, y]
-        both = (left if x == 0 else right)[y // 2]
-        return jnp.where(first == (y % 2 == 0), both, pltpu.roll(both, depth, 1))
-
     first = lax.broadcasted_iota(jnp.int32, (channels, lanes), 1) < depth
-    for x in range(extent_x + 2):
-        turned = [shifts(place(x, y)) for y in range(extent_y + 2)]
-        for y in range(extent_y + 1):
-            for e in range(3):
-                paired[x, y, e] = jnp.where(first, turned[y][e], turned[y + 1][e])
+    for side, source in enumerate((left, right)):
+        turned = []
+        for y in range(extent_y + 2):
+            both = source[y // 2]
+            both = jnp.where(first == (y % 2 == 0), both, pltpu.roll(both, depth, 1))
+            turned.append(shifts(both))
+        pair_columns(turned, outer, side)
     offset = column(bias)
     rows = lax.broadcasted_iota(jnp.int32, (slots * 8, 2 * lanes), 0)
     layer = rows % 8
     wanted = (layers * (rows // 8) + layer + depth // 2 - 1) % (depth // 2)
     source = lax.broadcasted_iota(jnp.int32, (slots * 8, 2 * lanes), 1) % depth // 2
     pool = jnp.where((source == wanted) & (layer < layers + 2), 0.125, 0.0).astype(BF16)
-    matrix = mix[...]
+    last = extent_x - 1
+    ends = (
+        [(outer, 0), (paired, 0), (paired, 1)],
+        [(paired, last - 1), (paired, last), (outer, 1)],
+    )
+    pairs = [(frame, py) for frame in ends for py in range(extent_y // 2)]
+    parts = mix_three(mix[...], offset, lanes, pairs)
+    for at, part in enumerate(parts):
+        out[last * (at // (extent_y // 2)), at % (extent_y // 2)] = part
+    out[1:last] = inside[...]
     for px in range(extent_x // 2):
-        results = []
-        for py in range(extent_y // 2):
-            stacked = jnp.concatenate(
-                [
-                    jnp.concatenate(
-                        [
-                            paired[x + a, 2 * py + c].reshape(3 * channels, lanes)
-                            for a in range(3)
-                            for c in range(3)
-                        ],
-                        axis=0,
-                    )
-                    for x in (2 * px, 2 * px + 1)
-                ],
-                axis=1,
-            )
-            result = jnp.dot(matrix, stacked, preferred_element_type=F32)
-            result = leaky(result + offset).astype(BF16)
-            out[2 * px, py] = result[:, :lanes]
-            out[2 * px + 1, py] = result[:, lanes:]
-            results.append(result)
+        results = [
+            jnp.concatenate([out[2 * px, py], out[2 * px + 1, py]], axis=1)
+            for py in range(extent_y // 2)
+        ]
         means = lax.dot_general(
             pool,
             jnp.concatenate(results, axis=0),
@@ -401,13 +423,27 @@
                 windows[sender, slot, 8 * px : 8 * px + 8] = means[8 * slot : 8 * slot + 8]
 
 
-def three(cells, left, right, weights, bias_values, count_x, count_y):
+def own_three(cells, mix, bias):
     extent_x, wide_y, channels, lanes = cells.shape
-    extent_y = wide_y - 2
-    depth = lanes // 2
-    out_channels = weights.shape[1]
-    layers = depth // 2 // count_y
-    mix = weights.transpose(1, 0, 2).reshape(out_channels, 27 * channels)
+    return pl.pallas_call(
+        own_three_kernel,
+        name="own_three",
+        out_shape=(
+            local((extent_x - 2, (wide_y - 2) // 2, mix.shape[0], lanes)),
+            local((extent_x, wide_y - 1, 3, channels, lanes)),
+        ),
+        in_specs=[VMEM] * 3,
+        out_specs=(VMEM, VMEM),
+        cost_estimate=COST,
+        compiler_params=pltpu.CompilerParams(vmem_limit_bytes=16 << 20),
+    )(*map(near_memory, (cells, mix, bias)))
+
+
+def three(paired, inside, left, right, mix, bias, count_x, count_y):
+    extent_x, wide_y, _, channels, lanes = paired.shape
+    extent_y = wide_y - 1
+    out_channels = mix.shape[0]
+    layers = lanes // 4 // count_y
     return pl.pallas_call(
         functools.partial(three_kernel, layers),
         name="three",
@@ -415,12 +451,12 @@
             local((extent_x, extent_y // 2, out_channels, lanes)),
             local((count_x, count_y, extent_x // 2 * 8, extent_y // 2 * out_channels)),
         ),
-        in_specs=[VMEM] * 5,
+        in_specs=[VMEM] * 6,
         out_specs=(VMEM, VMEM),
-        scratch_shapes=[pltpu.VMEM((extent_x + 2, extent_y + 1, 3, channels, lanes), BF16)],
+        scratch_shapes=[pltpu.VMEM((2, wide_y, 3, channels, lanes), BF16)],
         cost_estimate=COST,
         compiler_params=pltpu.CompilerParams(vmem_limit_bytes=16 << 20),
-    )(*map(near_memory, (cells, left, right, mix, bias_values)))
+    )(*map(near_memory, (paired, inside, left, right, mix, bias)))
 
 
 def four_kernel(count_y, tiles, weights, bias, columns, out, three_out, rolled, mix):
@@ -577,8 +613,10 @@
     level_two = store_two(flip, far_out, center, sides)
 
     left, right = shift_exchange(low, high, "gx")
+    three_mix = weight_three.transpose(1, 0, 2).reshape(weight_three.shape[1], -1)
+    inside, paired = own_three(pooled, three_mix, bias_three)
     columns, windows = three(
-        pooled, left, right, weight_three, bias_three, count_x, count_y
+        paired, inside, left, right, three_mix, bias_three, count_x, count_y
     )
     slots = count_x * count_y
     tiles = lax.all_to_all(

time: 38 us -> 37.7 us (level)
  waiting for transfers between devices: 11.2 us -> 10.8 us
    pallas_call x0 -> x1, Pallas kernels: none -> 0.4 us  [own_three(): pl.pallas_call(own_three_kernel, name='own_three', out_shape=(local((exte...]
  transfers between devices with their start and end apart: 9 -> 9, of which waited for: 4 -> 5; matrix products, arithmetic and copies ran while one was open for 0% -> 0% of each run, Pallas kernels for 10% -> 11%
where the time goes in v6:
time: 37.7 us; the launch traced here: 37.5 us
  starting transfers between devices  16.3 us (43%)
  waiting for transfers between devices  10.8 us (29%)
  Pallas kernels  8.8 us (23%)
  local copies, waits for them, and re-layouts  0.84 us (2%)
  between operations  0.81 us (2%)
    all_to_all x1, waiting for transfers between devices, shards(): lax.all_to_all(windows.reshape((slots,) + windows.shape[2:]), ('gx', 'gy'...  7.08 us
    ppermute x3, starting transfers between devices, shift_exchange(): lax.ppermute(low, axis, [((i + 1) % count, i) for i in range(count)])  4.81 us
    ppermute x1, starting transfers between devices, shards(): far = lax.ppermute(head, 'gy', far_pairs)  4.7 us
    ppermute x3, starting transfers between devices, shift_exchange(): lax.ppermute(high, axis, [(i, (i + 1) % count) for i in range(count)])  3.65 us
    pallas_call x5, Pallas kernels, kernel_call(): pl.pallas_call(body, out_shape=tuple((local(result) if isinstance(result,...  3.44 us
    all_to_all x1, starting transfers between devices, shards(): lax.all_to_all(windows.reshape((slots,) + windows.shape[2:]), ('gx', 'gy'...  2.58 us
    ppermute x3, waiting for transfers between devices, shift_exchange(): lax.ppermute(high, axis, [(i, (i + 1) % count) for i in range(count)])  1.46 us
    pallas_call x1, Pallas kernels, four(): pl.pallas_call(functools.partial(four_kernel, count_y), name='four', out_...  1.39 us
  transfers between devices with their start and end apart: 9, of which 5 were waited for; matrix products, arithmetic and copies ran while one was open for 0% of the time, Pallas kernels for 11%

profile of v6, /device:TPU:0, one launch (start us, length us, event | category | flops | bytes accessed | tf_op | source)
XLA Modules:
  0.0 37.5 jit_solution(12704976617546330126)
XLA Ops:
  0.7 1.2 %split.1 = (bf16[8,8,32,128]{3,2,1,0:T(8,128)(2,1)S(1)}, bf16[8,3,32,128]{3,2,1,0:T(8,128)(2,1)S(1)}, bf16[8,3,32,128]{3,2,1,0:T(8,128)(2,1)S(1)}) custom-call(s32[1]{0:T(128)} %bitcast.flip, bf16[32,8,8,128]{3,2,1,0:T(8,128)(2,1)} %features.1), custom_call_target="tpu_custom_call" | custom-call | flops 1073741824 | bytes 1048576 | tf_op jit(solution)/shard_map/split/pallas_call | solution.py:100
  1.9 0.0 copy-start.1
  1.9 0.6 %collective-permute-start.3 = (bf16[8,3,32,128]{3,2,1,0:T(8,128)(2,1)S(1)}, bf16[8,3,32,128]{3,2,1,0:T(8,128)(2,1)S(1)}, u32[]{:S(2)}, u32[]{:S(2)}) collective-permute-start(bf16[8,3,32,128]{3,2,1,0:T(8,128)(2,1)S(1)} %get-tuple-element.30), channel_id=1, source_target_pairs={{0,1},{1,0},{2,3},{3,2},{4,5},{5,4},{6,7},{7,6},{8,9},{9,8},{10,11... | collective-permute-start | bytes 589832 | tf_op jit(solution)/shard_map/ppermute | solution.py:552
  2.5 4.7 %collective-permute-start = (bf16[8,3,32,128]{3,2,1,0:T(8,128)(2,1)S(1)}, bf16[8,3,32,128]{3,2,1,0:T(8,128)(2,1)S(1)}, u32[]{:S(2)}, u32[]{:S(2)}) collective-permute-start(bf16[8,3,32,128]{3,2,1,0:T(8,128)(2,1)S(1)} %get-tuple-element.28), channel_id=1, source_target_pairs={{0,7},{1,2},{2,1},{3,4},{4,3},{5,6},{6,5},{7,0},{8,15},{9,10},{10,... | collective-permute-start | bytes 589832 | tf_op jit(solution)/shard_map/ppermute | solution.py:551
  7.2 0.1 copy.11.mix
  7.3 0.0 copy-start.2
  7.3 0.0 copy-start.3
  7.4 0.6 %copy-done.2 = f32[32]{0:T(128)S(1)} copy-done((f32[32]{0:T(128)S(1)}, f32[32]{0:T(128)}, u32[]{:S(2)}) %copy-start.2) | copy-done | bytes 152
  8.0 0.0 copy-done.3
  8.0 0.0 copy-done.4
  8.0 0.2 shard_map.94
  8.2 2.5 %collective-permute-start.5 = (bf16[11,32,128]{2,1,0:T(8,128)(2,1)S(1)}, bf16[11,32,128]{2,1,0:T(8,128)(2,1)S(1)}, u32[]{:S(2)}, u32[]{:S(2)}) collective-permute-start(bf16[11,32,128]{2,1,0:T(8,128)(2,1)S(1)} %pad_maximum_fusion.1), channel_id=1, source_target_pairs={{8,0},{16,8},{24,16},{0,24},{9,1},{17,9},{25,17},{1,25},{10,2},{18... | collective-permute-start | bytes 270344 | tf_op jit(solution)/shard_map/ppermute | solution.py:38
  10.7 0.1 collective-permute-start.4
  10.8 1.1 %collective-permute-done.far = bf16[8,3,32,128]{3,2,1,0:T(8,128)(2,1)S(1)} collective-permute-done((bf16[8,3,32,128]{3,2,1,0:T(8,128)(2,1)S(1)}, bf16[8,3,32,128]{3,2,1,0:T(8,128)(2,1)S(1)}, u32[]{:S(2)}, u32[]{:S(2)}) %collective-permute-start) | collective-permute-done | bytes 196640 | tf_op jit(solution)/shard_map/ppermute | solution.py:551
  11.9 1.5 %collective-permute-start.1 = (bf16[3,32,128]{2,1,0:T(8,128)(2,1)S(1)}, bf16[3,32,128]{2,1,0:T(8,128)(2,1)S(1)}, u32[]{:S(2)}, u32[]{:S(2)}) collective-permute-start(bf16[3,32,128]{2,1,0:T(8,128)(2,1)S(1)} %get-tuple-element.58), channel_id=1, source_target_pairs={{0,8},{8,16},{16,24},{24,0},{1,9},{9,17},{17,25},{25,1},{2,10},{10... | collective-permute-start | bytes 73736 | tf_op jit(solution)/shard_map/ppermute | solution.py:37
  13.4 1.4 %collective-permute-start.2 = (bf16[3,32,128]{2,1,0:T(8,128)(2,1)S(1)}, bf16[3,32,128]{2,1,0:T(8,128)(2,1)S(1)}, u32[]{:S(2)}, u32[]{:S(2)}) collective-permute-start(bf16[3,32,128]{2,1,0:T(8,128)(2,1)S(1)} %get-tuple-element.57), channel_id=1, source_target_pairs={{8,0},{16,8},{24,16},{0,24},{9,1},{17,9},{25,17},{1,25},{10,2},{18... | collective-permute-start | bytes 73736 | tf_op jit(solution)/shard_map/ppermute | solution.py:38
  14.8 1.0 %shard_map.96 = (bf16[4,6,32,128]{3,2,1,0:T(8,128)(2,1)S(1)}, bf16[2,4,32,128]{3,2,1,0:T(8,128)(2,1)S(1)}, bf16[3,6,3,32,128]{4,3,2,1,0:T(8,128)(2,1)S(1)}) custom-call(s32[1]{0:T(128)} %bitcast.flip, bf16[8,8,32,128]{3,2,1,0:T(8,128)(2,1)S(1)} %get-tuple-element.29.cells, bf16[8,3,32,128]{3,2,1,0:T(8,128)(2,1)S(1)} %collective-permute-done.3.near, ...), custom_call_target="tpu_custom_call" | custom-call | flops 1073741824 | bytes 1048576 | tf_op jit(solution)/shard_map/pallas_call | solution.py:304
  15.8 0.6 %shard_map.97 = (bf16[4,2,32,128]{3,2,1,0:T(8,128)(2,1)S(1)}, bf16[2,2,32,128]{3,2,1,0:T(8,128)(2,1)S(1)}) custom-call(s32[1]{0:T(128)} %bitcast.flip, bf16[8,3,32,128]{3,2,1,0:T(8,128)(2,1)S(1)} %collective-permute-done.far, bf16[3,6,3,32,128]{4,3,2,1,0:T(8,128)(2,1)S(1)} %get-tuple-element.34.edge, bf16[128,1536]{1,0:T(8,128)(2,1)S(1)} %get-tuple-element.31.mix, ...), custom_call_target="tpu_custom_call" | custom-call | flops 1073741824 | bytes 1048576 | tf_op jit(solution)/shard_map/pallas_call | solution.py:304
  16.4 0.1 collective-permute-done.4.left
  16.5 1.0 %shard_map.95 = (bf16[4,6,32,128]{3,2,1,0:T(8,128)(2,1)S(1)}, bf16[2,4,32,128]{3,2,1,0:T(8,128)(2,1)S(1)}, bf16[3,8,3,32,128]{4,3,2,1,0:T(8,128)(2,1)S(1)}) custom-call(s32[1]{0:T(128)} %bitcast.flip, bf16[8,8,32,128]{3,2,1,0:T(8,128)(2,1)S(1)} %get-tuple-element.29.cells, bf16[8,3,32,128]{3,2,1,0:T(8,128)(2,1)S(1)} %collective-permute-done.3.near, ...), custom_call_target="tpu_custom_call" | custom-call | flops 1073741824 | bytes 1048576 | tf_op jit(solution)/shard_map/pallas_call | solution.py:304
  17.5 0.6 %shard_map.98 = (bf16[8,2,32,128]{3,2,1,0:T(8,128)(2,1)S(1)}, bf16[4,6,32,128]{3,2,1,0:T(8,128)(2,1)S(1)}, bf16[3,32,128]{2,1,0:T(8,128)(2,1)S(1)}, bf16[3,32,128]{2,1,0:T(8,128)(2,1)S(1)}) custom-call(s32[1]{0:T(128)} %bitcast.flip, bf16[8,3,32,128]{3,2,1,0:T(8,128)(2,1)S(1)} %collective-permute-done.far, ...), custom_call_target="tpu_custom_call" | custom-call | flops 1073741824 | bytes 1048576 | tf_op jit(solution)/shard_map/pallas_call | solution.py:304
  18.2 2.1 %collective-permute-start.6 = (bf16[3,32,128]{2,1,0:T(8,128)(2,1)S(1)}, bf16[3,32,128]{2,1,0:T(8,128)(2,1)S(1)}, u32[]{:S(2)}, u32[]{:S(2)}) collective-permute-start(bf16[3,32,128]{2,1,0:T(8,128)(2,1)S(1)} %get-tuple-element.46), channel_id=1, source_target_pairs={{0,8},{8,16},{16,24},{24,0},{1,9},{9,17},{17,25},{25,1},{2,10},{10... | collective-permute-start | bytes 73736 | tf_op jit(solution)/shard_map/ppermute | solution.py:37
  20.3 0.9 %collective-permute-start.7 = (bf16[3,32,128]{2,1,0:T(8,128)(2,1)S(1)}, bf16[3,32,128]{2,1,0:T(8,128)(2,1)S(1)}, u32[]{:S(2)}, u32[]{:S(2)}) collective-permute-start(bf16[3,32,128]{2,1,0:T(8,128)(2,1)S(1)} %get-tuple-element.47), channel_id=1, source_target_pairs={{8,0},{16,8},{24,16},{0,24},{9,1},{17,9},{25,17},{1,25},{10,2},{18... | collective-permute-start | bytes 73736 | tf_op jit(solution)/shard_map/ppermute | solution.py:38
  21.2 0.4 %own_three.1 = (bf16[2,2,64,128]{3,2,1,0:T(8,128)(2,1)S(1)}, bf16[4,5,3,32,128]{4,3,2,1,0:T(8,128)(2,1)S(1)}) custom-call(bf16[4,6,32,128]{3,2,1,0:T(8,128)(2,1)S(1)} %get-tuple-element.42.cells, bf16[64,864]{1,0:T(8,128)(2,1)S(1)} %copy.11.mix, f32[1,64]{1,0:T(1,128)S(1)} %get-tuple-element.43.bias), custom_call_target="tpu_custom_call" | custom-call | flops 1073741824 | bytes 1048576 | tf_op jit(solution)/shard_map/own_three/pallas_call | solution.py:428
  21.6 1.4 %collective-permute-done.6.left = bf16[3,32,128]{2,1,0:T(8,128)(2,1)S(1)} collective-permute-done((bf16[3,32,128]{2,1,0:T(8,128)(2,1)S(1)}, bf16[3,32,128]{2,1,0:T(8,128)(2,1)S(1)}, u32[]{:S(2)}, u32[]{:S(2)}) %collective-permute-start.6) | collective-permute-done | bytes 24608 | tf_op jit(solution)/shard_map/ppermute | solution.py:37
  23.0 1.1 %collective-permute-done.7.right = bf16[3,32,128]{2,1,0:T(8,128)(2,1)S(1)} collective-permute-done((bf16[3,32,128]{2,1,0:T(8,128)(2,1)S(1)}, bf16[3,32,128]{2,1,0:T(8,128)(2,1)S(1)}, u32[]{:S(2)}, u32[]{:S(2)}) %collective-permute-start.7) | collective-permute-done | bytes 24608 | tf_op jit(solution)/shard_map/ppermute | solution.py:38
  24.1 1.3 %three.1 = (bf16[4,2,64,128]{3,2,1,0:T(8,128)(2,1)S(1)}, bf16[4,8,16,128]{3,2,1,0:T(8,128)(2,1)}) custom-call(bf16[4,5,3,32,128]{4,3,2,1,0:T(8,128)(2,1)S(1)} %get-tuple-element.44.paired, bf16[2,2,64,128]{3,2,1,0:T(8,128)(2,1)S(1)} %get-tuple-element.45.inside, bf16[3,32,128]{2,1,0:T(8,128)(2,1)S(1)} %collective-permute-done.6.left, ...), custom_call_target="tpu_custom_call" | custom-call | flops 1073741824 | bytes 1048576 | tf_op jit(solution)/shard_map/three/pallas_call | solution.py:447
  25.4 2.6 %all-to-all-start = ((bf16[32,16,128]{2,1,0:T(8,128)(2,1)}), bf16[32,16,128]{2,1,0:T(8,128)(2,1)S(1)}, u32[]{:S(2)}, u32[]{:S(2)}) async-start(bf16[32,16,128]{2,1,0:T(8,128)(2,1)} %bitcast.12), calls=%async_computation | async-start | bytes 262144 | tf_op jit(solution)/shard_map/all_to_all | solution.py:622
  28.0 0.0 copy-start
  28.0 1.1 %store_two.1 = bf16[32,8,8,128]{3,2,1,0:T(8,128)(2,1)} custom-call(s32[1]{0:T(128)} %bitcast.flip, bf16[8,2,32,128]{3,2,1,0:T(8,128)(2,1)S(1)} %get-tuple-element.39.far, bf16[4,6,32,128]{3,2,1,0:T(8,128)(2,1)S(1)} %get-tuple-element.40.center, bf16[4,6,32,128]{3,2,1,0:T(8,128)(2,1)S(1)} %get-tuple-element.41.sides), custom_call_target="tpu_custom_call" | custom-call | flops 1073741824 | bytes 1048576 | tf_op jit(solution)/shard_map/store_two/pallas_call | solution.py:334
  29.1 7.1 %all-to-all-done.tiles = bf16[32,16,128]{2,1,0:T(8,128)(2,1)S(1)} async-done(((bf16[32,16,128]{2,1,0:T(8,128)(2,1)}), bf16[32,16,128]{2,1,0:T(8,128)(2,1)S(1)}, u32[]{:S(2)}, u32[]{:S(2)}) %all-to-all-start) | async-done | bytes 131104 | tf_op jit(solution)/shard_map/all_to_all | solution.py:622
  36.1 1.4 %four.1 = (bf16[8,16,4,128]{3,2,1,0:T(4,128)(2,1)}, bf16[64,4,4,64]{3,2,1,0:T(4,128)(2,1)}) custom-call(bf16[32,16,128]{2,1,0:T(8,128)(2,1)S(1)} %all-to-all-done.tiles, bf16[27,64,128]{2,1,0:T(8,128)(2,1)S(1)} %bitcast.22, f32[1,128]{1,0:T(1,128)S(1)} %get-tuple-element.49.bias, bf16[4,2,64,128]{3,2,1,0:T(8,128)(2,1)S(1)} %get-tuple-element.50.columns), custom_call_target="tpu_custom_call" | custom-call | flops 1073741824 | bytes 1048576 | tf_op jit(solution)/shard_map/four/pallas_call | solution.py:525
  (14 shorter events, 0.1 us)
Async XLA Ops:
  0.6 6.5 %copy-start.5 = (bf16[27,64,32]{1,2,0:T(8,128)(2,1)S(1)}, bf16[27,64,32]{1,2,0:T(8,128)(2,1)}, u32[]{:S(2)}) copy-start(bf16[27,64,32]{1,2,0:T(8,128)(2,1)} %param.10) | copy-start | bytes 331780
  1.9 5.5 %copy-start.1 = (bf16[27,32,32]{2,1,0:T(8,128)(2,1)S(1)}, bf16[27,32,32]{2,1,0:T(8,128)(2,1)}, u32[]{:S(2)}) copy-start(bf16[27,32,32]{2,1,0:T(8,128)(2,1)} %weights.1) | copy-start | bytes 165892
  1.9 6.3 %collective-permute-start.3 = (bf16[8,3,32,128]{3,2,1,0:T(8,128)(2,1)S(1)}, bf16[8,3,32,128]{3,2,1,0:T(8,128)(2,1)S(1)}, u32[]{:S(2)}, u32[]{:S(2)}) collective-permute-start(bf16[8,3,32,128]{3,2,1,0:T(8,128)(2,1)S(1)} %get-tuple-element.30), channel_id=1, source_target_pairs={{0,1},{1,0},{2,3},{3,2},{4,5},{5,4},{6,7},{7,6},{8,9},{9,8},{10,11... | collective-permute-start | bytes 589832 | tf_op jit(solution)/shard_map/ppermute | solution.py:552
  2.5 9.4 %collective-permute-start = (bf16[8,3,32,128]{3,2,1,0:T(8,128)(2,1)S(1)}, bf16[8,3,32,128]{3,2,1,0:T(8,128)(2,1)S(1)}, u32[]{:S(2)}, u32[]{:S(2)}) collective-permute-start(bf16[8,3,32,128]{3,2,1,0:T(8,128)(2,1)S(1)} %get-tuple-element.28), channel_id=1, source_target_pairs={{0,7},{1,2},{2,1},{3,4},{4,3},{5,6},{6,5},{7,0},{8,15},{9,10},{10,... | collective-permute-start | bytes 589832 | tf_op jit(solution)/shard_map/ppermute | solution.py:551
  7.3 0.7 %copy-start.2 = (f32[32]{0:T(128)S(1)}, f32[32]{0:T(128)}, u32[]{:S(2)}) copy-start(f32[32]{0:T(128)} %param.9) | copy-start | bytes 388
  7.3 0.7 %copy-start.3 = (f32[64]{0:T(128)S(1)}, f32[64]{0:T(128)}, u32[]{:S(2)}) copy-start(f32[64]{0:T(128)} %param.11) | copy-start | bytes 772
  7.3 0.7 %copy-start.4 = (f32[128]{0:T(128)S(1)}, f32[128]{0:T(128)}, u32[]{:S(2)}) copy-start(f32[128]{0:T(128)} %param.13) | copy-start | bytes 1540
  8.2 8.2 %collective-permute-start.5 = (bf16[11,32,128]{2,1,0:T(8,128)(2,1)S(1)}, bf16[11,32,128]{2,1,0:T(8,128)(2,1)S(1)}, u32[]{:S(2)}, u32[]{:S(2)}) collective-permute-start(bf16[11,32,128]{2,1,0:T(8,128)(2,1)S(1)} %pad_maximum_fusion.1), channel_id=1, source_target_pairs={{8,0},{16,8},{24,16},{0,24},{9,1},{17,9},{25,17},{1,25},{10,2},{18... | collective-permute-start | bytes 270344 | tf_op jit(solution)/shard_map/ppermute | solution.py:38
  10.7 5.7 %collective-permute-start.4 = (bf16[11,32,128]{2,1,0:T(8,128)(2,1)S(1)}, bf16[11,32,128]{2,1,0:T(8,128)(2,1)S(1)}, u32[]{:S(2)}, u32[]{:S(2)}) collective-permute-start(bf16[11,32,128]{2,1,0:T(8,128)(2,1)S(1)} %pad_maximum_fusion), channel_id=1, source_target_pairs={{0,8},{8,16},{16,24},{24,0},{1,9},{9,17},{17,25},{25,1},{2,10},{10... | collective-permute-start | bytes 270344 | tf_op jit(solution)/shard_map/ppermute | solution.py:37
  11.9 5.6 %collective-permute-start.1 = (bf16[3,32,128]{2,1,0:T(8,128)(2,1)S(1)}, bf16[3,32,128]{2,1,0:T(8,128)(2,1)S(1)}, u32[]{:S(2)}, u32[]{:S(2)}) collective-permute-start(bf16[3,32,128]{2,1,0:T(8,128)(2,1)S(1)} %get-tuple-element.58), channel_id=1, source_target_pairs={{0,8},{8,16},{16,24},{24,0},{1,9},{9,17},{17,25},{25,1},{2,10},{10... | collective-permute-start | bytes 73736 | tf_op jit(solution)/shard_map/ppermute | solution.py:37
  13.4 4.2 %collective-permute-start.2 = (bf16[3,32,128]{2,1,0:T(8,128)(2,1)S(1)}, bf16[3,32,128]{2,1,0:T(8,128)(2,1)S(1)}, u32[]{:S(2)}, u32[]{:S(2)}) collective-permute-start(bf16[3,32,128]{2,1,0:T(8,128)(2,1)S(1)} %get-tuple-element.57), channel_id=1, source_target_pairs={{8,0},{16,8},{24,16},{0,24},{9,1},{17,9},{25,17},{1,25},{10,2},{18... | collective-permute-start | bytes 73736 | tf_op jit(solution)/shard_map/ppermute | solution.py:38
  18.2 4.8 %collective-permute-start.6 = (bf16[3,32,128]{2,1,0:T(8,128)(2,1)S(1)}, bf16[3,32,128]{2,1,0:T(8,128)(2,1)S(1)}, u32[]{:S(2)}, u32[]{:S(2)}) collective-permute-start(bf16[3,32,128]{2,1,0:T(8,128)(2,1)S(1)} %get-tuple-element.46), channel_id=1, source_target_pairs={{0,8},{8,16},{16,24},{24,0},{1,9},{9,17},{17,25},{25,1},{2,10},{10... | collective-permute-start | bytes 73736 | tf_op jit(solution)/shard_map/ppermute | solution.py:37
  20.3 3.8 %collective-permute-start.7 = (bf16[3,32,128]{2,1,0:T(8,128)(2,1)S(1)}, bf16[3,32,128]{2,1,0:T(8,128)(2,1)S(1)}, u32[]{:S(2)}, u32[]{:S(2)}) collective-permute-start(bf16[3,32,128]{2,1,0:T(8,128)(2,1)S(1)} %get-tuple-element.47), channel_id=1, source_target_pairs={{8,0},{16,8},{24,16},{0,24},{9,1},{17,9},{25,17},{1,25},{10,2},{18... | collective-permute-start | bytes 73736 | tf_op jit(solution)/shard_map/ppermute | solution.py:38
  25.4 10.7 %all-to-all-start = ((bf16[32,16,128]{2,1,0:T(8,128)(2,1)}), bf16[32,16,128]{2,1,0:T(8,128)(2,1)S(1)}, u32[]{:S(2)}, u32[]{:S(2)}) async-start(bf16[32,16,128]{2,1,0:T(8,128)(2,1)} %bitcast.12), calls=%async_computation | async-start | bytes 262144 | tf_op jit(solution)/shard_map/all_to_all | solution.py:622
  28.0 8.2 %copy-start = (bf16[27,128,64]{1,2,0:T(8,128)(2,1)S(1)}, bf16[27,128,64]{1,2,0:T(8,128)(2,1)}, u32[]{:S(2)}) copy-start(bf16[27,128,64]{1,2,0:T(8,128)(2,1)} %param.12) | copy-start | bytes 1327108
